TPU v7x, 32 devices: a whole 2x2x4 slice. The times are simulated.
32 devices in a mesh: leaf: 8 (over z, y), front: 4 (over x, core).
Axes of the slice: x: 2, y: 2, z: 4, core: 2. Of those that a mesh axis runs over, the one named last changes fastest.
Arguments:
- rhs_leaf: float32 [32, 8192], P(None, ('leaf', 'front')), may hold values from -6 to 6
- rhs_sep: float32 [32, 4096], P(None, ('leaf', 'front')), may hold values from -6 to 6
- inv_leaf: float32 [8, 1024, 1024], P('leaf', 'front'), may hold values from -0.1875 to 0.1875
- inv_sep: float32 [8, 512, 512], P('leaf', 'front'), may hold values from -0.25 to 0.25
- push_leaf: float32 [8, 128, 1024], P('leaf', None, 'front'), may hold values from -0.09375 to 0.09375
- push_sep: float32 [8, 128, 512], P('leaf', None, 'front'), may hold values from -0.125 to 0.125
- pull_leaf: float32 [8, 1024, 128], P('leaf', 'front'), may hold values from -0.25 to 0.25
- pull_sep: float32 [8, 512, 128], P('leaf', 'front'), may hold values from -0.25 to 0.25
- rows_leaf: int32 [8, 128], P('leaf'), may hold values from 0 to 511, as said below
- rows_sep: int32 [8, 128], P('leaf'), may hold values from 0 to 511, as said below
- pivot_leaf: int32 [8, 1024], P('leaf'), may hold values from 0 to 1023, each once within a row
- pivot_sep: int32 [8, 512], P('leaf'), may hold values from 0 to 511, each once within a row
- basis_leaf: float32 [50, 8192], P(None, ('leaf', 'front')), may hold values from -6 to 6
- basis_sep: float32 [50, 4096], P(None, ('leaf', 'front')), may hold values from -6 to 6
Outputs:
- q_leaf: float32 [32, 8192], P(None, ('leaf', 'front'))
- q_sep: float32 [32, 4096], P(None, ('leaf', 'front'))
- coeffs: float32 [50, 32], replicated
- rfac: float32 [32, 32], replicated
Inputs may be any that keep to these rules, and one draw needn't show every extreme that they name: `rows_leaf`: each row holds 128 different rows of a separator front. `rows_sep`: each row holds 128 different rows of a separator front. `pivot_leaf`: each row is a permutation. `pivot_sep`: each row is a permutation.
All inputs are finite; a program needn't handle non-finite values.
Results may differ from a plain program's by a relative error of at most 0.0001.
Values sent between devices are 32-bit elements; how exact they have to be, the bound alone decides.
No kernel may reach another device: no remote copies, remote signals or barrier semaphores. Data moves between devices by JAX's collectives and lax.ppermute only.
A program may use at most 64 MiB of HBM per device.

v0:
```python
import jax
import jax.numpy as jnp
from jax import lax
from jax.sharding import PartitionSpec as P

exact_mode = lax.Precision.HIGHEST


def contract(former, latter):
    return lax.dot_general(
        former,
        latter,
        (((1,), (1,)), ((), ())),
        precision=exact_mode,
        preferred_element_type=jnp.float32,
    )


def expand(coeff_block, basis):
    return jnp.dot(coeff_block.T, basis, precision=exact_mode, preferred_element_type=jnp.float32)


def apply_inverse(gathered, inverse, pivots):
    return contract(gathered[:, pivots], inverse)


def solve_if(active, gathered, inverse, pivots):

    def chosen(operand):
        return apply_inverse(operand, inverse, pivots)

    def skipped(operand):
        return jnp.zeros((operand.shape[0], inverse.shape[0]), jnp.float32)

    return lax.cond(active, chosen, skipped, gathered)


def pick_piece(pool, index, valid):
    safe = jnp.clip(index, 0, pool.shape[0] - 1)
    piece = lax.dynamic_index_in_dim(pool, safe, 0, keepdims=False)
    return jnp.where(valid, piece, jnp.zeros_like(piece))


def push_term(state, weights, row_list, sep_width):
    partial_term = contract(state, weights)
    dense = jnp.zeros((state.shape[0], sep_width), jnp.float32).at[:, row_list].add(partial_term)
    return lax.psum_scatter(dense, "front", scatter_dimension=1, tiled=True)


def sep_gathered(shares):
    return lax.all_gather(shares, "front", axis=1, tiled=True)


def leaf_gathered(shares):
    return lax.all_gather(shares, "front", axis=1, tiled=True)


def on_device(
    rhs_leaf,
    rhs_sep,
    inv_leaf,
    inv_sep,
    push_leaf,
    push_sep,
    pull_leaf,
    pull_sep,
    rows_leaf,
    rows_sep,
    pivot_leaf,
    pivot_sep,
    basis_leaf,
    basis_sep,
):
    holder = lax.axis_index("leaf")
    groups = lax.axis_size("leaf")
    top_level = groups.bit_length() - 1
    sep_width = pivot_sep.shape[1]
    leaf_inverse = inv_leaf[0]
    sep_inverse = inv_sep[0]
    leaf_pivots = pivot_leaf[0]
    sep_pivots = pivot_sep[0]
    level_of = jnp.full((), top_level + 1, jnp.int32)
    for bit_index in range(top_level, 0, -1):
        level_of = jnp.where(holder % 2**bit_index != 0, jnp.int32(bit_index), level_of)
    leaf_state = apply_inverse(leaf_gathered(rhs_leaf), leaf_inverse, leaf_pivots)
    sep_state = jnp.zeros_like(rhs_sep)
    leaf_push = push_term(leaf_state, push_leaf[0], rows_leaf[0], sep_width)
    sep_push = jnp.zeros_like(rhs_sep)
    for height in range(1, top_level + 2):
        if height == 1:
            lower_index = holder - 1
            upper_index = holder
        else:
            lower_index = holder - 2 ** (height - 2)
            upper_index = holder + 2 ** (height - 2)
        lower_valid = jnp.logical_and(lower_index >= 0, height <= top_level)
        upper_valid = upper_index < groups
        source = leaf_push if height == 1 else sep_push
        pool = lax.all_gather(source[None], "leaf", axis=0, tiled=True)
        arriving = pick_piece(pool, upper_index, upper_valid) + pick_piece(
            pool, lower_index, lower_valid
        )
        active = level_of == height
        applied = solve_if(active, sep_gathered(rhs_sep - arriving), sep_inverse, sep_pivots)
        sep_state = jnp.where(active, applied, sep_state)
        if height <= top_level:
            sep_push = jnp.where(
                active, push_term(sep_state, push_sep[0], rows_sep[0], sep_width), sep_push
            )
    sep_solution = sep_state
    leaf_solution = leaf_state
    for height in range(top_level, -1, -1):
        if height == top_level:
            parent_index = jnp.zeros((), jnp.int32)
        elif height >= 1:
            parent_index = (2 * (holder // 2 ** (height + 1)) + 1) * 2**height
        else:
            parent_index = holder // 2 * 2 + 1
        pool = lax.all_gather(sep_solution[None], "leaf", axis=0, tiled=True)
        picked = lax.dynamic_index_in_dim(pool, parent_index, 0, keepdims=False)
        parent = lax.all_gather(picked, "front", axis=1, tiled=True)
        if height >= 1:
            lifted = contract(parent[:, rows_sep[0]], pull_sep[0])
            active = level_of == height
            applied = solve_if(active, sep_gathered(lifted), sep_inverse, sep_pivots)
            sep_solution = jnp.where(active, sep_state - applied, sep_solution)
        else:
            lifted = contract(parent[:, rows_leaf[0]], pull_leaf[0])
            leaf_solution = leaf_state - apply_inverse(
                leaf_gathered(lifted), leaf_inverse, leaf_pivots
            )
    total_rows = groups * (pivot_leaf.shape[1] + sep_width)
    first_sum, metric_sum = lax.psum(
        (
            contract(basis_leaf, leaf_solution) + contract(basis_sep, sep_solution),
            contract(basis_leaf, basis_leaf) + contract(basis_sep, basis_sep),
        ),
        ("leaf", "front"),
    )
    first_proj = first_sum / total_rows
    metric = metric_sum / total_rows
    once_leaf = leaf_solution - expand(first_proj, basis_leaf)
    once_sep = sep_solution - expand(first_proj, basis_sep)
    second_sum, self_sum = lax.psum(
        (
            contract(basis_leaf, once_leaf) + contract(basis_sep, once_sep),
            contract(once_leaf, once_leaf) + contract(once_sep, once_sep),
        ),
        ("leaf", "front"),
    )
    second = second_sum / total_rows
    twice_leaf = once_leaf - expand(second, basis_leaf)
    twice_sep = once_sep - expand(second, basis_sep)
    cross = jnp.dot(second.T, second, precision=exact_mode, preferred_element_type=jnp.float32)
    curved = jnp.dot(
        second.T,
        jnp.dot(metric, second, precision=exact_mode, preferred_element_type=jnp.float32),
        precision=exact_mode,
        preferred_element_type=jnp.float32,
    )
    gram_matrix = self_sum / total_rows - 2.0 * cross + curved
    lower_factor = jnp.linalg.cholesky(gram_matrix)
    q_leaf = lax.linalg.triangular_solve(lower_factor, twice_leaf, left_side=True, lower=True)
    q_sep = lax.linalg.triangular_solve(lower_factor, twice_sep, left_side=True, lower=True)
    return (q_leaf, q_sep, first_proj + second, lower_factor.T)


def solution(mesh):
    placed = (
        P(None, ("leaf", "front")),
        P(None, ("leaf", "front")),
        P("leaf", "front", None),
        P("leaf", "front", None),
        P("leaf", None, "front"),
        P("leaf", None, "front"),
        P("leaf", "front", None),
        P("leaf", "front", None),
        P("leaf", None),
        P("leaf", None),
        P("leaf", None),
        P("leaf", None),
        P(None, ("leaf", "front")),
        P(None, ("leaf", "front")),
    )
    return jax.shard_map(
        on_device,
        mesh=mesh,
        in_specs=placed,
        out_specs=(P(None, ("leaf", "front")), P(None, ("leaf", "front")), P(), P()),
        check_vma=False,
    )
```

profile of v0, /device:TPU:0, one launch (start us, length us, event | category | flops | bytes accessed | tf_op | source)
XLA Modules:
  0.0 534.2 jit_solution(18016340628218547163)
XLA Ops:
  8.9 8.6 %all_gather.63 = f32[32,1024]{0,1:T(8,128)S(1)} all-gather(f32[32,256]{0,1:T(8,128)S(1)} %copy.76), channel_id=1, replica_groups=mesh['leaf'=8,'front'=4] {'front'}, dimensions={1}, use_global_device_ids=true | all-gather | bytes 163840 | tf_op jit(solution)/shard_map/all_gather | solution.py:55
  17.5 2.8 gather_fusion.7
  24.1 20.9 %reduce-scatter.5.cloned.1.call-done = f32[32,128]{0,1:T(8,128)} async-done(((f32[32,512]{0,1:T(8,128)}), f32[32,128]{0,1:T(8,128)}) %reduce-scatter.5.cloned.1.call-update) | async-done | bytes 16400 | tf_op jit(solution)/shard_map/reduce_scatter | solution.py:47
  45.9 30.8 %all-gather = f32[256,128]{1,0:T(8,128)S(1)} all-gather(f32[32,128]{1,0:T(8,128)S(1)} %copy.78), channel_id=2, replica_groups=mesh['leaf'=8,'front'=4] {'leaf'}, dimensions={0}, use_global_device_ids=true | all-gather | bytes 147456 | tf_op jit(solution)/shard_map/all_gather | solution.py:99
  76.7 5.2 all_gather.65
  86.7 19.5 %reduce-scatter.7.cloned.1.call-done = f32[32,128]{1,0:T(8,128)} async-done(((f32[32,512]{1,0:T(8,128)}), f32[32,128]{1,0:T(8,128)}) %reduce-scatter.7.cloned.1.call-update) | async-done | bytes 16400 | tf_op jit(solution)/shard_map/reduce_scatter | solution.py:47
  106.2 30.7 %all-gather.1 = f32[256,128]{1,0:T(8,128)S(1)} all-gather(f32[32,128]{1,0:T(8,128)S(1)} %broadcast_select_fusion), channel_id=3, replica_groups=mesh['leaf'=8,'front'=4] {'leaf'}, dimensions={0}, use_global_device_ids=true | all-gather | bytes 147456 | tf_op jit(solution)/shard_map/all_gather | solution.py:99
  137.0 5.2 all_gather.67
  145.3 19.3 %reduce-scatter.9.cloned.1.call-done = f32[32,128]{1,0:T(8,128)} async-done(((f32[32,512]{1,0:T(8,128)}), f32[32,128]{1,0:T(8,128)}) %reduce-scatter.9.cloned.1.call-update) | async-done | bytes 16400 | tf_op jit(solution)/shard_map/reduce_scatter | solution.py:47
  164.6 31.4 %all-gather.2 = f32[256,128]{1,0:T(8,128)S(1)} all-gather(f32[32,128]{1,0:T(8,128)S(1)} %broadcast_select_fusion.1), channel_id=4, replica_groups=mesh['leaf'=8,'front'=4] {'leaf'}, dimensions={0}, use_global_device_ids=true | all-gather | bytes 147456 | tf_op jit(solution)/shard_map/all_gather | solution.py:99
  196.0 5.2 all_gather.69
  203.5 18.8 %reduce-scatter.11.cloned.1.call-done = f32[32,128]{1,0:T(8,128)} async-done(((f32[32,512]{1,0:T(8,128)}), f32[32,128]{1,0:T(8,128)}) %reduce-scatter.11.cloned.1.call-update) | async-done | bytes 16400 | tf_op jit(solution)/shard_map/reduce_scatter | solution.py:47
  222.3 30.6 %all-gather.3 = f32[256,128]{1,0:T(8,128)S(1)} all-gather(f32[32,128]{1,0:T(8,128)S(1)} %broadcast_select_fusion.2), channel_id=5, replica_groups=mesh['leaf'=8,'front'=4] {'leaf'}, dimensions={0}, use_global_device_ids=true | all-gather | bytes 147456 | tf_op jit(solution)/shard_map/all_gather | solution.py:99
  252.9 5.2 all_gather.71
  258.2 1.8 conditional.10
  259.9 30.5 %all-gather.4 = f32[256,128]{1,0:T(8,128)S(1)} all-gather(f32[32,128]{1,0:T(8,128)S(1)} %broadcast_select_fusion.4), channel_id=6, replica_groups=mesh['leaf'=8,'front'=4] {'leaf'}, dimensions={0}, use_global_device_ids=true | all-gather | bytes 147456 | tf_op jit(solution)/shard_map/all_gather | solution.py:119
  290.5 5.2 all-gather.12
  296.9 5.3 all_gather.74
  302.2 30.5 %all-gather.6 = f32[256,128]{1,0:T(8,128)S(1)} all-gather(f32[32,128]{1,0:T(8,128)S(1)} %subtract_select_fusion), channel_id=8, replica_groups=mesh['leaf'=8,'front'=4] {'leaf'}, dimensions={0}, use_global_device_ids=true | all-gather | bytes 147456 | tf_op jit(solution)/shard_map/all_gather | solution.py:119
  332.8 6.0 %all-gather.7 = f32[1,32,512]{1,2,0:T(8,128)S(1)} all-gather(f32[1,32,128]{1,2,0:T(8,128)S(1)} %copy.107), channel_id=9, replica_groups=mesh['leaf'=8,'front'=4] {'front'}, dimensions={2}, use_global_device_ids=true | all-gather | bytes 81920 | tf_op jit(solution)/shard_map/all_gather | solution.py:121
  339.6 5.3 all_gather.77
  344.9 30.5 %all-gather.8 = f32[256,128]{1,0:T(8,128)S(1)} all-gather(f32[32,128]{1,0:T(8,128)S(1)} %subtract_select_fusion.2), channel_id=10, replica_groups=mesh['leaf'=8,'front'=4] {'leaf'}, dimensions={0}, use_global_device_ids=true | all-gather | bytes 147456 | tf_op jit(solution)/shard_map/all_gather | solution.py:119
  375.5 5.8 %all-gather.9 = f32[1,32,512]{1,2,0:T(8,128)S(1)} all-gather(f32[1,32,128]{1,2,0:T(8,128)S(1)} %copy.108), channel_id=11, replica_groups=mesh['leaf'=8,'front'=4] {'front'}, dimensions={2}, use_global_device_ids=true | all-gather | bytes 81920 | tf_op jit(solution)/shard_map/all_gather | solution.py:121
  382.1 5.3 all_gather.80
  387.4 30.5 %all-gather.10 = f32[256,128]{1,0:T(8,128)S(1)} all-gather(f32[32,128]{1,0:T(8,128)S(1)} %subtract_select_fusion.1), channel_id=12, replica_groups=mesh['leaf'=8,'front'=4] {'leaf'}, dimensions={0}, use_global_device_ids=true | all-gather | bytes 147456 | tf_op jit(solution)/shard_map/all_gather | solution.py:119
  418.1 5.8 %all-gather.11 = f32[1,32,512]{1,2,0:T(8,128)S(1)} all-gather(f32[1,32,128]{1,2,0:T(8,128)S(1)} %copy.109), channel_id=13, replica_groups=mesh['leaf'=8,'front'=4] {'front'}, dimensions={2}, use_global_device_ids=true | all-gather | bytes 81920 | tf_op jit(solution)/shard_map/all_gather | solution.py:121
  425.0 5.4 %all_gather.83 = f32[32,1024]{1,0:T(8,128)S(1)} all-gather(f32[32,256]{1,0:T(8,128)S(1)} %fusion.6), channel_id=1, replica_groups=mesh['leaf'=8,'front'=4] {'front'}, dimensions={1}, use_global_device_ids=true | all-gather | bytes 163840 | tf_op jit(solution)/shard_map/all_gather | solution.py:55
  430.6 2.8 gather_fusion.12
  434.8 38.7 %psum.28 = f32[50,32]{0,1:T(8,128)S(1)} all-reduce(f32[50,32]{0,1:T(8,128)S(1)} %fusion.2), channel_id=1, replica_groups=mesh['leaf'=8,'front'=4] {'leaf','front'}, use_global_device_ids=true, to_apply=%region_22.23 | all-reduce | flops 1600 | bytes 12800 | tf_op jit(solution)/shard_map/psum | solution.py:133
  474.5 42.6 %all-reduce = (f32[50,32]{0,1:T(8,128)S(1)}, f32[32,32]{0,1:T(8,128)S(1)}, f32[50,50]{1,0:T(8,128)S(1)}) all-reduce(f32[50,32]{0,1:T(8,128)S(1)} %fusion.1, f32[32,32]{0,1:T(8,128)S(1)} %convolution_add_fusion.3, f32[50,50]{1,0:T(8,128)S(1)} %convolution_add_fusion), channel_id=1, replica_groups=mesh['leaf'=8,'front'=4] {'leaf','front'}, use_global_device_ids=true, to_apply=%region_24.25 | all-reduce | flops 5124 | bytes 40992 | tf_op jit(solution)/shard_map/psum | solution.py:144
  518.6 2.9 cholesky.16
  522.8 2.4 custom-call.8
  (128 shorter events, 29.9 us)
Async XLA Ops:
  7.2 13.2 %copy-start = (f32[1,256,1024]{2,1,0:T(8,128)S(1)}, f32[1,256,1024]{2,1,0:T(8,128)}, u32[]{:S(2)}) copy-start(f32[1,256,1024]{2,1,0:T(8,128)} %param.30) | copy-start | bytes 3145732
  7.2 37.9 %reduce-scatter.5.cloned.1.call-start = ((), (), s32[]{:S(2)}) async-start(), calls=%async_computation.4 | async-start | bytes 327680 | tf_op jit(solution)/shard_map/reduce_scatter | solution.py:47
  20.3 1.0 copy-start.8
  21.6 0.7 copy-start.11
  21.6 0.7 copy-start.12
  24.0 58.0 %copy-start.1 = (f32[1,128,512]{2,1,0:T(8,128)S(1)}, f32[1,128,512]{2,1,0:T(8,128)}, u32[]{:S(2)}) copy-start(f32[1,128,512]{2,1,0:T(8,128)} %param.31) | copy-start | bytes 786436
  24.0 82.2 %reduce-scatter.7.cloned.1.call-start = ((), (), s32[]{:S(2)}) async-start(), calls=%async_computation.5 | async-start | bytes 81920 | tf_op jit(solution)/shard_map/reduce_scatter | solution.py:47
  45.9 30.8 %copy-start.6 = (f32[32,128]{1,0:T(8,128)S(1)}, f32[32,128]{1,0:T(8,128)}, u32[]{:S(2)}) copy-start(f32[32,128]{1,0:T(8,128)} %param.29) | copy-start | bytes 49156
  82.0 0.7 copy-start.9
  82.7 0.8 copy-start.4
  85.7 0.8 copy-start.2
  85.7 78.9 %reduce-scatter.9.cloned.1.call-start = ((), (), s32[]{:S(2)}) async-start(), calls=%async_computation.6 | async-start | bytes 81920 | tf_op jit(solution)/shard_map/reduce_scatter | solution.py:47
  144.4 0.7 copy-start.3
  144.4 20.2 %copy-start.10 = (f32[32,128]{1,0:T(8,128)S(1)}, f32[32,128]{1,0:T(8,128)}, u32[]{:S(2)}) copy-start(f32[32,128]{1,0:T(8,128)} %reduce-scatter.7.cloned.1.call-done) | copy-start | bytes 49156
  144.4 77.9 %reduce-scatter.11.cloned.1.call-start = ((), (), s32[]{:S(2)}) async-start(), calls=%async_computation.7 | async-start | bytes 81920 | tf_op jit(solution)/shard_map/reduce_scatter | solution.py:47
  295.8 0.8 copy-start.5
  423.8 0.9 copy-start.7
Sparse Core Ops, SparseCore 0:
  24.1 20.8 reduce-scatter.4
  85.8 20.3 reduce-scatter.6
  144.5 20.0 reduce-scatter.8
  203.5 18.7 reduce-scatter.10
where the time goes:
time: 535 us; the launch traced here: 534 us
  blocking collectives  400 us (75%)
  waiting for transfers between devices  78.7 us (15%)
  local copies, waits for them, and re-layouts  19.1 us (4%)
  between operations  14.3 us (3%)
  other arithmetic  13.1 us (2%)
  matrix products  8.44 us (2%)
    all_gather x4, blocking collectives, on_device(): pool = lax.all_gather(source[None], 'leaf', axis=0, tiled=True)  123 us
    all_gather x4, blocking collectives, on_device(): pool = lax.all_gather(sep_solution[None], 'leaf', axis=0, tiled=True)  122 us
    reduce_scatter x4, waiting for transfers between devices, push_term(): return lax.psum_scatter(dense, 'front', scatter_dimension=1, tiled=True)  78.6 us
    psum x1, blocking collectives, on_device(): lax.psum((contract(basis_leaf, once_leaf) + contract(basis_sep, once_sep)...  42.6 us
    psum x1, blocking collectives, on_device(): lax.psum((contract(basis_leaf, leaf_solution) + contract(basis_sep, sep_s...  38.7 us
    all_gather x7, blocking collectives, sep_gathered(): return lax.all_gather(shares, 'front', axis=1, tiled=True)  36.7 us
    all_gather x4, blocking collectives, on_device(): parent = lax.all_gather(picked, 'front', axis=1, tiled=True)  22.7 us
    all_gather x2, blocking collectives, leaf_gathered(): return lax.all_gather(shares, 'front', axis=1, tiled=True)  14.1 us
  transfers between devices with their start and end apart: 4, of which 4 were waited for; matrix products, arithmetic and copies ran while one was open for 0% of the time, Pallas kernels for 0%

commit v1 on v0

v1 whole, which is shorter than its diff:
```python
import jax
import jax.numpy as jnp
from jax import lax
from jax.sharding import PartitionSpec as P

exact_mode = lax.Precision.HIGHEST


def mm(former, latter, left=1, right=0):
    return lax.dot_general(
        former,
        latter,
        (((left,), (right,)), ((), ())),
        precision=exact_mode,
        preferred_element_type=jnp.float32,
    )


def swap(value, axis, mask):
    count = lax.axis_size(axis)
    return lax.ppermute(value, axis, [(one, one ^ mask) for one in range(count)])


def gathered_pieces(value, axis):
    return [value] + [swap(value, axis, mask) for mask in range(1, lax.axis_size(axis))]


def doubled_pieces(value, axis):
    count = lax.axis_size(axis)
    pieces = {0: value}
    mask = count // 2
    while mask:
        kept = sorted(pieces)
        moved = swap(jnp.concatenate([pieces[k] for k in kept], 0), axis, mask)
        height = value.shape[0]
        for place, k in enumerate(kept):
            pieces[k ^ mask] = moved[place * height : (place + 1) * height]
        mask //= 2
    return [pieces[k] for k in range(count)]


def summed_pairwise(pieces):
    while len(pieces) > 1:
        pieces = [pieces[k] + pieces[k + 1] for k in range(0, len(pieces), 2)]
    return pieces[0]


def local_place(index, width, own):
    return jnp.bitwise_xor(index // width, own) * width + index % width


def one_hot(places, size):
    return (places[:, None] == lax.broadcasted_iota(jnp.int32, (1, size), 1)).astype(jnp.float32)


def on_device(
    rhs_leaf,
    rhs_sep,
    inv_leaf,
    inv_sep,
    push_leaf,
    push_sep,
    pull_leaf,
    pull_sep,
    rows_leaf,
    rows_sep,
    pivot_leaf,
    pivot_sep,
    basis_leaf,
    basis_sep,
):
    group = lax.axis_index("leaf")
    own = lax.axis_index("front")
    groups = lax.axis_size("leaf")
    top = groups.bit_length() - 1
    leaf_rows = pivot_leaf.shape[1]
    sep_rows = pivot_sep.shape[1]
    leaf_width = rhs_leaf.shape[1]
    sep_width = rhs_sep.shape[1]
    couple = rows_leaf.shape[1]
    total_rows = groups * (leaf_rows + sep_rows)
    level = jnp.full((), top + 1, jnp.int32)
    for bit in range(top, 0, -1):
        level = jnp.where(group % 2**bit != 0, jnp.int32(bit), level)

    leaf_pieces = gathered_pieces(rhs_leaf, "front")
    sep_pieces = gathered_pieces(rhs_sep, "front")
    rhs_leaf_all = jnp.concatenate(leaf_pieces, 1)
    rhs_sep_all = jnp.concatenate(sep_pieces, 1)

    rows_up = jnp.where(level == 1, rows_leaf[0], 0)
    rows_lo = jnp.where(level == 1, swap(rows_leaf, "leaf", 1)[0], 0)
    for height in range(2, top + 2):
        step = 2 ** (height - 2)
        rows_up = jnp.where(level == height, swap(rows_sep, "leaf", step)[0], rows_up)
        if height <= top:
            rows_lo = jnp.where(level == height, swap(rows_sep, "leaf", 3 * step)[0], rows_lo)

    leaf_hot = one_hot(local_place(pivot_leaf[0], leaf_width, own), leaf_rows)
    leaf_map = mm(leaf_hot, inv_leaf[0], 0, 1)
    leaf_state = mm(rhs_leaf_all, leaf_map)
    leaf_push = summed_pairwise(
        gathered_pieces(mm(leaf_state, push_leaf[0], 1, 1), "front")
    )

    bulk = jnp.concatenate([inv_sep[0], push_sep[0].T, pull_sep[0]], 1)
    bulk = jnp.concatenate(doubled_pieces(bulk, "front"), 0)
    sep_inv = bulk[:, :sep_rows]
    push_out = bulk[:, sep_rows : sep_rows + couple]
    pull_all = bulk[:, sep_rows + couple :]
    sep_hot = one_hot(local_place(pivot_sep[0], sep_width, own), sep_rows)
    sep_map = mm(sep_hot, sep_inv, 0, 1)
    lo_hot = one_hot(local_place(rows_lo, sep_width, own), sep_rows)
    up_hot = one_hot(local_place(rows_up, sep_width, own), sep_rows)
    entering = jnp.concatenate([lo_hot, up_hot, pull_all.T, rhs_sep_all], 0)
    leaving = jnp.concatenate([push_out, lo_hot.T, up_hot.T], 1)
    moved = mm(entering, sep_map)
    reduced = mm(moved, leaving)
    up_weights = reduced[: 2 * couple, :couple]
    turn_weights = reduced[: 2 * couple, couple:]
    down_weights = reduced[2 * couple : 3 * couple, couple:]
    push_base = reduced[3 * couple :, :couple]
    row_base = reduced[3 * couple :, couple:]

    pull_leaf_all = jnp.concatenate(doubled_pieces(pull_leaf[0], "front"), 0)
    leaf_lift = mm(pull_leaf_all, leaf_map, 0, 0)

    pair = jnp.concatenate([swap(leaf_push, "leaf", 1), leaf_push], 1)
    pair = jnp.where(level == 1, pair, 0.0)
    for height in range(2, top + 2):
        step = 2 ** (height - 2)
        term = push_base - mm(pair, up_weights)
        upper = swap(term, "leaf", step)
        lower = swap(term, "leaf", 3 * step) if height <= top else jnp.zeros_like(upper)
        pair = jnp.where(level == height, jnp.concatenate([lower, upper], 1), pair)

    row_base = row_base - mm(pair, turn_weights)
    above = jnp.zeros((rhs_leaf.shape[0], couple), jnp.float32)
    for height in range(top + 1, 1, -1):
        step = 2 ** (height - 2)
        below = row_base - mm(above, down_weights)
        upper = swap(below[:, couple:], "leaf", step)
        if height <= top:
            lower = swap(below[:, :couple], "leaf", 3 * step)
            is_upper = (group // (2 * step)) % 2 == 1
            upper = jnp.where(is_upper, upper, lower)
        above = jnp.where(level == height - 1, upper, above)
    below = row_base - mm(above, down_weights)
    leaf_above = jnp.where(level == 1, below[:, couple:], swap(below[:, :couple], "leaf", 1))

    leaf_solution = leaf_state - mm(leaf_above, leaf_lift)
    sep_solution = moved[3 * couple :, :sep_width] - mm(
        jnp.concatenate([pair, above], 1), moved[: 3 * couple, :sep_width]
    )

    basis = jnp.concatenate([basis_leaf, basis_sep], 1)
    solved = jnp.concatenate([leaf_solution, sep_solution], 1)
    metric = mm(basis, basis, 1, 1)
    for axis in ("front", "leaf"):
        mask = 1
        while mask < lax.axis_size(axis):
            metric = metric + swap(metric, axis, mask)
            mask *= 2
    metric = metric / total_rows
    inner = mm(solved, jnp.concatenate([basis, solved], 0), 1, 1)
    inner = summed_pairwise(gathered_pieces(inner, "front"))
    inner = lax.all_to_all(
        jnp.broadcast_to(inner[None], (groups,) + inner.shape), "leaf", 0, 0
    ).sum(0)
    rank = basis.shape[0]
    inner = inner / total_rows
    first = inner[:, :rank]
    second = first - mm(first, metric)
    third = second - mm(second, metric)
    coeffs = first + second
    gram = inner[:, rank:] - mm(
        jnp.concatenate([first, second], 1),
        jnp.concatenate([coeffs, second + third], 1),
        1,
        1,
    )
    lower_factor = jnp.linalg.cholesky(gram, symmetrize_input=True)
    twice = solved - mm(coeffs, basis)
    scaled = lax.linalg.triangular_solve(lower_factor, twice, left_side=True, lower=True)
    return (
        scaled[:, :leaf_width],
        scaled[:, leaf_width:],
        coeffs.T,
        lower_factor.T,
    )


def solution(mesh):
    placed = (
        P(None, ("leaf", "front")),
        P(None, ("leaf", "front")),
        P("leaf", "front", None),
        P("leaf", "front", None),
        P("leaf", None, "front"),
        P("leaf", None, "front"),
        P("leaf", "front", None),
        P("leaf", "front", None),
        P("leaf", None),
        P("leaf", None),
        P("leaf", None),
        P("leaf", None),
        P(None, ("leaf", "front")),
        P(None, ("leaf", "front")),
    )
    return jax.shard_map(
        on_device,
        mesh=mesh,
        in_specs=placed,
        out_specs=(P(None, ("leaf", "front")), P(None, ("leaf", "front")), P(), P()),
        check_vma=False,
    )
```

time: 535 us -> 127 us (0.24)
  blocking collectives: 400 us -> 0 us
  starting transfers between devices: 0.16 us -> 44.5 us
  waiting for transfers between devices: 78.7 us -> 44.3 us
  between operations: 14.3 us -> 1.26 us
  local copies, waits for them, and re-layouts: 19.1 us -> 6.6 us
  matrix products: 8.44 us -> 15.2 us
    all_gather x21 -> x0, blocking collectives: 319 us -> none  [the longest x4 123 us: on_device(): pool = lax.all_gather(source[None], 'leaf', axis=0, tiled=True)]
    psum x2 -> x0, blocking collectives: 81.2 us -> none  [the longest x1 42.6 us: on_device(): lax.psum((contract(basis_leaf, once_leaf) + contract(basis_sep, once_sep)...]
    reduce_scatter x4 -> x0, waiting for transfers between devices: 78.6 us -> none  [push_term(): return lax.psum_scatter(dense, 'front', scatter_dimension=1, tiled=True)]
    ppermute x0 -> x39, waiting for transfers between devices: none -> 44.3 us  [swap(): lax.ppermute(value, axis, [(one, one ^ mask) for one in range(count)])]
    ppermute x0 -> x39, starting transfers between devices: none -> 40.1 us  [swap(): lax.ppermute(value, axis, [(one, one ^ mask) for one in range(count)])]
    gather x7 -> x0, local copies, waits for them, and re-layouts: 9.24 us -> none  [the longest x3 6.67 us: apply_inverse(): return contract(gathered[:, pivots], inverse)]
    dot_general x26 -> x23, matrix products: 6.76 us -> 14.9 us  [mm(): lax.dot_general(former, latter, (((left,), (right,)), ((), ())), precisio...]
  transfers between devices with their start and end apart: 4 -> 40, of which waited for: 4 -> 22; matrix products, arithmetic and copies ran while one was open for 0% -> 18% of each run, Pallas kernels for 0% -> 0%
where the time goes in v1:
time: 127 us; the launch traced here: 126 us
  starting transfers between devices  44.5 us (35%)
  waiting for transfers between devices  44.3 us (35%)
  matrix products  15.2 us (12%)
  other arithmetic  14.6 us (11%)
  local copies, waits for them, and re-layouts  6.6 us (5%)
    ppermute x39, waiting for transfers between devices, swap(): lax.ppermute(value, axis, [(one, one ^ mask) for one in range(count)])  44.3 us
    ppermute x39, starting transfers between devices, swap(): lax.ppermute(value, axis, [(one, one ^ mask) for one in range(count)])  40.1 us
    dot_general x23, matrix products, mm(): lax.dot_general(former, latter, (((left,), (right,)), ((), ())), precisio...  14.9 us
    all_to_all x1, starting transfers between devices, on_device(): lax.all_to_all(jnp.broadcast_to(inner[None], (groups,) + inner.shape), 'l...  4.34 us
    another operation x3, other arithmetic, on_device(): lower_factor = jnp.linalg.cholesky(gram, symmetrize_input=True)  3.6 us
    convert_element_type x4, other arithmetic, one_hot(): (places[:, None] == lax.broadcasted_iota(jnp.int32, (1, size), 1)).astype...  2.93 us
  transfers between devices with their start and end apart: 40, of which 22 were waited for; matrix products, arithmetic and copies ran while one was open for 18% of the time, Pallas kernels for 0%

profile of v1, /device:TPU:0, one launch (start us, length us, event | category | flops | bytes accessed | tf_op | source)
XLA Modules:
  0.0 126.4 jit_solution(10719601997497718610)
XLA Ops:
  0.6 2.5 %collective-permute-start.13 = (f32[32,128]{1,0:T(8,128)}, f32[32,128]{1,0:T(8,128)}, u32[]{:S(2)}, u32[]{:S(2)}) collective-permute-start(f32[32,128]{1,0:T(8,128)} %param.15), channel_id=1, source_target_pairs={{0,3},{1,2},{2,1},{3,0},{4,7},{5,6},{6,5},{7,4},{8,11},{9,10},{10,... | collective-permute-start | bytes 49160 | tf_op jit(solution)/shard_map/ppermute | solution.py:21
  3.8 2.6 %collective-permute-start.6 = (s32[1,128]{1,0:T(1,128)}, s32[1,128]{1,0:T(1,128)S(1)}, u32[]{:S(2)}, u32[]{:S(2)}) collective-permute-start(s32[1,128]{1,0:T(1,128)} %param.23), channel_id=1, source_target_pairs={{0,16},{4,20},{8,24},{12,28},{16,0},{20,4},{24,8},{28,12},{1,17},{... | collective-permute-start | bytes 1544 | tf_op jit(solution)/shard_map/ppermute | solution.py:21
  6.3 1.6 %collective-permute-start.7 = (s32[1,128]{1,0:T(1,128)}, s32[1,128]{1,0:T(1,128)S(1)}, u32[]{:S(2)}, u32[]{:S(2)}) collective-permute-start(s32[1,128]{1,0:T(1,128)} %param.23), channel_id=1, source_target_pairs={{0,8},{4,12},{8,0},{12,4},{16,24},{20,28},{24,16},{28,20},{1,9},{5... | collective-permute-start | bytes 1544 | tf_op jit(solution)/shard_map/ppermute | solution.py:21
  7.9 1.5 %collective-permute-start.8 = (s32[1,128]{1,0:T(1,128)}, s32[1,128]{1,0:T(1,128)S(1)}, u32[]{:S(2)}, u32[]{:S(2)}) collective-permute-start(s32[1,128]{1,0:T(1,128)} %param.23), channel_id=1, source_target_pairs={{0,4},{4,0},{8,12},{12,8},{16,20},{20,16},{24,28},{28,24},{1,5},{5... | collective-permute-start | bytes 1544 | tf_op jit(solution)/shard_map/ppermute | solution.py:21
  12.5 2.6 %fusion.1 = f32[1024,256]{1,0:T(8,128)S(1)} fusion(s32[1024]{0:T(1024)S(1)} %fusion.92, f32[1,256,1024]{2,1,0:T(8,128)S(1)} %copy-done), kind=kOutput, calls=%fused_computation.2 | convolution fusion | flops 3223322624 | bytes 2101248 | tf_op jit(solution)/shard_map/dot_general | solution.py:10
  16.1 1.5 %collective-permute-start.5 = (s32[1,128]{1,0:T(1,128)S(1)}, s32[1,128]{1,0:T(1,128)S(1)}, u32[]{:S(2)}, u32[]{:S(2)}) collective-permute-start(s32[1,128]{1,0:T(1,128)S(1)} %copy-done.13), channel_id=1, source_target_pairs={{0,4},{4,0},{8,12},{12,8},{16,20},{20,16},{24,28},{28,24},{1,5},{5... | collective-permute-start | bytes 1544 | tf_op jit(solution)/shard_map/ppermute | solution.py:21
  19.1 1.5 %collective-permute-done.3 = s32[1,128]{1,0:T(1,128)S(1)} collective-permute-done((s32[1,128]{1,0:T(1,128)S(1)}, s32[1,128]{1,0:T(1,128)S(1)}, u32[]{:S(2)}, u32[]{:S(2)}) %collective-permute-start.3) | collective-permute-done | bytes 544 | tf_op jit(solution)/shard_map/ppermute | solution.py:21
  24.2 9.3 %collective-permute-done.9 = f32[128,768]{1,0:T(8,128)S(1)} collective-permute-done((f32[128,768]{1,0:T(8,128)S(1)}, f32[128,768]{1,0:T(8,128)S(1)}, u32[]{:S(2)}, u32[]{:S(2)}) %collective-permute-start.9) | collective-permute-done | bytes 393248 | tf_op jit(solution)/shard_map/ppermute | solution.py:21
  45.1 2.1 %fusion.7 = f32[416,512]{1,0:T(8,128)S(1)} fusion(f32[512,512]{1,0:T(8,128)S(1)} %fusion.5, f32[32,512]{0,1:T(8,128)S(1)} %copy.53, f32[128,512]{0,1:T(8,128)S(1)} %maximum_bitcast_fusion, f32[128,512]{0,1:T(8,128)S(1)} %copy-done.4, f32[128,512]{0,1:T(8,128)S(1)} %copy-done.5), kind=kOutput, calls=%fused_computation.21 | convolution fusion | flops 1309261824 | bytes 2752512 | tf_op jit(solution)/shard_map/dot_general | solution.py:10
  47.2 1.5 %fusion.19 = f32[416,384]{1,0:T(8,128)S(1)} fusion(f32[416,512]{1,0:T(8,128)S(1)} %fusion.7, f32[128,768]{1,0:T(8,128)S(1)} %get-tuple-element.21, f32[128,768]{1,0:T(8,128)S(1)} %collective-permute-done.9, f32[128,768]{1,0:T(8,128)S(1)} %get-tuple-element.20, f32[128,128]{1,0:T(8,128)S(1)} %bitcast.70, f32[128,128]{1,0:T(8,128)S(1)} %copy.52, ...), kind=kOutput, calls=%fused_computation.35 | convolution fusion | flops 983826432 | bytes 3588096 | tf_op jit(solution)/shard_map/dot_general | solution.py:10
  49.0 1.6 %collective-permute-start.19 = (f32[32,128]{1,0:T(8,128)S(1)}, f32[32,128]{1,0:T(8,128)S(1)}, u32[]{:S(2)}, u32[]{:S(2)}) collective-permute-start(f32[32,128]{1,0:T(8,128)S(1)} %convolution_subtract_fusion.12), channel_id=1, source_target_pairs={{0,4},{4,0},{8,12},{12,8},{16,20},{20,16},{24,28},{28,24},{1,5},{5... | collective-permute-start | bytes 49160 | tf_op jit(solution)/shard_map/ppermute | solution.py:21
  50.6 2.2 %collective-permute-done.19 = f32[32,128]{1,0:T(8,128)S(1)} collective-permute-done((f32[32,128]{1,0:T(8,128)S(1)}, f32[32,128]{1,0:T(8,128)S(1)}, u32[]{:S(2)}, u32[]{:S(2)}) %collective-permute-start.19) | collective-permute-done | bytes 16416 | tf_op jit(solution)/shard_map/ppermute | solution.py:21
  52.8 2.4 %collective-permute-done.18 = f32[32,128]{1,0:T(8,128)S(1)} collective-permute-done((f32[32,128]{1,0:T(8,128)S(1)}, f32[32,128]{1,0:T(8,128)S(1)}, u32[]{:S(2)}, u32[]{:S(2)}) %collective-permute-start.18) | collective-permute-done | bytes 16416 | tf_op jit(solution)/shard_map/ppermute | solution.py:21
  55.5 3.4 %collective-permute-start.20 = (f32[32,128]{1,0:T(8,128)S(1)}, f32[32,128]{1,0:T(8,128)S(1)}, u32[]{:S(2)}, u32[]{:S(2)}) collective-permute-start(f32[32,128]{1,0:T(8,128)S(1)} %convolution_subtract_fusion.11), channel_id=1, source_target_pairs={{0,24},{4,28},{8,16},{12,20},{16,8},{20,12},{24,0},{28,4},{1,25},{... | collective-permute-start | bytes 49160 | tf_op jit(solution)/shard_map/ppermute | solution.py:21
  59.2 1.9 %collective-permute-done.20 = f32[32,128]{1,0:T(8,128)S(1)} collective-permute-done((f32[32,128]{1,0:T(8,128)S(1)}, f32[32,128]{1,0:T(8,128)S(1)}, u32[]{:S(2)}, u32[]{:S(2)}) %collective-permute-start.20) | collective-permute-done | bytes 16416 | tf_op jit(solution)/shard_map/ppermute | solution.py:21
  61.7 4.3 %collective-permute-done.22 = f32[32,128]{1,0:T(8,128)S(1)} collective-permute-done((f32[32,128]{1,0:T(8,128)S(1)}, f32[32,128]{1,0:T(8,128)S(1)}, u32[]{:S(2)}, u32[]{:S(2)}) %collective-permute-start.22) | collective-permute-done | bytes 16416 | tf_op jit(solution)/shard_map/ppermute | solution.py:21
  67.5 3.4 %collective-permute-done.23 = f32[32,128]{1,0:T(8,128)S(1)} collective-permute-done((f32[32,128]{1,0:T(8,128)S(1)}, f32[32,128]{1,0:T(8,128)S(1)}, u32[]{:S(2)}, u32[]{:S(2)}) %collective-permute-start.23) | collective-permute-done | bytes 16416 | tf_op jit(solution)/shard_map/ppermute | solution.py:21
  72.2 2.5 %collective-permute-start.25 = (f32[32,128]{1,0:T(8,128)S(1)}, f32[32,128]{1,0:T(8,128)S(1)}, u32[]{:S(2)}, u32[]{:S(2)}) collective-permute-start(f32[32,128]{1,0:T(8,128)S(1)} %get-tuple-element.28), channel_id=1, source_target_pairs={{0,24},{4,28},{8,16},{12,20},{16,8},{20,12},{24,0},{28,4},{1,25},{... | collective-permute-start | bytes 49160 | tf_op jit(solution)/shard_map/ppermute | solution.py:21
  75.0 2.8 %collective-permute-done.25 = f32[32,128]{1,0:T(8,128)S(1)} collective-permute-done((f32[32,128]{1,0:T(8,128)S(1)}, f32[32,128]{1,0:T(8,128)S(1)}, u32[]{:S(2)}, u32[]{:S(2)}) %collective-permute-start.25) | collective-permute-done | bytes 16416 | tf_op jit(solution)/shard_map/ppermute | solution.py:21
  79.3 2.2 %fusion.29 = f32[128,256]{1,0:T(8,128)S(1)} fusion(f32[1024,256]{1,0:T(8,128)S(1)} %fusion.1, f32[256,128]{1,0:T(8,128)S(1)} %get-tuple-element.23, f32[256,128]{1,0:T(8,128)} %collective-permute-done.29, f32[256,128]{1,0:T(8,128)S(1)} %get-tuple-element.22, f32[256,128]{1,0:T(8,128)} %bitcast.11), kind=kOutput, calls=%fused_computation.49 | convolution fusion | flops 403046400 | bytes 1703936 | tf_op jit(solution)/shard_map/dot_general | solution.py:10
  81.8 1.5 %collective-permute-done.27 = f32[32,128]{1,0:T(8,128)S(1)} collective-permute-done((f32[32,128]{1,0:T(8,128)S(1)}, f32[32,128]{1,0:T(8,128)S(1)}, u32[]{:S(2)}, u32[]{:S(2)}) %collective-permute-start.27) | collective-permute-done | bytes 16416 | tf_op jit(solution)/shard_map/ppermute | solution.py:21
  89.9 1.6 %collective-permute-done.32 = f32[32,82]{1,0:T(8,128)S(1)} collective-permute-done((f32[32,82]{1,0:T(8,128)S(1)}, f32[32,82]{1,0:T(8,128)S(1)}, u32[]{:S(2)}, u32[]{:S(2)}) %collective-permute-start.32) | collective-permute-done | bytes 10528 | tf_op jit(solution)/shard_map/ppermute | solution.py:21
  92.9 4.3 %all-to-all-start = ((f32[8,32,82]{2,1,0:T(8,128)}), f32[8,32,82]{2,1,0:T(8,128)S(1)}, u32[]{:S(2)}, u32[]{:S(2)}) async-start(f32[8,32,82]{2,1,0:T(8,128)} %broadcast_in_dim.26), calls=%async_computation | async-start | bytes 262144 | tf_op jit(solution)/shard_map/all_to_all | solution.py:167
  99.9 2.8 %collective-permute-done.35 = f32[50,50]{1,0:T(8,128)S(1)} collective-permute-done((f32[50,50]{1,0:T(8,128)S(1)}, f32[50,50]{1,0:T(8,128)S(1)}, u32[]{:S(2)}, u32[]{:S(2)}) %collective-permute-start.35) | collective-permute-done | bytes 10032 | tf_op jit(solution)/shard_map/ppermute | solution.py:21
  102.7 2.0 %collective-permute-start.36 = (f32[50,50]{1,0:T(8,128)S(1)}, f32[50,50]{1,0:T(8,128)S(1)}, u32[]{:S(2)}, u32[]{:S(2)}) collective-permute-start(f32[50,50]{1,0:T(8,128)S(1)} %add.176), channel_id=1, source_target_pairs={{0,4},{4,0},{8,12},{12,8},{16,20},{20,16},{24,28},{28,24},{1,5},{5... | collective-permute-start | bytes 30008 | tf_op jit(solution)/shard_map/ppermute | solution.py:21
  104.7 1.8 %collective-permute-done.36 = f32[50,50]{1,0:T(8,128)S(1)} collective-permute-done((f32[50,50]{1,0:T(8,128)S(1)}, f32[50,50]{1,0:T(8,128)S(1)}, u32[]{:S(2)}, u32[]{:S(2)}) %collective-permute-start.36) | collective-permute-done | bytes 10032 | tf_op jit(solution)/shard_map/ppermute | solution.py:21
  106.6 2.0 %collective-permute-start.37 = (f32[50,50]{1,0:T(8,128)S(1)}, f32[50,50]{1,0:T(8,128)S(1)}, u32[]{:S(2)}, u32[]{:S(2)}) collective-permute-start(f32[50,50]{1,0:T(8,128)S(1)} %add.177), channel_id=1, source_target_pairs={{0,8},{4,12},{8,0},{12,4},{16,24},{20,28},{24,16},{28,20},{1,9},{5... | collective-permute-start | bytes 30008 | tf_op jit(solution)/shard_map/ppermute | solution.py:21
  108.6 1.8 %collective-permute-done.37 = f32[50,50]{1,0:T(8,128)S(1)} collective-permute-done((f32[50,50]{1,0:T(8,128)S(1)}, f32[50,50]{1,0:T(8,128)S(1)}, u32[]{:S(2)}, u32[]{:S(2)}) %collective-permute-start.37) | collective-permute-done | bytes 10032 | tf_op jit(solution)/shard_map/ppermute | solution.py:21
  110.4 3.1 %collective-permute-start.38 = (f32[50,50]{1,0:T(8,128)S(1)}, f32[50,50]{1,0:T(8,128)S(1)}, u32[]{:S(2)}, u32[]{:S(2)}) collective-permute-start(f32[50,50]{1,0:T(8,128)S(1)} %add.178), channel_id=1, source_target_pairs={{0,16},{4,20},{8,24},{12,28},{16,0},{20,4},{24,8},{28,12},{1,17},{... | collective-permute-start | bytes 30008 | tf_op jit(solution)/shard_map/ppermute | solution.py:21
  113.7 1.7 %collective-permute-done.38 = f32[50,50]{1,0:T(8,128)S(1)} collective-permute-done((f32[50,50]{1,0:T(8,128)S(1)}, f32[50,50]{1,0:T(8,128)S(1)}, u32[]{:S(2)}, u32[]{:S(2)}) %collective-permute-start.38) | collective-permute-done | bytes 10032 | tf_op jit(solution)/shard_map/ppermute | solution.py:21
  116.8 2.9 %cholesky.16 = f32[32,32]{1,0:T(8,128)S(1)} custom-call(f32[32,32]{1,0:T(8,128)S(1)} %fusion.81), custom_call_target="Cholesky" | custom-call | tf_op jit(solution)/shard_map/jit(cholesky)/cholesky | solution.py:182
  121.1 2.4 %custom-call.6 = f32[1,32,32]{1,2,0:T(8,128)S(1)} custom-call(f32[1,32,32]{2,1,0:T(8,128)S(1)} %get-tuple-element.31), custom_call_target="InvertDiagBlocksLowerTriangular" | custom-call | tf_op jit(solution)/shard_map/triangular_solve | solution.py:184
  (156 shorter events, 43.4 us)
Async XLA Ops:
  0.6 36.2 %collective-permute-start.13 = (f32[32,128]{1,0:T(8,128)}, f32[32,128]{1,0:T(8,128)}, u32[]{:S(2)}, u32[]{:S(2)}) collective-permute-start(f32[32,128]{1,0:T(8,128)} %param.15), channel_id=1, source_target_pairs={{0,3},{1,2},{2,1},{3,0},{4,7},{5,6},{6,5},{7,4},{8,11},{9,10},{10,... | collective-permute-start | bytes 49160 | tf_op jit(solution)/shard_map/ppermute | solution.py:21
  3.1 34.9 %collective-permute-start.12 = (f32[32,128]{1,0:T(8,128)}, f32[32,128]{1,0:T(8,128)}, u32[]{:S(2)}, u32[]{:S(2)}) collective-permute-start(f32[32,128]{1,0:T(8,128)} %param.15), channel_id=1, source_target_pairs={{0,2},{1,3},{2,0},{3,1},{4,6},{5,7},{6,4},{7,5},{8,10},{9,11},{10,... | collective-permute-start | bytes 49160 | tf_op jit(solution)/shard_map/ppermute | solution.py:21
  3.8 11.4 %collective-permute-start.6 = (s32[1,128]{1,0:T(1,128)}, s32[1,128]{1,0:T(1,128)S(1)}, u32[]{:S(2)}, u32[]{:S(2)}) collective-permute-start(s32[1,128]{1,0:T(1,128)} %param.23), channel_id=1, source_target_pairs={{0,16},{4,20},{8,24},{12,28},{16,0},{20,4},{24,8},{28,12},{1,17},{... | collective-permute-start | bytes 1544 | tf_op jit(solution)/shard_map/ppermute | solution.py:21
  6.3 9.2 %collective-permute-start.7 = (s32[1,128]{1,0:T(1,128)}, s32[1,128]{1,0:T(1,128)S(1)}, u32[]{:S(2)}, u32[]{:S(2)}) collective-permute-start(s32[1,128]{1,0:T(1,128)} %param.23), channel_id=1, source_target_pairs={{0,8},{4,12},{8,0},{12,4},{16,24},{20,28},{24,16},{28,20},{1,9},{5... | collective-permute-start | bytes 1544 | tf_op jit(solution)/shard_map/ppermute | solution.py:21
  7.9 8.2 %collective-permute-start.8 = (s32[1,128]{1,0:T(1,128)}, s32[1,128]{1,0:T(1,128)S(1)}, u32[]{:S(2)}, u32[]{:S(2)}) collective-permute-start(s32[1,128]{1,0:T(1,128)} %param.23), channel_id=1, source_target_pairs={{0,4},{4,0},{8,12},{12,8},{16,20},{20,16},{24,28},{28,24},{1,5},{5... | collective-permute-start | bytes 1544 | tf_op jit(solution)/shard_map/ppermute | solution.py:21
  15.2 5.4 %collective-permute-start.3 = (s32[1,128]{1,0:T(1,128)S(1)}, s32[1,128]{1,0:T(1,128)S(1)}, u32[]{:S(2)}, u32[]{:S(2)}) collective-permute-start(s32[1,128]{1,0:T(1,128)S(1)} %copy-done.14), channel_id=1, source_target_pairs={{0,24},{4,28},{8,16},{12,20},{16,8},{20,12},{24,0},{28,4},{1,25},{... | collective-permute-start | bytes 1544 | tf_op jit(solution)/shard_map/ppermute | solution.py:21
  15.5 5.1 %collective-permute-start.4 = (s32[1,128]{1,0:T(1,128)S(1)}, s32[1,128]{1,0:T(1,128)S(1)}, u32[]{:S(2)}, u32[]{:S(2)}) collective-permute-start(s32[1,128]{1,0:T(1,128)S(1)} %copy-done.14), channel_id=1, source_target_pairs={{0,12},{4,8},{8,4},{12,0},{16,28},{20,24},{24,20},{28,16},{1,13},{... | collective-permute-start | bytes 1544 | tf_op jit(solution)/shard_map/ppermute | solution.py:21
  16.1 6.0 %collective-permute-start.5 = (s32[1,128]{1,0:T(1,128)S(1)}, s32[1,128]{1,0:T(1,128)S(1)}, u32[]{:S(2)}, u32[]{:S(2)}) collective-permute-start(s32[1,128]{1,0:T(1,128)S(1)} %copy-done.13), channel_id=1, source_target_pairs={{0,4},{4,0},{8,12},{12,8},{16,20},{20,16},{24,28},{28,24},{1,5},{5... | collective-permute-start | bytes 1544 | tf_op jit(solution)/shard_map/ppermute | solution.py:21
  20.6 13.8 %collective-permute-start.2 = (f32[32,256]{1,0:T(8,128)S(1)}, f32[32,256]{1,0:T(8,128)S(1)}, u32[]{:S(2)}, u32[]{:S(2)}) collective-permute-start(f32[32,256]{1,0:T(8,128)S(1)} %copy-done.10), channel_id=1, source_target_pairs={{0,3},{1,2},{2,1},{3,0},{4,7},{5,6},{6,5},{7,4},{8,11},{9,10},{10,... | collective-permute-start | bytes 98312 | tf_op jit(solution)/shard_map/ppermute | solution.py:21
  20.7 14.3 %collective-permute-start.1 = (f32[32,256]{1,0:T(8,128)S(1)}, f32[32,256]{1,0:T(8,128)S(1)}, u32[]{:S(2)}, u32[]{:S(2)}) collective-permute-start(f32[32,256]{1,0:T(8,128)S(1)} %copy-done.10), channel_id=1, source_target_pairs={{0,2},{1,3},{2,0},{3,1},{4,6},{5,7},{6,4},{7,5},{8,10},{9,11},{10,... | collective-permute-start | bytes 98312 | tf_op jit(solution)/shard_map/ppermute | solution.py:21
  22.1 11.4 %collective-permute-start.9 = (f32[128,768]{1,0:T(8,128)S(1)}, f32[128,768]{1,0:T(8,128)S(1)}, u32[]{:S(2)}, u32[]{:S(2)}) collective-permute-start(f32[128,768]{1,0:T(8,128)S(1)} %pad_maximum_fusion.4), channel_id=1, source_target_pairs={{0,2},{1,3},{2,0},{3,1},{4,6},{5,7},{6,4},{7,5},{8,10},{9,11},{10,... | collective-permute-start | bytes 1179656 | tf_op jit(solution)/shard_map/ppermute | solution.py:21
  34.5 4.3 %collective-permute-start.11 = (f32[32,128]{1,0:T(8,128)}, f32[32,128]{1,0:T(8,128)S(1)}, u32[]{:S(2)}, u32[]{:S(2)}) collective-permute-start(f32[32,128]{1,0:T(8,128)} %param.15), channel_id=1, source_target_pairs={{0,1},{1,0},{2,3},{3,2},{4,5},{5,4},{6,7},{7,6},{8,9},{9,8},{10,11... | collective-permute-start | bytes 49160 | tf_op jit(solution)/shard_map/ppermute | solution.py:21
  35.0 31.5 %collective-permute-start.29 = (f32[256,128]{1,0:T(8,128)}, f32[256,128]{1,0:T(8,128)}, u32[]{:S(2)}, u32[]{:S(2)}) collective-permute-start(f32[256,128]{1,0:T(8,128)} %bitcast.11), channel_id=1, source_target_pairs={{0,2},{1,3},{2,0},{3,1},{4,6},{5,7},{6,4},{7,5},{8,10},{9,11},{10,... | collective-permute-start | bytes 393224 | tf_op jit(solution)/shard_map/ppermute | solution.py:21
  36.0 5.8 %collective-permute-start.10 = (f32[256,768]{1,0:T(8,128)}, f32[256,768]{1,0:T(8,128)}, u32[]{:S(2)}, u32[]{:S(2)}) collective-permute-start(f32[256,768]{1,0:T(8,128)} %pad_maximum_fusion.3), channel_id=1, source_target_pairs={{0,1},{1,0},{2,3},{3,2},{4,5},{5,4},{6,7},{7,6},{8,9},{9,8},{10,11... | collective-permute-start | bytes 2359304 | tf_op jit(solution)/shard_map/ppermute | solution.py:21
  36.9 4.2 %collective-permute-start.15 = (f32[32,128]{1,0:T(8,128)S(1)}, f32[32,128]{1,0:T(8,128)S(1)}, u32[]{:S(2)}, u32[]{:S(2)}) collective-permute-start(f32[32,128]{1,0:T(8,128)S(1)} %fusion.60), channel_id=1, source_target_pairs={{0,2},{1,3},{2,0},{3,1},{4,6},{5,7},{6,4},{7,5},{8,10},{9,11},{10,... | collective-permute-start | bytes 49160 | tf_op jit(solution)/shard_map/ppermute | solution.py:21
  41.2 7.5 %collective-permute-start.17 = (f32[32,128]{1,0:T(8,128)S(1)}, f32[32,128]{1,0:T(8,128)S(1)}, u32[]{:S(2)}, u32[]{:S(2)}) collective-permute-start(f32[32,128]{1,0:T(8,128)S(1)} %add_add_fusion.1), channel_id=1, source_target_pairs={{0,4},{4,0},{8,12},{12,8},{16,20},{20,16},{24,28},{28,24},{1,5},{5... | collective-permute-start | bytes 49160 | tf_op jit(solution)/shard_map/ppermute | solution.py:21
  49.0 3.8 %collective-permute-start.19 = (f32[32,128]{1,0:T(8,128)S(1)}, f32[32,128]{1,0:T(8,128)S(1)}, u32[]{:S(2)}, u32[]{:S(2)}) collective-permute-start(f32[32,128]{1,0:T(8,128)S(1)} %convolution_subtract_fusion.12), channel_id=1, source_target_pairs={{0,4},{4,0},{8,12},{12,8},{16,20},{20,16},{24,28},{28,24},{1,5},{5... | collective-permute-start | bytes 49160 | tf_op jit(solution)/shard_map/ppermute | solution.py:21
  50.5 4.6 %collective-permute-start.18 = (f32[32,128]{1,0:T(8,128)S(1)}, f32[32,128]{1,0:T(8,128)S(1)}, u32[]{:S(2)}, u32[]{:S(2)}) collective-permute-start(f32[32,128]{1,0:T(8,128)S(1)} %convolution_subtract_fusion.12), channel_id=1, source_target_pairs={{0,12},{4,8},{8,4},{12,0},{16,28},{20,24},{24,20},{28,16},{1,13},{... | collective-permute-start | bytes 49160 | tf_op jit(solution)/shard_map/ppermute | solution.py:21
  55.4 3.8 %collective-permute-start.21 = (f32[32,128]{1,0:T(8,128)S(1)}, f32[32,128]{1,0:T(8,128)S(1)}, u32[]{:S(2)}, u32[]{:S(2)}) collective-permute-start(f32[32,128]{1,0:T(8,128)S(1)} %convolution_subtract_fusion.11), channel_id=1, source_target_pairs={{0,8},{4,12},{8,0},{12,4},{16,24},{20,28},{24,16},{28,20},{1,9},{5... | collective-permute-start | bytes 49160 | tf_op jit(solution)/shard_map/ppermute | solution.py:21
  55.5 5.6 %collective-permute-start.20 = (f32[32,128]{1,0:T(8,128)S(1)}, f32[32,128]{1,0:T(8,128)S(1)}, u32[]{:S(2)}, u32[]{:S(2)}) collective-permute-start(f32[32,128]{1,0:T(8,128)S(1)} %convolution_subtract_fusion.11), channel_id=1, source_target_pairs={{0,24},{4,28},{8,16},{12,20},{16,8},{20,12},{24,0},{28,4},{1,25},{... | collective-permute-start | bytes 49160 | tf_op jit(solution)/shard_map/ppermute | solution.py:21
  61.3 4.7 %collective-permute-start.22 = (f32[32,128]{1,0:T(8,128)S(1)}, f32[32,128]{1,0:T(8,128)S(1)}, u32[]{:S(2)}, u32[]{:S(2)}) collective-permute-start(f32[32,128]{1,0:T(8,128)S(1)} %convolution_subtract_fusion.10), channel_id=1, source_target_pairs={{0,16},{4,20},{8,24},{12,28},{16,0},{20,4},{24,8},{28,12},{1,17},{... | collective-permute-start | bytes 49160 | tf_op jit(solution)/shard_map/ppermute | solution.py:21
  66.3 4.7 %collective-permute-start.23 = (f32[32,128]{1,0:T(8,128)S(1)}, f32[32,128]{1,0:T(8,128)S(1)}, u32[]{:S(2)}, u32[]{:S(2)}) collective-permute-start(f32[32,128]{1,0:T(8,128)S(1)} %slice_subtract_fusion), channel_id=1, source_target_pairs={{0,16},{4,20},{8,24},{12,28},{16,0},{20,4},{24,8},{28,12},{1,17},{... | collective-permute-start | bytes 49160 | tf_op jit(solution)/shard_map/ppermute | solution.py:21
  67.5 7.3 %collective-permute-start.30 = (f32[512,128]{1,0:T(8,128)S(1)}, f32[512,128]{1,0:T(8,128)S(1)}, u32[]{:S(2)}, u32[]{:S(2)}) collective-permute-start(f32[512,128]{1,0:T(8,128)S(1)} %pad_maximum_fusion.5), channel_id=1, source_target_pairs={{0,1},{1,0},{2,3},{3,2},{4,5},{5,4},{6,7},{7,6},{8,9},{9,8},{10,11... | collective-permute-start | bytes 786440 | tf_op jit(solution)/shard_map/ppermute | solution.py:21
  71.2 3.8 %collective-permute-start.24 = (f32[32,128]{1,0:T(8,128)S(1)}, f32[32,128]{1,0:T(8,128)S(1)}, u32[]{:S(2)}, u32[]{:S(2)}) collective-permute-start(f32[32,128]{1,0:T(8,128)S(1)} %get-tuple-element.29), channel_id=1, source_target_pairs={{0,8},{4,12},{8,0},{12,4},{16,24},{20,28},{24,16},{28,20},{1,9},{5... | collective-permute-start | bytes 49160 | tf_op jit(solution)/shard_map/ppermute | solution.py:21
  72.2 5.5 %collective-permute-start.25 = (f32[32,128]{1,0:T(8,128)S(1)}, f32[32,128]{1,0:T(8,128)S(1)}, u32[]{:S(2)}, u32[]{:S(2)}) collective-permute-start(f32[32,128]{1,0:T(8,128)S(1)} %get-tuple-element.28), channel_id=1, source_target_pairs={{0,24},{4,28},{8,16},{12,20},{16,8},{20,12},{24,0},{28,4},{1,25},{... | collective-permute-start | bytes 49160 | tf_op jit(solution)/shard_map/ppermute | solution.py:21
  78.7 4.6 %collective-permute-start.27 = (f32[32,128]{1,0:T(8,128)S(1)}, f32[32,128]{1,0:T(8,128)S(1)}, u32[]{:S(2)}, u32[]{:S(2)}) collective-permute-start(f32[32,128]{1,0:T(8,128)S(1)} %get-tuple-element.26), channel_id=1, source_target_pairs={{0,12},{4,8},{8,4},{12,0},{16,28},{20,24},{24,20},{28,16},{1,13},{... | collective-permute-start | bytes 49160 | tf_op jit(solution)/shard_map/ppermute | solution.py:21
  83.5 3.8 %collective-permute-start.28 = (f32[32,128]{1,0:T(8,128)S(1)}, f32[32,128]{1,0:T(8,128)S(1)}, u32[]{:S(2)}, u32[]{:S(2)}) collective-permute-start(f32[32,128]{1,0:T(8,128)S(1)} %slice.125), channel_id=1, source_target_pairs={{0,4},{4,0},{8,12},{12,8},{16,20},{20,16},{24,28},{28,24},{1,5},{5... | collective-permute-start | bytes 49160 | tf_op jit(solution)/shard_map/ppermute | solution.py:21
  92.9 20.6 %all-to-all-start = ((f32[8,32,82]{2,1,0:T(8,128)}), f32[8,32,82]{2,1,0:T(8,128)S(1)}, u32[]{:S(2)}, u32[]{:S(2)}) async-start(f32[8,32,82]{2,1,0:T(8,128)} %broadcast_in_dim.26), calls=%async_computation | async-start | bytes 262144 | tf_op jit(solution)/shard_map/all_to_all | solution.py:167
  98.8 3.9 %collective-permute-start.35 = (f32[50,50]{1,0:T(8,128)S(1)}, f32[50,50]{1,0:T(8,128)S(1)}, u32[]{:S(2)}, u32[]{:S(2)}) collective-permute-start(f32[50,50]{1,0:T(8,128)S(1)} %add.175), channel_id=1, source_target_pairs={{0,2},{1,3},{2,0},{3,1},{4,6},{5,7},{6,4},{7,5},{8,10},{9,11},{10,... | collective-permute-start | bytes 30008 | tf_op jit(solution)/shard_map/ppermute | solution.py:21
  102.7 3.9 %collective-permute-start.36 = (f32[50,50]{1,0:T(8,128)S(1)}, f32[50,50]{1,0:T(8,128)S(1)}, u32[]{:S(2)}, u32[]{:S(2)}) collective-permute-start(f32[50,50]{1,0:T(8,128)S(1)} %add.176), channel_id=1, source_target_pairs={{0,4},{4,0},{8,12},{12,8},{16,20},{20,16},{24,28},{28,24},{1,5},{5... | collective-permute-start | bytes 30008 | tf_op jit(solution)/shard_map/ppermute | solution.py:21
  106.6 3.9 %collective-permute-start.37 = (f32[50,50]{1,0:T(8,128)S(1)}, f32[50,50]{1,0:T(8,128)S(1)}, u32[]{:S(2)}, u32[]{:S(2)}) collective-permute-start(f32[50,50]{1,0:T(8,128)S(1)} %add.177), channel_id=1, source_target_pairs={{0,8},{4,12},{8,0},{12,4},{16,24},{20,28},{24,16},{28,20},{1,9},{5... | collective-permute-start | bytes 30008 | tf_op jit(solution)/shard_map/ppermute | solution.py:21
  110.4 5.0 %collective-permute-start.38 = (f32[50,50]{1,0:T(8,128)S(1)}, f32[50,50]{1,0:T(8,128)S(1)}, u32[]{:S(2)}, u32[]{:S(2)}) collective-permute-start(f32[50,50]{1,0:T(8,128)S(1)} %add.178), channel_id=1, source_target_pairs={{0,16},{4,20},{8,24},{12,28},{16,0},{20,4},{24,8},{28,12},{1,17},{... | collective-permute-start | bytes 30008 | tf_op jit(solution)/shard_map/ppermute | solution.py:21
  (23 other events, 92.6 us)

commit v2 on v1

v2 whole, which is shorter than its diff:
```python
import jax
import jax.numpy as jnp
from jax import lax
from jax.experimental import pallas as pl
from jax.experimental.pallas import tpu as pltpu
from jax.sharding import PartitionSpec as P


exact_mode = lax.Precision.HIGHEST


def mm(former, latter, left=1, right=0):
    return lax.dot_general(
        former,
        latter,
        (((left,), (right,)), ((), ())),
        precision=exact_mode,
        preferred_element_type=jnp.float32,
    )


def swap(value, axis, mask):
    count = lax.axis_size(axis)
    return lax.ppermute(value, axis, [(one, one ^ mask) for one in range(count)])


def gathered_pieces(value, axis):
    pieces = [value]
    count = lax.axis_size(axis)
    for mask in range(1, count):
        pieces.append(swap(value, axis, mask))
    return pieces


def doubled_pieces(value, axis):
    pieces = {0: value}
    mask = lax.axis_size(axis) // 2
    while mask:
        for k in sorted(pieces):
            pieces[k ^ mask] = swap(pieces[k], axis, mask)
        mask //= 2
    return [pieces[k] for k in sorted(pieces)]


def summed_pairwise(pieces):
    while len(pieces) > 1:
        pieces = [pieces[k] + pieces[k + 1] for k in range(0, len(pieces), 2)]
    return pieces[0]


def local_place(index, width, own):
    return jnp.bitwise_xor(index // width, own) * width + index % width


def one_hot(places, size):
    return (places[:, None] == lax.broadcasted_iota(jnp.int32, (1, size), 1)).astype(jnp.float32)


def pack(inv_ref, push_ref, pull_ref, rhs_ref, out_ref):
    width = push_ref.shape[1]
    place = 0
    for column in range(0, inv_ref.shape[1], width):
        out_ref[place : place + width, :] = inv_ref[:, column : column + width]
        place += width
    for ref in (push_ref, pull_ref, rhs_ref):
        out_ref[place : place + ref.shape[0], :] = ref[...]
        place += ref.shape[0]


def halves(value):
    high = value.astype(jnp.bfloat16)
    rest = value - high.astype(jnp.float32)
    middle = rest.astype(jnp.bfloat16)
    return high, middle, (rest - middle.astype(jnp.float32)).astype(jnp.bfloat16)


def dot(former, latter, left, right):
    return lax.dot_general(
        former, latter, (((left,), (right,)), ((), ())), preferred_element_type=jnp.float32
    )


def reduce_front(members, pivot_ref, rows_ref, *refs):
    pieces = refs[:members]
    moved_ref, up_ref, turn_ref, down_ref, push_base_ref, row_base_ref, root_ref = refs[members:]
    rows = pivot_ref.shape[1]
    width = pieces[0].shape[1]
    couple = rows_ref.shape[1] // 2
    entry = lax.broadcasted_iota(jnp.int32, (rows, rows), 0)
    hot = (entry == pivot_ref[...]).astype(jnp.float32).astype(jnp.bfloat16)
    chosen = (entry[:, : 2 * couple] == rows_ref[...]).astype(jnp.float32).astype(jnp.bfloat16)
    mapped = []
    for piece in pieces:
        inverse = jnp.concatenate(
            [piece[place : place + width, :] for place in range(0, rows, width)], 1
        )
        mapped.append(sum(dot(hot, part, 1, 1) for part in halves(inverse)))
    mapped = jnp.concatenate(mapped, 1)
    push = jnp.concatenate([piece[rows : rows + couple, :] for piece in pieces], 1)
    pull = jnp.concatenate([piece[rows + couple : rows + couple + width, :] for piece in pieces], 0)
    rhs = jnp.concatenate([piece[rows + couple + width :, :] for piece in pieces], 1)
    below = sum(dot(chosen, part, 0, 0) for part in halves(mapped))
    above = mm(pull, mapped, 0, 0)
    base = mm(rhs, mapped, 1, 0)
    moved = jnp.concatenate([below, above, base], 0)
    push_part = mm(moved, push, 1, 1)
    rows_part = sum(dot(part, chosen, 1, 0) for part in halves(moved))
    moved_ref[...] = moved[:, :width]
    up_ref[...] = push_part[: 2 * couple]
    turn_ref[...] = rows_part[: 2 * couple]
    down_ref[...] = rows_part[2 * couple : 3 * couple]
    push_base_ref[...] = push_part[3 * couple :]
    row_base_ref[...] = rows_part[3 * couple :]
    root_ref[:couple, :] = rows_part[couple : 2 * couple, :couple]
    root_ref[couple:, :] = rows_part[3 * couple :, :couple]


def finish(total_rows, inner_ref, leaf_ref, sep_ref, basis_leaf_ref, basis_sep_ref, *outs):
    q_leaf_ref, q_sep_ref, coeffs_ref, rfac_ref = outs
    block = leaf_ref.shape[0]
    rank = basis_leaf_ref.shape[0]
    inner = jnp.sum(inner_ref[...], 0) * (1.0 / total_rows)
    metric = inner[:, :rank]
    first = inner[:, rank : rank + block]
    second = first - mm(metric, first)
    third = second - mm(metric, second)
    coeffs = first + second
    gram = inner[:block, rank + block :] - mm(first, coeffs, 0, 0) - mm(second, second + third, 0, 0)
    coeffs_ref[...] = coeffs.T
    row = lax.broadcasted_iota(jnp.int32, (block, 2 * block), 0)
    lane = lax.broadcasted_iota(jnp.int32, (block, 2 * block), 1)
    table = jnp.concatenate([gram, (row == lane)[:, :block].astype(jnp.float32)], 1)
    pivots = jnp.ones((block, 2 * block), jnp.float32)
    width = 8
    for start in range(0, block, width):
        columns = [
            jnp.broadcast_to(table[:, k : k + 1], table.shape)
            for k in range(start, min(start + width, block))
        ]
        for place in range(len(columns)):
            k = start + place
            pivot = columns[place][k : k + 1, :]
            pivots = jnp.where(row == k, pivot, pivots)
            factor = jnp.where(row > k, columns[place] / pivot, 0.0)
            table = table - factor * table[k : k + 1, :]
            for later in range(place + 1, len(columns)):
                columns[later] = columns[later] - factor * columns[later][k : k + 1, :]
    table = table / jnp.sqrt(pivots)
    rfac_ref[...] = jnp.where(row <= lane, table, 0.0)[:, :block]
    back = table[:, block:]
    spread = mm(back, coeffs, 1, 1)
    q_leaf_ref[...] = mm(back, leaf_ref[...]) - mm(spread, basis_leaf_ref[...])
    q_sep_ref[...] = mm(back, sep_ref[...]) - mm(spread, basis_sep_ref[...])


def on_device(
    rhs_leaf,
    rhs_sep,
    inv_leaf,
    inv_sep,
    push_leaf,
    push_sep,
    pull_leaf,
    pull_sep,
    rows_leaf,
    rows_sep,
    pivot_leaf,
    pivot_sep,
    basis_leaf,
    basis_sep,
):
    group = lax.axis_index("leaf")
    own = lax.axis_index("front")
    groups = lax.axis_size("leaf")
    top = groups.bit_length() - 1
    leaf_rows = pivot_leaf.shape[1]
    sep_rows = pivot_sep.shape[1]
    leaf_width = rhs_leaf.shape[1]
    sep_width = rhs_sep.shape[1]
    couple = rows_leaf.shape[1]
    total_rows = groups * (leaf_rows + sep_rows)
    level = jnp.full((), top + 1, jnp.int32)
    for bit in range(top, 0, -1):
        level = jnp.where(group % 2**bit != 0, jnp.int32(bit), level)

    rhs_leaf_all = jnp.concatenate(gathered_pieces(rhs_leaf, "front"), 1)
    bulk = pl.pallas_call(
        pack,
        out_shape=jax.ShapeDtypeStruct(
            (sep_rows + 2 * couple + rhs_sep.shape[0], sep_width), jnp.float32
        ),
        name="pack",
    )(inv_sep[0], push_sep[0], pull_sep[0], rhs_sep)
    bulk = doubled_pieces(bulk, "front")

    lists = jnp.concatenate([rows_leaf, rows_sep], 0)
    lists = lax.all_to_all(
        jnp.broadcast_to(lists[None], (groups,) + lists.shape), "leaf", 0, 0
    )
    reach = jnp.where(level == 1, 0, jnp.left_shift(1, jnp.maximum(level - 2, 0)))
    upper_child = group + reach
    lower_child = jnp.where(level == 1, group - 1, jnp.where(level > top, reach, group - reach))
    kind = jnp.where(level == 1, 0, 1)
    rows = jnp.concatenate(
        [
            lax.dynamic_slice(lists, (child, kind, 0), (1, 1, couple))[0]
            for child in (lower_child, upper_child)
        ],
        1,
    )

    leaf_hot = one_hot(local_place(pivot_leaf[0], leaf_width, own), leaf_rows)
    leaf_map = mm(leaf_hot, inv_leaf[0], 0, 1)
    leaf_state = mm(rhs_leaf_all, leaf_map)
    leaf_push = summed_pairwise(
        gathered_pieces(mm(leaf_state, push_leaf[0], 1, 1), "front")
    )

    vmem = pl.BlockSpec(memory_space=pltpu.VMEM)
    block = rhs_sep.shape[0]
    shapes = (
        (3 * couple + block, sep_width),
        (2 * couple, couple),
        (2 * couple, 2 * couple),
        (couple, 2 * couple),
        (block, couple),
        (block, 2 * couple),
        (couple + block, couple),
    )
    moved, up_weights, turn_weights, down_weights, push_base, row_base, root_op = pl.pallas_call(
        lambda *refs: reduce_front(len(bulk), *refs),
        out_shape=tuple(jax.ShapeDtypeStruct(shape, jnp.float32) for shape in shapes),
        out_specs=(vmem,) * len(shapes),
        name="reduce_front",
    )(
        local_place(pivot_sep, sep_width, own),
        local_place(rows, sep_width, own),
        *bulk,
    )

    pull_leaf_all = jnp.concatenate(doubled_pieces(pull_leaf[0], "front"), 0)
    leaf_lift = mm(pull_leaf_all, leaf_map, 0, 0)

    half = groups // 2
    root_op = swap(root_op, "leaf", half)

    pair = jnp.concatenate([swap(leaf_push, "leaf", 1), leaf_push], 1)
    pair = jnp.where(level == 1, pair, 0.0)
    for height in range(2, top + 1):
        step = 2 ** (height - 2)
        term = push_base - mm(pair, up_weights)
        upper = swap(term, "leaf", step)
        lower = swap(term, "leaf", 3 * step)
        pair = jnp.where(level == height, jnp.concatenate([lower, upper], 1), pair)

    term = push_base - mm(pair, up_weights)
    above = jnp.where(level == top, root_op[couple:] - mm(term, root_op[:couple]), 0.0)
    back = swap(term, "leaf", half)

    row_base = row_base - mm(pair, turn_weights)
    for height in range(top, 1, -1):
        step = 2 ** (height - 2)
        below = row_base - mm(above, down_weights)
        upper = swap(below[:, couple:], "leaf", step)
        lower = swap(below[:, :couple], "leaf", 3 * step)
        is_upper = (group // (2 * step)) % 2 == 1
        above = jnp.where(level == height - 1, jnp.where(is_upper, upper, lower), above)
    below = row_base - mm(above, down_weights)
    leaf_above = jnp.where(level == 1, below[:, couple:], swap(below[:, :couple], "leaf", 1))
    around = jnp.concatenate([pair, above], 1)
    root_around = jnp.pad(back, ((0, 0), (couple, couple)))
    around = jnp.where(level > top, root_around, around)

    leaf_solution = leaf_state - mm(leaf_above, leaf_lift)
    sep_solution = moved[3 * couple :] - mm(
        around, moved[: 3 * couple]
    )

    rank = basis_leaf.shape[0]
    metric = mm(basis_leaf, basis_leaf, 1, 1) + mm(basis_sep, basis_sep, 1, 1)
    cross = mm(basis_leaf, leaf_solution, 1, 1) + mm(basis_sep, sep_solution, 1, 1)
    length = mm(leaf_solution, leaf_solution, 1, 1) + mm(sep_solution, sep_solution, 1, 1)
    inner = jnp.concatenate([metric, cross, jnp.pad(length, ((0, rank - block), (0, 0)))], 1)
    inner = summed_pairwise(gathered_pieces(inner, "front"))
    inner = lax.all_to_all(
        jnp.broadcast_to(inner[None], (groups,) + inner.shape), "leaf", 0, 0
    )
    q_leaf, q_sep, coeffs, rfac = pl.pallas_call(
        lambda *refs: finish(total_rows, *refs),
        out_shape=(
            jax.ShapeDtypeStruct((block, leaf_width), jnp.float32),
            jax.ShapeDtypeStruct((block, sep_width), jnp.float32),
            jax.ShapeDtypeStruct((block, rank), jnp.float32),
            jax.ShapeDtypeStruct((block, block), jnp.float32),
        ),
        name="finish",
    )(inner, leaf_solution, sep_solution, basis_leaf, basis_sep)
    return q_leaf, q_sep, coeffs.T, rfac


def solution(mesh):
    placed = (
        P(None, ("leaf", "front")),
        P(None, ("leaf", "front")),
        P("leaf", "front", None),
        P("leaf", "front", None),
        P("leaf", None, "front"),
        P("leaf", None, "front"),
        P("leaf", "front", None),
        P("leaf", "front", None),
        P("leaf", None),
        P("leaf", None),
        P("leaf", None),
        P("leaf", None),
        P(None, ("leaf", "front")),
        P(None, ("leaf", "front")),
    )

    return jax.shard_map(
        on_device,
        mesh=mesh,
        in_specs=placed,
        out_specs=(P(None, ("leaf", "front")), P(None, ("leaf", "front")), P(), P()),
        check_vma=False,
    )
```

time: 127 us -> 90 us (0.71)
  waiting for transfers between devices: 44.3 us -> 16.2 us
  Pallas kernels: 0 us -> 12.3 us
  blocking collectives: 0 us -> 12.1 us
  other arithmetic: 14.6 us -> 2.68 us
  starting transfers between devices: 44.5 us -> 33.2 us
  local copies, waits for them, and re-layouts: 6.6 us -> 1.58 us
  matrix products: 15.2 us -> 10.3 us
    ppermute x39 -> x27, waiting for transfers between devices: 44.3 us -> 16.2 us  [swap(): lax.ppermute(value, axis, [(one, one ^ mask) for one in range(count)])]
    ppermute x39 -> x27, starting transfers between devices: 40.1 us -> 27.4 us  [swap(): lax.ppermute(value, axis, [(one, one ^ mask) for one in range(count)])]
    pallas_call x0 -> x3, Pallas kernels: none -> 12.3 us  [the longest x1 6.35 us: on_device(): pl.pallas_call(lambda *refs: reduce_front(len(bulk), *refs), out_shape=tu...]
    all_to_all x0 -> x1, blocking collectives: none -> 12.1 us  [on_device(): lax.all_to_all(jnp.broadcast_to(inner[None], (groups,) + inner.shape), 'l...]
    another operation x4 -> x0, other arithmetic: 6.03 us -> none  [the longest x3 3.6 us: on_device(): lower_factor = jnp.linalg.cholesky(gram, symmetrize_input=True)]
    dot_general x23 -> x20, matrix products: 14.9 us -> 10.3 us  [mm(): lax.dot_general(former, latter, (((left,), (right,)), ((), ())), precisio...]
    convert_element_type x4 -> x0, other arithmetic: 2.93 us -> none  [one_hot(): (places[:, None] == lax.broadcasted_iota(jnp.int32, (1, size), 1)).astype...]
    slice x5 -> x0, local copies, waits for them, and re-layouts: 2.48 us -> none  [the longest x2 1.18 us: doubled_pieces(): pieces[k ^ mask] = moved[place * height:(place + 1) * height]]
  transfers between devices with their start and end apart: 40 -> 28, of which waited for: 22 -> 12; matrix products, arithmetic and copies ran while one was open for 18% -> 13% of each run, Pallas kernels for 0% -> 7%
where the time goes in v2:
time: 90 us; the launch traced here: 89.6 us
  starting transfers between devices  33.2 us (37%)
  waiting for transfers between devices  16.2 us (18%)
  Pallas kernels  12.3 us (14%)
  blocking collectives  12.1 us (13%)
  matrix products  10.3 us (11%)
  other arithmetic  2.68 us (3%)
  local copies, waits for them, and re-layouts  1.58 us (2%)
  between operations  1.15 us (1%)
    ppermute x27, starting transfers between devices, swap(): lax.ppermute(value, axis, [(one, one ^ mask) for one in range(count)])  27.4 us
    ppermute x27, waiting for transfers between devices, swap(): lax.ppermute(value, axis, [(one, one ^ mask) for one in range(count)])  16.2 us
    all_to_all x1, blocking collectives, on_device(): lax.all_to_all(jnp.broadcast_to(inner[None], (groups,) + inner.shape), 'l...  12.1 us
    dot_general x20, matrix products, mm(): lax.dot_general(former, latter, (((left,), (right,)), ((), ())), precisio...  10.3 us
    pallas_call x1, Pallas kernels, on_device(): pl.pallas_call(lambda *refs: reduce_front(len(bulk), *refs), out_shape=tu...  6.35 us
    all_to_all x1, starting transfers between devices, on_device(): lax.all_to_all(jnp.broadcast_to(lists[None], (groups,) + lists.shape), 'l...  5.83 us
    pallas_call x1, Pallas kernels, on_device(): pl.pallas_call(lambda *refs: finish(total_rows, *refs), out_shape=(jax.Sh...  4.1 us
    add x3, other arithmetic, local_place(): return jnp.bitwise_xor(index // width, own) * width + index % width  1.87 us
  transfers between devices with their start and end apart: 28, of which 12 were waited for; matrix products, arithmetic and copies ran while one was open for 13% of the time, Pallas kernels for 7%

profile of v2, /device:TPU:0, one launch (start us, length us, event | category | flops | bytes accessed | tf_op | source)
XLA Modules:
  0.0 89.6 jit_solution(5688022027424673953)
XLA Ops:
  0.6 1.8 %pack.1.refs_2_ = f32[800,128]{1,0:T(8,128)} custom-call(f32[128,512]{1,0:T(8,128)} %bitcast.46, f32[128,128]{1,0:T(8,128)} %bitcast.50, f32[128,128]{1,0:T(8,128)} %bitcast.51, f32[32,128]{1,0:T(8,128)} %rhs_ref.1), custom_call_target="tpu_custom_call" | custom-call | tf_op jit(solution)/shard_map/pack/pallas_call | solution.py:187
  2.5 3.0 %collective-permute-start.4 = (f32[800,128]{1,0:T(8,128)}, f32[800,128]{1,0:T(8,128)S(1)}, u32[]{:S(2)}, u32[]{:S(2)}) collective-permute-start(f32[800,128]{1,0:T(8,128)} %pack.1.refs_2_), channel_id=1, source_target_pairs={{0,2},{1,3},{2,0},{3,1},{4,6},{5,7},{6,4},{7,5},{8,10},{9,11},{10,... | collective-permute-start | bytes 1228808 | tf_op jit(solution)/shard_map/ppermute | solution.py:24
  6.0 1.4 %collective-permute-start.2 = (f32[32,256]{1,0:T(8,128)}, f32[32,256]{1,0:T(8,128)S(1)}, u32[]{:S(2)}, u32[]{:S(2)}) collective-permute-start(f32[32,256]{1,0:T(8,128)} %param.14), channel_id=1, source_target_pairs={{0,3},{1,2},{2,1},{3,0},{4,7},{5,6},{6,5},{7,4},{8,11},{9,10},{10,... | collective-permute-start | bytes 98312 | tf_op jit(solution)/shard_map/ppermute | solution.py:24
  8.6 5.8 %all-to-all-start = ((s32[8,2,128]{2,1,0:T(2,128)}), s32[8,2,128]{2,1,0:T(2,128)S(1)}, u32[]{:S(2)}, u32[]{:S(2)}) async-start(s32[8,2,128]{2,1,0:T(2,128)} %broadcast_in_dim.12), calls=%async_computation | async-start | bytes 16384 | tf_op jit(solution)/shard_map/all_to_all | solution.py:197
  15.2 2.6 %fusion.1 = f32[1024,256]{1,0:T(8,128)S(1)} fusion(s32[1024]{0:T(1024)S(1)} %fusion.39, f32[1,256,1024]{2,1,0:T(8,128)S(1)} %copy-done), kind=kOutput, calls=%fused_computation.2 | convolution fusion | flops 3223322624 | bytes 2101248 | tf_op jit(solution)/shard_map/dot_general | solution.py:13
  20.4 0.9 collective-permute-start.8
  22.1 1.7 %collective-permute-done.7 = f32[32,128]{1,0:T(8,128)S(1)} collective-permute-done((f32[32,128]{1,0:T(8,128)S(1)}, f32[32,128]{1,0:T(8,128)S(1)}, u32[]{:S(2)}, u32[]{:S(2)}) %collective-permute-start.7) | collective-permute-done | bytes 16416 | tf_op jit(solution)/shard_map/ppermute | solution.py:24
  23.8 1.8 %collective-permute-start.9 = (f32[32,128]{1,0:T(8,128)S(1)}, f32[32,128]{1,0:T(8,128)S(1)}, u32[]{:S(2)}, u32[]{:S(2)}) collective-permute-start(f32[32,128]{1,0:T(8,128)S(1)} %add_add_fusion.1), channel_id=1, source_target_pairs={{0,4},{4,0},{8,12},{12,8},{16,20},{20,16},{24,28},{28,24},{1,5},{5... | collective-permute-start | bytes 49160 | tf_op jit(solution)/shard_map/ppermute | solution.py:24
  27.0 6.3 %reduce_front.1 = (f32[416,128]{1,0:T(8,128)}, f32[256,128]{1,0:T(8,128)}, f32[256,256]{1,0:T(8,128)}, f32[128,256]{1,0:T(8,128)}, f32[32,128]{1,0:T(8,128)}, /*index=5*/f32[32,256]{1,0:T(8,128)}, f32[160,128]{1,0:T(8,128)}) custom-call(s32[1,512]{1,0:T(1,128)} %fusion.44.refs_0_, s32[1,256]{1,0:T(1,128)} %fusion.45.refs_1_, f32[800,128]{1,0:T(8,128)} %pack.1.refs_2_, ...), custom_call_target="tpu_custom_call" | custom-call | tf_op jit(solution)/shard_map/reduce_front/pallas_call | solution.py:230
  33.4 1.2 %convolution_subtract_fusion.6 = f32[32,128]{1,0:T(8,128)S(1)} fusion(f32[32,128]{1,0:T(8,128)} %get-tuple-element.16, f32[256,128]{1,0:T(8,128)} %get-tuple-element.17, f32[32,128]{1,0:T(8,128)S(1)} %add_add_fusion.1, f32[32,128]{1,0:T(8,128)S(1)} %collective-permute-done.9, pred[]{:T(512)S(6)} %eq.50), kind=kOutput, calls=%fused_computation.14 | convolution fusion | flops 12603392 | bytes 196609 | tf_op jit(solution)/shard_map/dot_general | solution.py:13
  34.6 1.5 %collective-permute-start.10 = (f32[32,128]{1,0:T(8,128)S(1)}, f32[32,128]{1,0:T(8,128)S(1)}, u32[]{:S(2)}, u32[]{:S(2)}) collective-permute-start(f32[32,128]{1,0:T(8,128)S(1)} %convolution_subtract_fusion.6), channel_id=1, source_target_pairs={{0,12},{4,8},{8,4},{12,0},{16,28},{20,24},{24,20},{28,16},{1,13},{... | collective-permute-start | bytes 49160 | tf_op jit(solution)/shard_map/ppermute | solution.py:24
  36.1 1.5 %collective-permute-start.11 = (f32[32,128]{1,0:T(8,128)S(1)}, f32[32,128]{1,0:T(8,128)S(1)}, u32[]{:S(2)}, u32[]{:S(2)}) collective-permute-start(f32[32,128]{1,0:T(8,128)S(1)} %convolution_subtract_fusion.6), channel_id=1, source_target_pairs={{0,4},{4,0},{8,12},{12,8},{16,20},{20,16},{24,28},{28,24},{1,5},{5... | collective-permute-start | bytes 49160 | tf_op jit(solution)/shard_map/ppermute | solution.py:24
  37.5 1.3 %collective-permute-start.21 = (f32[256,128]{1,0:T(8,128)S(1)}, f32[256,128]{1,0:T(8,128)S(1)}, u32[]{:S(2)}, u32[]{:S(2)}) collective-permute-start(f32[256,128]{1,0:T(8,128)S(1)} %bitcast.47), channel_id=1, source_target_pairs={{0,2},{1,3},{2,0},{3,1},{4,6},{5,7},{6,4},{7,5},{8,10},{9,11},{10,... | collective-permute-start | bytes 393224 | tf_op jit(solution)/shard_map/ppermute | solution.py:24
  39.8 1.1 %convolution_subtract_fusion.5 = f32[32,128]{1,0:T(8,128)S(1)} fusion(f32[32,128]{1,0:T(8,128)} %get-tuple-element.16, f32[256,128]{1,0:T(8,128)} %get-tuple-element.17, f32[32,128]{1,0:T(8,128)S(1)} %collective-permute-done.11, f32[32,128]{1,0:T(8,128)S(1)} %collective-permute-done.10, f32[32,128]{1,0:T(8,128)S(1)} %add_add_fusion.1, ...), kind=kOutput, calls=%fused_computation.13 | convolution fusion | flops 12619776 | bytes 229378 | tf_op jit(solution)/shard_map/dot_general | solution.py:13
  40.9 2.8 %collective-permute-start.12 = (f32[32,128]{1,0:T(8,128)S(1)}, f32[32,128]{1,0:T(8,128)S(1)}, u32[]{:S(2)}, u32[]{:S(2)}) collective-permute-start(f32[32,128]{1,0:T(8,128)S(1)} %convolution_subtract_fusion.5), channel_id=1, source_target_pairs={{0,24},{4,28},{8,16},{12,20},{16,8},{20,12},{24,0},{28,4},{1,25},{... | collective-permute-start | bytes 49160 | tf_op jit(solution)/shard_map/ppermute | solution.py:24
  44.1 1.5 %collective-permute-start.14 = (f32[160,128]{1,0:T(8,128)}, f32[160,128]{1,0:T(8,128)S(1)}, u32[]{:S(2)}, u32[]{:S(2)}) collective-permute-start(f32[160,128]{1,0:T(8,128)} %get-tuple-element.19), channel_id=1, source_target_pairs={{0,16},{4,20},{8,24},{12,28},{16,0},{20,4},{24,8},{28,12},{1,17},{... | collective-permute-start | bytes 245768 | tf_op jit(solution)/shard_map/ppermute | solution.py:24
  45.6 0.9 collective-permute-done.12
  46.5 1.4 %collective-permute-done.13 = f32[32,128]{1,0:T(8,128)S(1)} collective-permute-done((f32[32,128]{1,0:T(8,128)S(1)}, f32[32,128]{1,0:T(8,128)S(1)}, u32[]{:S(2)}, u32[]{:S(2)}) %collective-permute-start.13) | collective-permute-done | bytes 16416 | tf_op jit(solution)/shard_map/ppermute | solution.py:24
  48.0 1.2 %fusion.60 = f32[32,256]{1,0:T(8,128)S(1)} fusion(f32[32,256]{1,0:T(8,128)S(1)} %maximum_select_fusion.4, f32[256,256]{1,0:T(8,128)} %get-tuple-element.18), kind=kOutput, calls=%fused_computation.100 | convolution fusion | flops 25165824 | bytes 327680 | tf_op jit(solution)/shard_map/dot_general | solution.py:13
  50.1 1.9 %collective-permute-start.15 = (f32[32,128]{1,0:T(8,128)S(1)}, f32[32,128]{1,0:T(8,128)S(1)}, u32[]{:S(2)}, u32[]{:S(2)}) collective-permute-start(f32[32,128]{1,0:T(8,128)S(1)} %get-tuple-element.29), channel_id=1, source_target_pairs={{0,8},{4,12},{8,0},{12,4},{16,24},{20,28},{24,16},{28,20},{1,9},{5... | collective-permute-start | bytes 49160 | tf_op jit(solution)/shard_map/ppermute | solution.py:24
  52.0 1.1 %collective-permute-start.16 = (f32[32,128]{1,0:T(8,128)S(1)}, f32[32,128]{1,0:T(8,128)S(1)}, u32[]{:S(2)}, u32[]{:S(2)}) collective-permute-start(f32[32,128]{1,0:T(8,128)S(1)} %get-tuple-element.28), channel_id=1, source_target_pairs={{0,24},{4,28},{8,16},{12,20},{16,8},{20,12},{24,0},{28,4},{1,25},{... | collective-permute-start | bytes 49160 | tf_op jit(solution)/shard_map/ppermute | solution.py:24
  54.0 3.6 %collective-permute-done.16 = f32[32,128]{1,0:T(8,128)S(1)} collective-permute-done((f32[32,128]{1,0:T(8,128)S(1)}, f32[32,128]{1,0:T(8,128)S(1)}, u32[]{:S(2)}, u32[]{:S(2)}) %collective-permute-start.16) | collective-permute-done | bytes 16416 | tf_op jit(solution)/shard_map/ppermute | solution.py:24
  57.7 1.2 %collective-permute-start.17 = (f32[32,128]{1,0:T(8,128)S(1)}, f32[32,128]{1,0:T(8,128)S(1)}, u32[]{:S(2)}, u32[]{:S(2)}) collective-permute-start(f32[32,128]{1,0:T(8,128)S(1)} %get-tuple-element.27), channel_id=1, source_target_pairs={{0,4},{4,0},{8,12},{12,8},{16,20},{20,16},{24,28},{28,24},{1,5},{5... | collective-permute-start | bytes 49160 | tf_op jit(solution)/shard_map/ppermute | solution.py:24
  58.9 1.1 %fusion.6 = f32[128,256]{1,0:T(8,128)S(1)} fusion(f32[1024,256]{1,0:T(8,128)S(1)} %fusion.1, f32[256,128]{1,0:T(8,128)S(1)} %collective-permute-done.22, f32[256,128]{1,0:T(8,128)S(1)} %collective-permute-done.21, f32[256,128]{1,0:T(8,128)S(1)} %collective-permute-done.20, f32[256,128]{1,0:T(8,128)S(1)} %bitcast.49), kind=kOutput, calls=%fused_computation.16 | convolution fusion | flops 403046400 | bytes 1703936 | tf_op jit(solution)/shard_map/dot_general | solution.py:13
  60.0 2.1 %collective-permute-start.23 = (f32[32,128]{1,0:T(8,128)S(1)}, f32[32,128]{1,0:T(8,128)S(1)}, u32[]{:S(2)}, u32[]{:S(2)}) collective-permute-start(f32[32,128]{1,0:T(8,128)S(1)} %convolution_subtract_fusion.4), channel_id=1, source_target_pairs={{0,16},{4,20},{8,24},{12,28},{16,0},{20,4},{24,8},{28,12},{1,17},{... | collective-permute-start | bytes 49160 | tf_op jit(solution)/shard_map/ppermute | solution.py:24
  62.1 1.4 %collective-permute-done.18 = f32[32,128]{1,0:T(8,128)S(1)} collective-permute-done((f32[32,128]{1,0:T(8,128)S(1)}, f32[32,128]{1,0:T(8,128)S(1)}, u32[]{:S(2)}, u32[]{:S(2)}) %collective-permute-start.18) | collective-permute-done | bytes 16416 | tf_op jit(solution)/shard_map/ppermute | solution.py:24
  63.8 1.0 %collective-permute-start.19 = (f32[32,128]{1,0:T(8,128)S(1)}, f32[32,128]{1,0:T(8,128)S(1)}, u32[]{:S(2)}, u32[]{:S(2)}) collective-permute-start(f32[32,128]{1,0:T(8,128)S(1)} %slice.47), channel_id=1, source_target_pairs={{0,4},{4,0},{8,12},{12,8},{16,20},{20,16},{24,28},{28,24},{1,5},{5... | collective-permute-start | bytes 49160 | tf_op jit(solution)/shard_map/ppermute | solution.py:24
  65.0 2.6 %collective-permute-done.19 = f32[32,128]{1,0:T(8,128)S(1)} collective-permute-done((f32[32,128]{1,0:T(8,128)S(1)}, f32[32,128]{1,0:T(8,128)S(1)}, u32[]{:S(2)}, u32[]{:S(2)}) %collective-permute-start.19) | collective-permute-done | bytes 16416 | tf_op jit(solution)/shard_map/ppermute | solution.py:24
  68.7 1.4 %collective-permute-start.25 = (f32[50,114]{1,0:T(8,128)S(1)}, f32[50,114]{1,0:T(8,128)S(1)}, u32[]{:S(2)}, u32[]{:S(2)}) collective-permute-start(f32[50,114]{1,0:T(8,128)S(1)} %select_maximum_fusion), channel_id=1, source_target_pairs={{0,2},{1,3},{2,0},{3,1},{4,6},{5,7},{6,4},{7,5},{8,10},{9,11},{10,... | collective-permute-start | bytes 68408 | tf_op jit(solution)/shard_map/ppermute | solution.py:24
  70.6 2.1 %collective-permute-done.25 = f32[50,114]{1,0:T(8,128)S(1)} collective-permute-done((f32[50,114]{1,0:T(8,128)S(1)}, f32[50,114]{1,0:T(8,128)S(1)}, u32[]{:S(2)}, u32[]{:S(2)}) %collective-permute-start.25) | collective-permute-done | bytes 22832 | tf_op jit(solution)/shard_map/ppermute | solution.py:24
  73.4 12.1 %all_to_all.10.refs_0_ = f32[8,50,114]{2,1,0:T(8,128)} all-to-all(f32[8,50,114]{2,1,0:T(8,128)S(1)} %broadcast_in_dim.24), channel_id=1, replica_groups=mesh['leaf'=8,'front'=4] {'leaf'}, dimensions={0} | all-to-all | bytes 364800 | tf_op jit(solution)/shard_map/all_to_all | solution.py:285
  85.5 4.1 %finish.1 = (f32[32,256]{1,0:T(8,128)}, f32[32,128]{1,0:T(8,128)}, f32[32,50]{1,0:T(8,128)}, f32[32,32]{1,0:T(8,128)}) custom-call(f32[8,50,114]{2,1,0:T(8,128)} %all_to_all.10.refs_0_, f32[32,256]{1,0:T(8,128)} %copy-done.4, f32[32,128]{1,0:T(8,128)} %copy-done.6, f32[50,256]{1,0:T(8,128)} %refs_3_.1, f32[50,128]{1,0:T(8,128)} %refs_4_.1), custom_call_target="tpu_custom_call" | custom-call | tf_op jit(solution)/shard_map/finish/pallas_call | solution.py:288
  (98 shorter events, 13.2 us)
Async XLA Ops:
  2.5 18.9 %collective-permute-start.4 = (f32[800,128]{1,0:T(8,128)}, f32[800,128]{1,0:T(8,128)S(1)}, u32[]{:S(2)}, u32[]{:S(2)}) collective-permute-start(f32[800,128]{1,0:T(8,128)} %pack.1.refs_2_), channel_id=1, source_target_pairs={{0,2},{1,3},{2,0},{3,1},{4,6},{5,7},{6,4},{7,5},{8,10},{9,11},{10,... | collective-permute-start | bytes 1228808 | tf_op jit(solution)/shard_map/ppermute | solution.py:24
  5.5 20.7 %collective-permute-start.3 = (f32[800,128]{1,0:T(8,128)}, f32[800,128]{1,0:T(8,128)S(1)}, u32[]{:S(2)}, u32[]{:S(2)}) collective-permute-start(f32[800,128]{1,0:T(8,128)} %pack.1.refs_2_), channel_id=1, source_target_pairs={{0,1},{1,0},{2,3},{3,2},{4,5},{5,4},{6,7},{7,6},{8,9},{9,8},{10,11... | collective-permute-start | bytes 1228808 | tf_op jit(solution)/shard_map/ppermute | solution.py:24
  5.5 13.0 %collective-permute-start = (f32[32,256]{1,0:T(8,128)}, f32[32,256]{1,0:T(8,128)S(1)}, u32[]{:S(2)}, u32[]{:S(2)}) collective-permute-start(f32[32,256]{1,0:T(8,128)} %param.14), channel_id=1, source_target_pairs={{0,1},{1,0},{2,3},{3,2},{4,5},{5,4},{6,7},{7,6},{8,9},{9,8},{10,11... | collective-permute-start | bytes 98312 | tf_op jit(solution)/shard_map/ppermute | solution.py:24
  6.0 12.5 %collective-permute-start.1 = (f32[32,256]{1,0:T(8,128)}, f32[32,256]{1,0:T(8,128)S(1)}, u32[]{:S(2)}, u32[]{:S(2)}) collective-permute-start(f32[32,256]{1,0:T(8,128)} %param.14), channel_id=1, source_target_pairs={{0,2},{1,3},{2,0},{3,1},{4,6},{5,7},{6,4},{7,5},{8,10},{9,11},{10,... | collective-permute-start | bytes 98312 | tf_op jit(solution)/shard_map/ppermute | solution.py:24
  6.0 12.5 %collective-permute-start.2 = (f32[32,256]{1,0:T(8,128)}, f32[32,256]{1,0:T(8,128)S(1)}, u32[]{:S(2)}, u32[]{:S(2)}) collective-permute-start(f32[32,256]{1,0:T(8,128)} %param.14), channel_id=1, source_target_pairs={{0,3},{1,2},{2,1},{3,0},{4,7},{5,6},{6,5},{7,4},{8,11},{9,10},{10,... | collective-permute-start | bytes 98312 | tf_op jit(solution)/shard_map/ppermute | solution.py:24
  8.6 13.5 %all-to-all-start = ((s32[8,2,128]{2,1,0:T(2,128)}), s32[8,2,128]{2,1,0:T(2,128)S(1)}, u32[]{:S(2)}, u32[]{:S(2)}) async-start(s32[8,2,128]{2,1,0:T(2,128)} %broadcast_in_dim.12), calls=%async_computation | async-start | bytes 16384 | tf_op jit(solution)/shard_map/all_to_all | solution.py:197
  19.1 18.5 %copy-start.12 = (f32[1,256,128]{2,1,0:T(8,128)S(1)}, f32[1,256,128]{2,1,0:T(8,128)}, u32[]{:S(2)}) copy-start(f32[1,256,128]{2,1,0:T(8,128)} %param.20) | copy-start | bytes 393220
  19.3 2.7 %collective-permute-start.6 = (f32[32,128]{1,0:T(8,128)S(1)}, f32[32,128]{1,0:T(8,128)S(1)}, u32[]{:S(2)}, u32[]{:S(2)}) collective-permute-start(f32[32,128]{1,0:T(8,128)S(1)} %fusion.24), channel_id=1, source_target_pairs={{0,1},{1,0},{2,3},{3,2},{4,5},{5,4},{6,7},{7,6},{8,9},{9,8},{10,11... | collective-permute-start | bytes 49160 | tf_op jit(solution)/shard_map/ppermute | solution.py:24
  19.9 3.9 %collective-permute-start.7 = (f32[32,128]{1,0:T(8,128)S(1)}, f32[32,128]{1,0:T(8,128)S(1)}, u32[]{:S(2)}, u32[]{:S(2)}) collective-permute-start(f32[32,128]{1,0:T(8,128)S(1)} %fusion.24), channel_id=1, source_target_pairs={{0,2},{1,3},{2,0},{3,1},{4,6},{5,7},{6,4},{7,5},{8,10},{9,11},{10,... | collective-permute-start | bytes 49160 | tf_op jit(solution)/shard_map/ppermute | solution.py:24
  20.4 3.3 %collective-permute-start.8 = (f32[32,128]{1,0:T(8,128)S(1)}, f32[32,128]{1,0:T(8,128)S(1)}, u32[]{:S(2)}, u32[]{:S(2)}) collective-permute-start(f32[32,128]{1,0:T(8,128)S(1)} %fusion.24), channel_id=1, source_target_pairs={{0,3},{1,2},{2,1},{3,0},{4,7},{5,6},{6,5},{7,4},{8,11},{9,10},{10,... | collective-permute-start | bytes 49160 | tf_op jit(solution)/shard_map/ppermute | solution.py:24
  21.3 4.9 %collective-permute-start.5 = (f32[800,128]{1,0:T(8,128)S(1)}, f32[800,128]{1,0:T(8,128)}, u32[]{:S(2)}, u32[]{:S(2)}) collective-permute-start(f32[800,128]{1,0:T(8,128)S(1)} %collective-permute-done.4.refs_4_), channel_id=1, source_target_pairs={{0,1},{1,0},{2,3},{3,2},{4,5},{5,4},{6,7},{7,6},{8,9},{9,8},{10,11... | collective-permute-start | bytes 1228808 | tf_op jit(solution)/shard_map/ppermute | solution.py:24
  23.8 20.1 %copy-start.3 = (f32[50,256]{1,0:T(8,128)S(1)}, f32[50,256]{1,0:T(8,128)}, u32[]{:S(2)}) copy-start(f32[50,256]{1,0:T(8,128)} %refs_3_.1) | copy-start | bytes 153604
  23.8 9.6 %collective-permute-start.9 = (f32[32,128]{1,0:T(8,128)S(1)}, f32[32,128]{1,0:T(8,128)S(1)}, u32[]{:S(2)}, u32[]{:S(2)}) collective-permute-start(f32[32,128]{1,0:T(8,128)S(1)} %add_add_fusion.1), channel_id=1, source_target_pairs={{0,4},{4,0},{8,12},{12,8},{16,20},{20,16},{24,28},{28,24},{1,5},{5... | collective-permute-start | bytes 49160 | tf_op jit(solution)/shard_map/ppermute | solution.py:24
  33.3 19.8 %copy-start.5 = (f32[50,128]{1,0:T(8,128)S(1)}, f32[50,128]{1,0:T(8,128)}, u32[]{:S(2)}) copy-start(f32[50,128]{1,0:T(8,128)} %refs_4_.1) | copy-start | bytes 76804
  34.6 4.7 %collective-permute-start.10 = (f32[32,128]{1,0:T(8,128)S(1)}, f32[32,128]{1,0:T(8,128)S(1)}, u32[]{:S(2)}, u32[]{:S(2)}) collective-permute-start(f32[32,128]{1,0:T(8,128)S(1)} %convolution_subtract_fusion.6), channel_id=1, source_target_pairs={{0,12},{4,8},{8,4},{12,0},{16,28},{20,24},{24,20},{28,16},{1,13},{... | collective-permute-start | bytes 49160 | tf_op jit(solution)/shard_map/ppermute | solution.py:24
  36.1 3.7 %collective-permute-start.11 = (f32[32,128]{1,0:T(8,128)S(1)}, f32[32,128]{1,0:T(8,128)S(1)}, u32[]{:S(2)}, u32[]{:S(2)}) collective-permute-start(f32[32,128]{1,0:T(8,128)S(1)} %convolution_subtract_fusion.6), channel_id=1, source_target_pairs={{0,4},{4,0},{8,12},{12,8},{16,20},{20,16},{24,28},{28,24},{1,5},{5... | collective-permute-start | bytes 49160 | tf_op jit(solution)/shard_map/ppermute | solution.py:24
  37.5 15.8 %collective-permute-start.21 = (f32[256,128]{1,0:T(8,128)S(1)}, f32[256,128]{1,0:T(8,128)S(1)}, u32[]{:S(2)}, u32[]{:S(2)}) collective-permute-start(f32[256,128]{1,0:T(8,128)S(1)} %bitcast.47), channel_id=1, source_target_pairs={{0,2},{1,3},{2,0},{3,1},{4,6},{5,7},{6,4},{7,5},{8,10},{9,11},{10,... | collective-permute-start | bytes 393224 | tf_op jit(solution)/shard_map/ppermute | solution.py:24
  38.9 20.1 %collective-permute-start.20 = (f32[256,128]{1,0:T(8,128)S(1)}, f32[256,128]{1,0:T(8,128)S(1)}, u32[]{:S(2)}, u32[]{:S(2)}) collective-permute-start(f32[256,128]{1,0:T(8,128)S(1)} %bitcast.48), channel_id=1, source_target_pairs={{0,1},{1,0},{2,3},{3,2},{4,5},{5,4},{6,7},{7,6},{8,9},{9,8},{10,11... | collective-permute-start | bytes 393224 | tf_op jit(solution)/shard_map/ppermute | solution.py:24
  40.9 5.6 %collective-permute-start.12 = (f32[32,128]{1,0:T(8,128)S(1)}, f32[32,128]{1,0:T(8,128)S(1)}, u32[]{:S(2)}, u32[]{:S(2)}) collective-permute-start(f32[32,128]{1,0:T(8,128)S(1)} %convolution_subtract_fusion.5), channel_id=1, source_target_pairs={{0,24},{4,28},{8,16},{12,20},{16,8},{20,12},{24,0},{28,4},{1,25},{... | collective-permute-start | bytes 49160 | tf_op jit(solution)/shard_map/ppermute | solution.py:24
  43.7 4.2 %collective-permute-start.13 = (f32[32,128]{1,0:T(8,128)S(1)}, f32[32,128]{1,0:T(8,128)S(1)}, u32[]{:S(2)}, u32[]{:S(2)}) collective-permute-start(f32[32,128]{1,0:T(8,128)S(1)} %convolution_subtract_fusion.5), channel_id=1, source_target_pairs={{0,8},{4,12},{8,0},{12,4},{16,24},{20,28},{24,16},{28,20},{1,9},{5... | collective-permute-start | bytes 49160 | tf_op jit(solution)/shard_map/ppermute | solution.py:24
  44.1 5.6 %collective-permute-start.14 = (f32[160,128]{1,0:T(8,128)}, f32[160,128]{1,0:T(8,128)S(1)}, u32[]{:S(2)}, u32[]{:S(2)}) collective-permute-start(f32[160,128]{1,0:T(8,128)} %get-tuple-element.19), channel_id=1, source_target_pairs={{0,16},{4,20},{8,24},{12,28},{16,0},{20,4},{24,8},{28,12},{1,17},{... | collective-permute-start | bytes 245768 | tf_op jit(solution)/shard_map/ppermute | solution.py:24
  50.1 3.8 %collective-permute-start.15 = (f32[32,128]{1,0:T(8,128)S(1)}, f32[32,128]{1,0:T(8,128)S(1)}, u32[]{:S(2)}, u32[]{:S(2)}) collective-permute-start(f32[32,128]{1,0:T(8,128)S(1)} %get-tuple-element.29), channel_id=1, source_target_pairs={{0,8},{4,12},{8,0},{12,4},{16,24},{20,28},{24,16},{28,20},{1,9},{5... | collective-permute-start | bytes 49160 | tf_op jit(solution)/shard_map/ppermute | solution.py:24
  52.0 5.5 %collective-permute-start.16 = (f32[32,128]{1,0:T(8,128)S(1)}, f32[32,128]{1,0:T(8,128)S(1)}, u32[]{:S(2)}, u32[]{:S(2)}) collective-permute-start(f32[32,128]{1,0:T(8,128)S(1)} %get-tuple-element.28), channel_id=1, source_target_pairs={{0,24},{4,28},{8,16},{12,20},{16,8},{20,12},{24,0},{28,4},{1,25},{... | collective-permute-start | bytes 49160 | tf_op jit(solution)/shard_map/ppermute | solution.py:24
  53.4 5.6 %collective-permute-start.22 = (f32[256,128]{1,0:T(8,128)S(1)}, f32[256,128]{1,0:T(8,128)S(1)}, u32[]{:S(2)}, u32[]{:S(2)}) collective-permute-start(f32[256,128]{1,0:T(8,128)S(1)} %collective-permute-done.21), channel_id=1, source_target_pairs={{0,1},{1,0},{2,3},{3,2},{4,5},{5,4},{6,7},{7,6},{8,9},{9,8},{10,11... | collective-permute-start | bytes 393224 | tf_op jit(solution)/shard_map/ppermute | solution.py:24
  57.7 4.4 %collective-permute-start.17 = (f32[32,128]{1,0:T(8,128)S(1)}, f32[32,128]{1,0:T(8,128)S(1)}, u32[]{:S(2)}, u32[]{:S(2)}) collective-permute-start(f32[32,128]{1,0:T(8,128)S(1)} %get-tuple-element.27), channel_id=1, source_target_pairs={{0,4},{4,0},{8,12},{12,8},{16,20},{20,16},{24,28},{28,24},{1,5},{5... | collective-permute-start | bytes 49160 | tf_op jit(solution)/shard_map/ppermute | solution.py:24
  58.9 4.6 %collective-permute-start.18 = (f32[32,128]{1,0:T(8,128)S(1)}, f32[32,128]{1,0:T(8,128)S(1)}, u32[]{:S(2)}, u32[]{:S(2)}) collective-permute-start(f32[32,128]{1,0:T(8,128)S(1)} %get-tuple-element.26), channel_id=1, source_target_pairs={{0,12},{4,8},{8,4},{12,0},{16,28},{20,24},{24,20},{28,16},{1,13},{... | collective-permute-start | bytes 49160 | tf_op jit(solution)/shard_map/ppermute | solution.py:24
  60.0 4.7 %collective-permute-start.23 = (f32[32,128]{1,0:T(8,128)S(1)}, f32[32,128]{1,0:T(8,128)S(1)}, u32[]{:S(2)}, u32[]{:S(2)}) collective-permute-start(f32[32,128]{1,0:T(8,128)S(1)} %convolution_subtract_fusion.4), channel_id=1, source_target_pairs={{0,16},{4,20},{8,24},{12,28},{16,0},{20,4},{24,8},{28,12},{1,17},{... | collective-permute-start | bytes 49160 | tf_op jit(solution)/shard_map/ppermute | solution.py:24
  63.8 3.8 %collective-permute-start.19 = (f32[32,128]{1,0:T(8,128)S(1)}, f32[32,128]{1,0:T(8,128)S(1)}, u32[]{:S(2)}, u32[]{:S(2)}) collective-permute-start(f32[32,128]{1,0:T(8,128)S(1)} %slice.47), channel_id=1, source_target_pairs={{0,4},{4,0},{8,12},{12,8},{16,20},{20,16},{24,28},{28,24},{1,5},{5... | collective-permute-start | bytes 49160 | tf_op jit(solution)/shard_map/ppermute | solution.py:24
  65.0 20.5 %copy-start.6 = (f32[32,128]{1,0:T(8,128)}, f32[32,128]{1,0:T(8,128)S(1)}, u32[]{:S(2)}) copy-start(f32[32,128]{1,0:T(8,128)S(1)} %slice_subtract_fusion.1.refs_2_) | copy-start | bytes 49156
  68.6 1.9 %collective-permute-start.24 = (f32[50,114]{1,0:T(8,128)S(1)}, f32[50,114]{1,0:T(8,128)S(1)}, u32[]{:S(2)}, u32[]{:S(2)}) collective-permute-start(f32[50,114]{1,0:T(8,128)S(1)} %select_maximum_fusion), channel_id=1, source_target_pairs={{0,1},{1,0},{2,3},{3,2},{4,5},{5,4},{6,7},{7,6},{8,9},{9,8},{10,11... | collective-permute-start | bytes 68408 | tf_op jit(solution)/shard_map/ppermute | solution.py:24
  68.7 3.9 %collective-permute-start.25 = (f32[50,114]{1,0:T(8,128)S(1)}, f32[50,114]{1,0:T(8,128)S(1)}, u32[]{:S(2)}, u32[]{:S(2)}) collective-permute-start(f32[50,114]{1,0:T(8,128)S(1)} %select_maximum_fusion), channel_id=1, source_target_pairs={{0,2},{1,3},{2,0},{3,1},{4,6},{5,7},{6,4},{7,5},{8,10},{9,11},{10,... | collective-permute-start | bytes 68408 | tf_op jit(solution)/shard_map/ppermute | solution.py:24
  70.1 3.3 %collective-permute-start.26 = (f32[50,114]{1,0:T(8,128)S(1)}, f32[50,114]{1,0:T(8,128)S(1)}, u32[]{:S(2)}, u32[]{:S(2)}) collective-permute-start(f32[50,114]{1,0:T(8,128)S(1)} %select_maximum_fusion), channel_id=1, source_target_pairs={{0,3},{1,2},{2,1},{3,0},{4,7},{5,6},{6,5},{7,4},{8,11},{9,10},{10,... | collective-permute-start | bytes 68408 | tf_op jit(solution)/shard_map/ppermute | solution.py:24
  (12 other events, 116.4 us)

commit v3 on v2

--- a/solution.py
+++ b/solution.py
@@ -49,11 +49,20 @@
 
 
 def local_place(index, width, own):
+    if width & (width - 1) == 0:
+        return jnp.bitwise_xor(index, own * width)
     return jnp.bitwise_xor(index // width, own) * width + index % width
 
 
-def one_hot(places, size):
-    return (places[:, None] == lax.broadcasted_iota(jnp.int32, (1, size), 1)).astype(jnp.float32)
+def level_of(group, top):
+    level = jnp.int32(top + 1)
+    for bit in range(top, 0, -1):
+        level = jnp.where(group % 2**bit != 0, jnp.int32(bit), level)
+    return level
+
+
+def held(arrays):
+    return [pltpu.with_memory_space_constraint(array, pltpu.VMEM) for array in arrays]
 
 
 def pack(inv_ref, push_ref, pull_ref, rhs_ref, out_ref):
@@ -80,15 +89,52 @@
     )
 
 
-def reduce_front(members, pivot_ref, rows_ref, *refs):
-    pieces = refs[:members]
-    moved_ref, up_ref, turn_ref, down_ref, push_base_ref, row_base_ref, root_ref = refs[members:]
+def permuting(pivot_ref, width):
+    rows = pivot_ref.shape[1]
+    places = local_place(pivot_ref[...], width, lax.axis_index("front"))
+    entry = lax.broadcasted_iota(jnp.int32, (rows, rows), 0)
+    return (entry == places).astype(jnp.float32).astype(jnp.bfloat16)
+
+
+def solve_leaf(pivot_ref, inv_ref, push_ref, *refs):
+    pieces, (state_ref, term_ref) = refs[:-2], refs[-2:]
+    hot = permuting(pivot_ref, pieces[0].shape[1])
+    rhs = jnp.concatenate([piece[...] for piece in pieces], 1)
+    block = rhs.shape[0]
+    turned = dot(jnp.concatenate(halves(rhs), 0), hot, 1, 0)
+    turned = turned[:block] + turned[block : 2 * block] + turned[2 * block :]
+    state = mm(turned, inv_ref[...], 1, 1)
+    state_ref[...] = state
+    term_ref[...] = mm(state, push_ref[...], 1, 1)
+
+
+def turn_pull(pivot_ref, *refs):
+    pieces, turned_ref = refs[:-1], refs[-1]
+    hot = permuting(pivot_ref, pieces[0].shape[0])
+    pull = jnp.concatenate([piece[...] for piece in pieces], 0).T
+    couple = pull.shape[0]
+    turned = dot(jnp.concatenate(halves(pull), 0), hot, 1, 0)
+    turned_ref[...] = turned[:couple] + turned[couple : 2 * couple] + turned[2 * couple :]
+
+
+def reduce_front(top, pivot_ref, lists_ref, *refs):
+    pieces = refs[:-8]
+    below_ref, rest_ref, up_ref, turn_ref, down_ref, push_base_ref, row_base_ref, root_ref = refs[-8:]
     rows = pivot_ref.shape[1]
     width = pieces[0].shape[1]
-    couple = rows_ref.shape[1] // 2
-    entry = lax.broadcasted_iota(jnp.int32, (rows, rows), 0)
-    hot = (entry == pivot_ref[...]).astype(jnp.float32).astype(jnp.bfloat16)
-    chosen = (entry[:, : 2 * couple] == rows_ref[...]).astype(jnp.float32).astype(jnp.bfloat16)
+    couple = lists_ref.shape[1]
+    hot = permuting(pivot_ref, width)
+    group = lax.axis_index("leaf")
+    level = level_of(group, top)
+    reach = jnp.where(level == 1, 0, jnp.left_shift(1, jnp.maximum(level - 2, 0)))
+    lower = jnp.where(level == 1, group - 1, jnp.where(level > top, reach, group - reach))
+    kind = jnp.where(level == 1, 0, 1)
+    children = jnp.concatenate(
+        [lists_ref[pl.ds(2 * child + kind, 1), :] for child in (lower, group + reach)], 1
+    )
+    children = local_place(children, width, lax.axis_index("front"))
+    entry = lax.broadcasted_iota(jnp.int32, (rows, 2 * couple), 0)
+    chosen = (entry == children).astype(jnp.float32).astype(jnp.bfloat16)
     mapped = []
     for piece in pieces:
         inverse = jnp.concatenate(
@@ -100,12 +146,11 @@
     pull = jnp.concatenate([piece[rows + couple : rows + couple + width, :] for piece in pieces], 0)
     rhs = jnp.concatenate([piece[rows + couple + width :, :] for piece in pieces], 1)
     below = sum(dot(chosen, part, 0, 0) for part in halves(mapped))
-    above = mm(pull, mapped, 0, 0)
-    base = mm(rhs, mapped, 1, 0)
-    moved = jnp.concatenate([below, above, base], 0)
+    moved = jnp.concatenate([below, mm(jnp.concatenate([pull.T, rhs], 0), mapped)], 0)
     push_part = mm(moved, push, 1, 1)
     rows_part = sum(dot(part, chosen, 1, 0) for part in halves(moved))
-    moved_ref[...] = moved[:, :width]
+    below_ref[...] = moved[: 2 * couple, :width]
+    rest_ref[...] = moved[2 * couple :, :width]
     up_ref[...] = push_part[: 2 * couple]
     turn_ref[...] = rows_part[: 2 * couple]
     down_ref[...] = rows_part[2 * couple : 3 * couple]
@@ -115,18 +160,69 @@
     root_ref[couple:, :] = rows_part[3 * couple :, :couple]
 
 
+def project(top, *refs):
+    state_ref, below_ref, moved_in_ref, lift_ref, pair_ref, above_ref, back_ref = refs[:7]
+    below_map_ref, rest_ref, metric_ref, basis_leaf_ref, basis_sep_ref = refs[7:12]
+    leaf_ref, sep_ref, inner_ref = refs[12:]
+    couple = moved_in_ref.shape[1]
+    block = state_ref.shape[0]
+    rank = basis_leaf_ref.shape[0]
+    level = level_of(lax.axis_index("leaf"), top)
+    above = jnp.where(level == 1, below_ref[:, couple:], moved_in_ref[...])
+    leaf = state_ref[...] - mm(above, lift_ref[...])
+    width = sep_ref.shape[1]
+    is_root = level > top
+    upper = jnp.where(is_root, back_ref[...], pair_ref[:, couple:])
+    around = jnp.concatenate([jnp.where(is_root, 0.0, pair_ref[:, :couple]), upper], 1)
+    sep = (
+        rest_ref[couple:, :width]
+        - mm(around, below_map_ref[...])
+        - mm(above_ref[...], rest_ref[:couple, :width])
+    )
+    leaf_ref[...] = leaf
+    sep_ref[...] = sep
+    row = lax.broadcasted_iota(jnp.int32, (block, block), 0)
+    lane = lax.broadcasted_iota(jnp.int32, (block, block), 1)
+    corner = metric_ref[:block, :block]
+    length = mm(leaf, leaf, 1, 1) + mm(sep, sep, 1, 1)
+    inner_ref[...] = jnp.zeros(inner_ref.shape, jnp.float32)
+    inner_ref[:, :rank] = mm(leaf, basis_leaf_ref[...], 1, 1) + mm(sep, basis_sep_ref[...], 1, 1)
+    inner_ref[:, rank : rank + block] = jnp.where(row <= lane, length, corner)
+    place = rank + block
+    inner_ref[:, place : place + 1] = jnp.sum(jnp.where(row == lane, corner, 0.0), 1, keepdims=True)
+    rest = rank - block
+    inner_ref[:, place + 1 : place + 1 + rest] = metric_ref[:block, block:]
+    inner_ref[:rest, place + 1 + rest : place + 1 + 2 * rest] = metric_ref[block:, block:]
+
+
 def finish(total_rows, inner_ref, leaf_ref, sep_ref, basis_leaf_ref, basis_sep_ref, *outs):
     q_leaf_ref, q_sep_ref, coeffs_ref, rfac_ref = outs
     block = leaf_ref.shape[0]
     rank = basis_leaf_ref.shape[0]
+    rest = rank - block
     inner = jnp.sum(inner_ref[...], 0) * (1.0 / total_rows)
-    metric = inner[:, :rank]
-    first = inner[:, rank : rank + block]
-    second = first - mm(metric, first)
-    third = second - mm(metric, second)
+    row = lax.broadcasted_iota(jnp.int32, (block, block), 0)
+    lane = lax.broadcasted_iota(jnp.int32, (block, block), 1)
+    first = inner[:, :rank]
+    both = inner[:, rank : rank + block]
+    place = rank + block
+    length = jnp.where(row <= lane, both, both.T)
+    corner = jnp.where(row > lane, both, both.T)
+    corner = jnp.where(row == lane, inner[:, place : place + 1], corner)
+    side = inner[:, place + 1 : place + 1 + rest]
+    last = inner[:rest, place + 1 + rest : place + 1 + 2 * rest]
+
+    def by_metric(value):
+        low, high = value[:, :block], value[:, block:]
+        return jnp.concatenate(
+            [mm(low, corner) + mm(high, side, 1, 1), mm(low, side) + mm(high, last)], 1
+        )
+
+    second = first - by_metric(first)
+    third = second - by_metric(second)
     coeffs = first + second
-    gram = inner[:block, rank + block :] - mm(first, coeffs, 0, 0) - mm(second, second + third, 0, 0)
-    coeffs_ref[...] = coeffs.T
+    gram = length - mm(first, coeffs, 1, 1) - mm(second, second + third, 1, 1)
+    coeffs_ref[...] = coeffs
     row = lax.broadcasted_iota(jnp.int32, (block, 2 * block), 0)
     lane = lax.broadcasted_iota(jnp.int32, (block, 2 * block), 1)
     table = jnp.concatenate([gram, (row == lane)[:, :block].astype(jnp.float32)], 1)
@@ -148,7 +244,7 @@
     table = table / jnp.sqrt(pivots)
     rfac_ref[...] = jnp.where(row <= lane, table, 0.0)[:, :block]
     back = table[:, block:]
-    spread = mm(back, coeffs, 1, 1)
+    spread = mm(back, coeffs)
     q_leaf_ref[...] = mm(back, leaf_ref[...]) - mm(spread, basis_leaf_ref[...])
     q_sep_ref[...] = mm(back, sep_ref[...]) - mm(spread, basis_sep_ref[...])
 
@@ -170,7 +266,6 @@
     basis_sep,
 ):
     group = lax.axis_index("leaf")
-    own = lax.axis_index("front")
     groups = lax.axis_size("leaf")
     top = groups.bit_length() - 1
     leaf_rows = pivot_leaf.shape[1]
@@ -179,16 +274,15 @@
     sep_width = rhs_sep.shape[1]
     couple = rows_leaf.shape[1]
     total_rows = groups * (leaf_rows + sep_rows)
-    level = jnp.full((), top + 1, jnp.int32)
-    for bit in range(top, 0, -1):
-        level = jnp.where(group % 2**bit != 0, jnp.int32(bit), level)
-
-    rhs_leaf_all = jnp.concatenate(gathered_pieces(rhs_leaf, "front"), 1)
+    level = level_of(group, top)
+
+    leaf_pieces = gathered_pieces(rhs_leaf, "front")
+
     bulk = pl.pallas_call(
         pack,
-        out_shape=jax.ShapeDtypeStruct(
-            (sep_rows + 2 * couple + rhs_sep.shape[0], sep_width), jnp.float32
-        ),
+        out_shape=pltpu.VMEM((sep_rows + 2 * couple + rhs_sep.shape[0], sep_width), jnp.float32),
+        in_specs=[pl.BlockSpec(memory_space=pltpu.VMEM)] * 4,
+        out_specs=pl.BlockSpec(memory_space=pltpu.VMEM),
         name="pack",
     )(inv_sep[0], push_sep[0], pull_sep[0], rhs_sep)
     bulk = doubled_pieces(bulk, "front")
@@ -197,29 +291,23 @@
     lists = lax.all_to_all(
         jnp.broadcast_to(lists[None], (groups,) + lists.shape), "leaf", 0, 0
     )
-    reach = jnp.where(level == 1, 0, jnp.left_shift(1, jnp.maximum(level - 2, 0)))
-    upper_child = group + reach
-    lower_child = jnp.where(level == 1, group - 1, jnp.where(level > top, reach, group - reach))
-    kind = jnp.where(level == 1, 0, 1)
-    rows = jnp.concatenate(
-        [
-            lax.dynamic_slice(lists, (child, kind, 0), (1, 1, couple))[0]
-            for child in (lower_child, upper_child)
-        ],
-        1,
-    )
-
-    leaf_hot = one_hot(local_place(pivot_leaf[0], leaf_width, own), leaf_rows)
-    leaf_map = mm(leaf_hot, inv_leaf[0], 0, 1)
-    leaf_state = mm(rhs_leaf_all, leaf_map)
-    leaf_push = summed_pairwise(
-        gathered_pieces(mm(leaf_state, push_leaf[0], 1, 1), "front")
-    )
-
     vmem = pl.BlockSpec(memory_space=pltpu.VMEM)
     block = rhs_sep.shape[0]
+    leaf_state, leaf_push = pl.pallas_call(
+        solve_leaf,
+        out_shape=(
+            pltpu.VMEM((block, leaf_width), jnp.float32),
+            pltpu.VMEM((block, couple), jnp.float32),
+        ),
+        in_specs=[vmem] * (3 + len(leaf_pieces)),
+        out_specs=(vmem,) * 2,
+        name="solve_leaf",
+    )(pivot_leaf, inv_leaf[0], push_leaf[0], leaf_pieces[0], *held(leaf_pieces[1:]))
+    leaf_push = summed_pairwise(gathered_pieces(leaf_push, "front"))
+
     shapes = (
-        (3 * couple + block, sep_width),
+        (2 * couple, sep_width),
+        (couple + block, sep_width),
         (2 * couple, couple),
         (2 * couple, 2 * couple),
         (couple, 2 * couple),
@@ -227,19 +315,32 @@
         (block, 2 * couple),
         (couple + block, couple),
     )
-    moved, up_weights, turn_weights, down_weights, push_base, row_base, root_op = pl.pallas_call(
-        lambda *refs: reduce_front(len(bulk), *refs),
-        out_shape=tuple(jax.ShapeDtypeStruct(shape, jnp.float32) for shape in shapes),
+    (
+        below_map,
+        rest,
+        up_weights,
+        turn_weights,
+        down_weights,
+        push_base,
+        row_base,
+        root_op,
+    ) = pl.pallas_call(
+        lambda *refs: reduce_front(top, *refs),
+        out_shape=tuple(pltpu.VMEM(shape, jnp.float32) for shape in shapes),
+        in_specs=[vmem] * (2 + len(bulk)),
         out_specs=(vmem,) * len(shapes),
         name="reduce_front",
-    )(
-        local_place(pivot_sep, sep_width, own),
-        local_place(rows, sep_width, own),
-        *bulk,
-    )
-
-    pull_leaf_all = jnp.concatenate(doubled_pieces(pull_leaf[0], "front"), 0)
-    leaf_lift = mm(pull_leaf_all, leaf_map, 0, 0)
+    )(pivot_sep, lists.reshape(2 * groups, couple), *bulk)
+
+    pull_pieces = doubled_pieces(pull_leaf[0], "front")
+    leaf_turned = pl.pallas_call(
+        turn_pull,
+        out_shape=pltpu.VMEM((couple, leaf_rows), jnp.float32),
+        in_specs=[vmem] * (1 + len(pull_pieces)),
+        out_specs=vmem,
+        name="turn_pull",
+    )(pivot_leaf, pull_pieces[0], *held(pull_pieces[1:]))
+    leaf_lift = mm(leaf_turned, inv_leaf[0], 1, 1)
 
     half = groups // 2
     root_op = swap(root_op, "leaf", half)
@@ -266,21 +367,25 @@
         is_upper = (group // (2 * step)) % 2 == 1
         above = jnp.where(level == height - 1, jnp.where(is_upper, upper, lower), above)
     below = row_base - mm(above, down_weights)
-    leaf_above = jnp.where(level == 1, below[:, couple:], swap(below[:, :couple], "leaf", 1))
-    around = jnp.concatenate([pair, above], 1)
-    root_around = jnp.pad(back, ((0, 0), (couple, couple)))
-    around = jnp.where(level > top, root_around, around)
-
-    leaf_solution = leaf_state - mm(leaf_above, leaf_lift)
-    sep_solution = moved[3 * couple :] - mm(
-        around, moved[: 3 * couple]
-    )
-
+    moved_in = swap(below[:, :couple], "leaf", 1)
     rank = basis_leaf.shape[0]
     metric = mm(basis_leaf, basis_leaf, 1, 1) + mm(basis_sep, basis_sep, 1, 1)
-    cross = mm(basis_leaf, leaf_solution, 1, 1) + mm(basis_sep, sep_solution, 1, 1)
-    length = mm(leaf_solution, leaf_solution, 1, 1) + mm(sep_solution, sep_solution, 1, 1)
-    inner = jnp.concatenate([metric, cross, jnp.pad(length, ((0, rank - block), (0, 0)))], 1)
+    lanes = -(-(3 * rank - block + 1) // 128) * 128
+    leaf_solution, sep_solution, inner = pl.pallas_call(
+        lambda *refs: project(top, *refs),
+        out_shape=(
+            pltpu.VMEM((block, leaf_width), jnp.float32),
+            pltpu.VMEM((block, sep_width), jnp.float32),
+            pltpu.VMEM((block, lanes), jnp.float32),
+        ),
+        in_specs=[vmem] * 12,
+        out_specs=(vmem,) * 3,
+        name="project",
+    )(
+        *held([leaf_state, below, moved_in, leaf_lift, pair, above, back, below_map, rest, metric]),
+        basis_leaf,
+        basis_sep,
+    )
     inner = summed_pairwise(gathered_pieces(inner, "front"))
     inner = lax.all_to_all(
         jnp.broadcast_to(inner[None], (groups,) + inner.shape), "leaf", 0, 0
@@ -293,8 +398,9 @@
             jax.ShapeDtypeStruct((block, rank), jnp.float32),
             jax.ShapeDtypeStruct((block, block), jnp.float32),
         ),
+        in_specs=[vmem] * 5,
         name="finish",
-    )(inner, leaf_solution, sep_solution, basis_leaf, basis_sep)
+    )(*held([inner, leaf_solution, sep_solution]), basis_leaf, basis_sep)
     return q_leaf, q_sep, coeffs.T, rfac
 
 

time: 90 us -> 101 us (1.12)
  waiting for transfers between devices: 16.2 us -> 34.9 us
  matrix products: 10.3 us -> 3.07 us
  Pallas kernels: 12.3 us -> 16.3 us
  other arithmetic: 2.68 us -> 0.05 us
  blocking collectives: 12.1 us -> 10.7 us
    ppermute x27, waiting for transfers between devices: 16.2 us -> 28.4 us  [swap(): lax.ppermute(value, axis, [(one, one ^ mask) for one in range(count)])]
    dot_general x20 -> x11, matrix products: 10.3 us -> 3.07 us  [mm(): lax.dot_general(former, latter, (((left,), (right,)), ((), ())), precisio...]
    all_to_all x1, waiting for transfers between devices: 0.01 us -> 6.52 us  [on_device(): lax.all_to_all(jnp.broadcast_to(lists[None], (groups,) + lists.shape), 'l...]
    pallas_call x2 -> x5, Pallas kernels: 8.19 us -> 12.7 us  [the longest x1 5.25 us: on_device(): pl.pallas_call(lambda *refs: reduce_front(top, *refs), out_shape=tuple((p...]
    add x3 -> x0, other arithmetic: 1.87 us -> none  [local_place(): return jnp.bitwise_xor(index // width, own) * width + index % width]
    all_to_all x1, blocking collectives: 12.1 us -> 10.7 us  [on_device(): lax.all_to_all(jnp.broadcast_to(inner[None], (groups,) + inner.shape), 'l...]
  transfers between devices with their start and end apart: 28 -> 28, of which waited for: 12 -> 13; matrix products, arithmetic and copies ran while one was open for 13% -> 3% of each run, Pallas kernels for 7% -> 10%
where the time goes in v3:
time: 101 us; the launch traced here: 100 us
  waiting for transfers between devices  34.9 us (35%)
  starting transfers between devices  32.6 us (32%)
  Pallas kernels  16.3 us (16%)
  blocking collectives  10.7 us (11%)
  matrix products  3.07 us (3%)
  local copies, waits for them, and re-layouts  1.6 us (2%)
  between operations  1.03 us (1%)
    ppermute x27, waiting for transfers between devices, swap(): lax.ppermute(value, axis, [(one, one ^ mask) for one in range(count)])  28.4 us
    ppermute x27, starting transfers between devices, swap(): lax.ppermute(value, axis, [(one, one ^ mask) for one in range(count)])  27.7 us
    all_to_all x1, blocking collectives, on_device(): lax.all_to_all(jnp.broadcast_to(inner[None], (groups,) + inner.shape), 'l...  10.7 us
    all_to_all x1, waiting for transfers between devices, on_device(): lax.all_to_all(jnp.broadcast_to(lists[None], (groups,) + lists.shape), 'l...  6.52 us
    pallas_call x1, Pallas kernels, on_device(): pl.pallas_call(lambda *refs: reduce_front(top, *refs), out_shape=tuple((p...  5.25 us
    all_to_all x1, starting transfers between devices, on_device(): lax.all_to_all(jnp.broadcast_to(lists[None], (groups,) + lists.shape), 'l...  4.87 us
    pallas_call x1, Pallas kernels, on_device(): pl.pallas_call(lambda *refs: finish(total_rows, *refs), out_shape=(jax.Sh...  3.6 us
    dot_general x11, matrix products, mm(): lax.dot_general(former, latter, (((left,), (right,)), ((), ())), precisio...  3.07 us
  transfers between devices with their start and end apart: 28, of which 13 were waited for; matrix products, arithmetic and copies ran while one was open for 3% of the time, Pallas kernels for 10%

profile of v3, /device:TPU:0, one launch (start us, length us, event | category | flops | bytes accessed | tf_op | source)
XLA Modules:
  0.0 100.2 jit_solution(17639552296296367783)
XLA Ops:
  1.7 3.0 %collective-permute-start.4 = (f32[800,128]{1,0:T(8,128)S(1)}, f32[800,128]{1,0:T(8,128)S(1)}, u32[]{:S(2)}, u32[]{:S(2)}) collective-permute-start(f32[800,128]{1,0:T(8,128)S(1)} %pack.1.refs_2_), channel_id=1, source_target_pairs={{0,2},{1,3},{2,0},{3,1},{4,6},{5,7},{6,4},{7,5},{8,10},{9,11},{10,... | collective-permute-start | bytes 1228808 | tf_op jit(solution)/shard_map/ppermute | solution.py:24
  4.7 9.5 %collective-permute-done.4.refs_4_ = f32[800,128]{1,0:T(8,128)S(1)} collective-permute-done((f32[800,128]{1,0:T(8,128)S(1)}, f32[800,128]{1,0:T(8,128)S(1)}, u32[]{:S(2)}, u32[]{:S(2)}) %collective-permute-start.4) | collective-permute-done | bytes 409632 | tf_op jit(solution)/shard_map/ppermute | solution.py:24
  14.7 1.7 %collective-permute-start.1 = (f32[32,256]{1,0:T(8,128)S(1)}, f32[32,256]{1,0:T(8,128)S(1)}, u32[]{:S(2)}, u32[]{:S(2)}) collective-permute-start(f32[32,256]{1,0:T(8,128)S(1)} %copy-done.9), channel_id=1, source_target_pairs={{0,2},{1,3},{2,0},{3,1},{4,6},{5,7},{6,4},{7,5},{8,10},{9,11},{10,... | collective-permute-start | bytes 98312 | tf_op jit(solution)/shard_map/ppermute | solution.py:24
  16.4 2.2 %collective-permute-done.1.refs_2_ = f32[32,256]{1,0:T(8,128)S(1)} collective-permute-done((f32[32,256]{1,0:T(8,128)S(1)}, f32[32,256]{1,0:T(8,128)S(1)}, u32[]{:S(2)}, u32[]{:S(2)}) %collective-permute-start.1) | collective-permute-done | bytes 32800 | tf_op jit(solution)/shard_map/ppermute | solution.py:24
  18.6 1.5 %collective-permute-done.2.refs_3_ = f32[32,256]{1,0:T(8,128)S(1)} collective-permute-done((f32[32,256]{1,0:T(8,128)S(1)}, f32[32,256]{1,0:T(8,128)S(1)}, u32[]{:S(2)}, u32[]{:S(2)}) %collective-permute-start.2) | collective-permute-done | bytes 32800 | tf_op jit(solution)/shard_map/ppermute | solution.py:24
  20.1 3.1 %solve_leaf.1 = (f32[32,256]{1,0:T(8,128)S(1)}, f32[32,128]{1,0:T(8,128)S(1)}) custom-call(s32[1,1024]{1,0:T(1,128)} %pivot_ref.3, f32[256,1024]{1,0:T(8,128)} %bitcast.27, f32[128,256]{1,0:T(8,128)} %bitcast.29, f32[32,256]{1,0:T(8,128)} %refs_0_.2, f32[32,256]{1,0:T(8,128)S(1)} %collective-permute-done.refs_1_, ...), custom_call_target="tpu_custom_call" | custom-call | tf_op jit(solution)/shard_map/solve_leaf/pallas_call | solution.py:296
  23.6 1.1 %collective-permute-start.8 = (f32[32,128]{1,0:T(8,128)S(1)}, f32[32,128]{1,0:T(8,128)S(1)}, u32[]{:S(2)}, u32[]{:S(2)}) collective-permute-start(f32[32,128]{1,0:T(8,128)S(1)} %get-tuple-element.24), channel_id=1, source_target_pairs={{0,3},{1,2},{2,1},{3,0},{4,7},{5,6},{6,5},{7,4},{8,11},{9,10},{10,... | collective-permute-start | bytes 49160 | tf_op jit(solution)/shard_map/ppermute | solution.py:24
  25.4 1.6 %collective-permute-done.7 = f32[32,128]{1,0:T(8,128)S(1)} collective-permute-done((f32[32,128]{1,0:T(8,128)S(1)}, f32[32,128]{1,0:T(8,128)S(1)}, u32[]{:S(2)}, u32[]{:S(2)}) %collective-permute-start.7) | collective-permute-done | bytes 16416 | tf_op jit(solution)/shard_map/ppermute | solution.py:24
  27.0 1.8 %collective-permute-start.9 = (f32[32,128]{1,0:T(8,128)S(1)}, f32[32,128]{1,0:T(8,128)S(1)}, u32[]{:S(2)}, u32[]{:S(2)}) collective-permute-start(f32[32,128]{1,0:T(8,128)S(1)} %add_add_fusion.1), channel_id=1, source_target_pairs={{0,4},{4,0},{8,12},{12,8},{16,20},{20,16},{24,28},{28,24},{1,5},{5... | collective-permute-start | bytes 49160 | tf_op jit(solution)/shard_map/ppermute | solution.py:24
  29.4 4.9 %all-to-all-start = ((s32[8,2,128]{2,1,0:T(2,128)}), s32[8,2,128]{2,1,0:T(2,128)S(1)}, u32[]{:S(2)}, u32[]{:S(2)}) async-start(s32[8,2,128]{2,1,0:T(2,128)} %broadcast_in_dim.20), calls=%async_computation | async-start | bytes 16384 | tf_op jit(solution)/shard_map/all_to_all | solution.py:291
  34.3 6.5 %all-to-all-done = s32[8,2,128]{2,1,0:T(2,128)S(1)} async-done(((s32[8,2,128]{2,1,0:T(2,128)}), s32[8,2,128]{2,1,0:T(2,128)S(1)}, u32[]{:S(2)}, u32[]{:S(2)}) %all-to-all-start) | async-done | bytes 8224 | tf_op jit(solution)/shard_map/all_to_all | solution.py:291
  41.7 5.2 %reduce_front.1 = (f32[256,128]{1,0:T(8,128)S(1)}, f32[160,128]{1,0:T(8,128)S(1)}, f32[256,128]{1,0:T(8,128)S(1)}, f32[256,256]{1,0:T(8,128)S(1)}, f32[128,256]{...) custom-call(s32[1,512]{1,0:T(1,128)} %refs_0_.3, s32[16,128]{1,0:T(8,128)} %bitcast.35, ...), custom_call_target="tpu_custom_call" | custom-call | tf_op jit(solution)/shard_map/reduce_front/pallas_call | solution.py:327
  47.8 1.4 %collective-permute-start.10 = (f32[32,128]{1,0:T(8,128)S(1)}, f32[32,128]{1,0:T(8,128)S(1)}, u32[]{:S(2)}, u32[]{:S(2)}) collective-permute-start(f32[32,128]{1,0:T(8,128)S(1)} %convolution_subtract_fusion.5), channel_id=1, source_target_pairs={{0,12},{4,8},{8,4},{12,0},{16,28},{20,24},{24,20},{28,16},{1,13},{... | collective-permute-start | bytes 49160 | tf_op jit(solution)/shard_map/ppermute | solution.py:24
  49.3 1.8 %collective-permute-done.11 = f32[32,128]{1,0:T(8,128)S(1)} collective-permute-done((f32[32,128]{1,0:T(8,128)S(1)}, f32[32,128]{1,0:T(8,128)S(1)}, u32[]{:S(2)}, u32[]{:S(2)}) %collective-permute-start.11) | collective-permute-done | bytes 16416 | tf_op jit(solution)/shard_map/ppermute | solution.py:24
  51.0 1.4 %collective-permute-done.10 = f32[32,128]{1,0:T(8,128)S(1)} collective-permute-done((f32[32,128]{1,0:T(8,128)S(1)}, f32[32,128]{1,0:T(8,128)S(1)}, u32[]{:S(2)}, u32[]{:S(2)}) %collective-permute-start.10) | collective-permute-done | bytes 16416 | tf_op jit(solution)/shard_map/ppermute | solution.py:24
  53.3 1.4 %collective-permute-start.12 = (f32[32,128]{1,0:T(8,128)S(1)}, f32[32,128]{1,0:T(8,128)S(1)}, u32[]{:S(2)}, u32[]{:S(2)}) collective-permute-start(f32[32,128]{1,0:T(8,128)S(1)} %convolution_subtract_fusion.4), channel_id=1, source_target_pairs={{0,24},{4,28},{8,16},{12,20},{16,8},{20,12},{24,0},{28,4},{1,25},{... | collective-permute-start | bytes 49160 | tf_op jit(solution)/shard_map/ppermute | solution.py:24
  54.7 1.4 %collective-permute-start.21 = (f32[256,128]{1,0:T(8,128)S(1)}, f32[256,128]{1,0:T(8,128)S(1)}, u32[]{:S(2)}, u32[]{:S(2)}) collective-permute-start(f32[256,128]{1,0:T(8,128)S(1)} %bitcast.32), channel_id=1, source_target_pairs={{0,2},{1,3},{2,0},{3,1},{4,6},{5,7},{6,4},{7,5},{8,10},{9,11},{10,... | collective-permute-start | bytes 393224 | tf_op jit(solution)/shard_map/ppermute | solution.py:24
  56.2 1.5 %collective-permute-start.14 = (f32[160,128]{1,0:T(8,128)S(1)}, f32[160,128]{1,0:T(8,128)S(1)}, u32[]{:S(2)}, u32[]{:S(2)}) collective-permute-start(f32[160,128]{1,0:T(8,128)S(1)} %get-tuple-element.27), channel_id=1, source_target_pairs={{0,16},{4,20},{8,24},{12,28},{16,0},{20,4},{24,8},{28,12},{1,17},{... | collective-permute-start | bytes 245768 | tf_op jit(solution)/shard_map/ppermute | solution.py:24
  57.7 1.2 %collective-permute-done.12 = f32[32,128]{1,0:T(8,128)S(1)} collective-permute-done((f32[32,128]{1,0:T(8,128)S(1)}, f32[32,128]{1,0:T(8,128)S(1)}, u32[]{:S(2)}, u32[]{:S(2)}) %collective-permute-start.12) | collective-permute-done | bytes 16416 | tf_op jit(solution)/shard_map/ppermute | solution.py:24
  59.3 3.9 %collective-permute-done.14 = f32[160,128]{1,0:T(8,128)S(1)} collective-permute-done((f32[160,128]{1,0:T(8,128)S(1)}, f32[160,128]{1,0:T(8,128)S(1)}, u32[]{:S(2)}, u32[]{:S(2)}) %collective-permute-start.14) | collective-permute-done | bytes 81952 | tf_op jit(solution)/shard_map/ppermute | solution.py:24
  63.7 2.7 %collective-permute-start.16 = (f32[32,128]{1,0:T(8,128)S(1)}, f32[32,128]{1,0:T(8,128)S(1)}, u32[]{:S(2)}, u32[]{:S(2)}) collective-permute-start(f32[32,128]{1,0:T(8,128)S(1)} %get-tuple-element.40), channel_id=1, source_target_pairs={{0,24},{4,28},{8,16},{12,20},{16,8},{20,12},{24,0},{28,4},{1,25},{... | collective-permute-start | bytes 49160 | tf_op jit(solution)/shard_map/ppermute | solution.py:24
  67.4 1.9 %collective-permute-done.16 = f32[32,128]{1,0:T(8,128)S(1)} collective-permute-done((f32[32,128]{1,0:T(8,128)S(1)}, f32[32,128]{1,0:T(8,128)S(1)}, u32[]{:S(2)}, u32[]{:S(2)}) %collective-permute-start.16) | collective-permute-done | bytes 16416 | tf_op jit(solution)/shard_map/ppermute | solution.py:24
  69.5 1.6 %collective-permute-start.17 = (f32[32,128]{1,0:T(8,128)S(1)}, f32[32,128]{1,0:T(8,128)S(1)}, u32[]{:S(2)}, u32[]{:S(2)}) collective-permute-start(f32[32,128]{1,0:T(8,128)S(1)} %get-tuple-element.39), channel_id=1, source_target_pairs={{0,4},{4,0},{8,12},{12,8},{16,20},{20,16},{24,28},{28,24},{1,5},{5... | collective-permute-start | bytes 49160 | tf_op jit(solution)/shard_map/ppermute | solution.py:24
  71.4 1.9 %turn_pull.1 = f32[128,1024]{1,0:T(8,128)S(1)} custom-call(s32[1,1024]{1,0:T(1,128)} %pivot_ref.3, f32[256,128]{1,0:T(8,128)} %bitcast.30, f32[256,128]{1,0:T(8,128)S(1)} %collective-permute-done.20.refs_1_, f32[256,128]{1,0:T(8,128)S(1)} %collective-permute-done.21.refs_2_, f32[256,128]{1,0:T(8,128)S(1)} %collective-permute-done.22.refs_3_), custom_call_target="tpu_custom_call" | custom-call | tf_op jit(solution)/shard_map/turn_pull/pallas_call | solution.py:336
  73.4 3.1 %collective-permute-start.23 = (f32[32,128]{1,0:T(8,128)S(1)}, f32[32,128]{1,0:T(8,128)S(1)}, u32[]{:S(2)}, u32[]{:S(2)}) collective-permute-start(f32[32,128]{1,0:T(8,128)S(1)} %convolution_subtract_fusion.3), channel_id=1, source_target_pairs={{0,16},{4,20},{8,24},{12,28},{16,0},{20,4},{24,8},{28,12},{1,17},{... | collective-permute-start | bytes 49160 | tf_op jit(solution)/shard_map/ppermute | solution.py:24
  76.7 1.6 %collective-permute-start.19 = (f32[32,128]{1,0:T(8,128)S(1)}, f32[32,128]{1,0:T(8,128)S(1)}, u32[]{:S(2)}, u32[]{:S(2)}) collective-permute-start(f32[32,128]{1,0:T(8,128)S(1)} %slice.34), channel_id=1, source_target_pairs={{0,4},{4,0},{8,12},{12,8},{16,20},{20,16},{24,28},{28,24},{1,5},{5... | collective-permute-start | bytes 49160 | tf_op jit(solution)/shard_map/ppermute | solution.py:24
  78.3 1.2 %fusion.8.refs_3_ = f32[128,256]{1,0:T(8,128)S(1)} fusion(f32[128,1024]{1,0:T(8,128)S(1)} %turn_pull.1, f32[1,256,1024]{2,1,0:T(8,128)S(1)} %copy-done.1), kind=kOutput, calls=%fused_computation.23 | convolution fusion | flops 402653184 | bytes 1703936 | tf_op jit(solution)/shard_map/dot_general | solution.py:13
  80.5 1.5 %project.1 = (f32[32,256]{1,0:T(8,128)S(1)}, f32[32,128]{1,0:T(8,128)S(1)}, f32[32,128]{1,0:T(8,128)S(1)}) custom-call(f32[32,256]{1,0:T(8,128)S(1)} %get-tuple-element.21.refs_0_, f32[32,256]{1,0:T(8,128)S(1)} %convolution_subtract_fusion.refs_1_, f32[32,128]{1,0:T(8,128)S(1)} %collective-permute-done.19.refs_2_, f32[128,256]{1,0:T(8,128)S(1)} %fusion.8.refs_3_, ...), custom_call_target="tpu_custom_call" | custom-call | tf_op jit(solution)/shard_map/project/pallas_call | solution.py:374
  82.6 1.5 %collective-permute-start.24 = (f32[32,128]{1,0:T(8,128)S(1)}, f32[32,128]{1,0:T(8,128)S(1)}, u32[]{:S(2)}, u32[]{:S(2)}) collective-permute-start(f32[32,128]{1,0:T(8,128)S(1)} %get-tuple-element.31), channel_id=1, source_target_pairs={{0,1},{1,0},{2,3},{3,2},{4,5},{5,4},{6,7},{7,6},{8,9},{9,8},{10,11... | collective-permute-start | bytes 49160 | tf_op jit(solution)/shard_map/ppermute | solution.py:24
  84.2 1.8 %collective-permute-done.25 = f32[32,128]{1,0:T(8,128)S(1)} collective-permute-done((f32[32,128]{1,0:T(8,128)S(1)}, f32[32,128]{1,0:T(8,128)S(1)}, u32[]{:S(2)}, u32[]{:S(2)}) %collective-permute-start.25) | collective-permute-done | bytes 16416 | tf_op jit(solution)/shard_map/ppermute | solution.py:24
  86.0 10.7 %all_to_all.10.refs_0_ = f32[8,32,128]{2,1,0:T(8,128)S(1)} all-to-all(f32[8,32,128]{2,1,0:T(8,128)S(1)} %broadcast_in_dim.23), channel_id=1, replica_groups=mesh['leaf'=8,'front'=4] {'leaf'}, dimensions={0} | all-to-all | bytes 262144 | tf_op jit(solution)/shard_map/all_to_all | solution.py:390
  96.6 3.6 %finish.1 = (f32[32,256]{1,0:T(8,128)}, f32[32,128]{1,0:T(8,128)}, f32[32,50]{1,0:T(8,128)}, f32[32,32]{1,0:T(8,128)}) custom-call(f32[8,32,128]{2,1,0:T(8,128)S(1)} %all_to_all.10.refs_0_, f32[32,256]{1,0:T(8,128)S(1)} %get-tuple-element.32.refs_1_, f32[32,128]{1,0:T(8,128)S(1)} %get-tuple-element.33.refs_2_, f32[50,256]{1,0:T(8,128)} %refs_3_.1, ...), custom_call_target="tpu_custom_call" | custom-call | tf_op jit(solution)/shard_map/finish/pallas_call | solution.py:393
  (78 shorter events, 10.1 us)
Async XLA Ops:
  0.6 13.6 %copy-start.9 = (f32[32,256]{1,0:T(8,128)S(1)}, f32[32,256]{1,0:T(8,128)}, u32[]{:S(2)}) copy-start(f32[32,256]{1,0:T(8,128)} %refs_0_.2) | copy-start | bytes 98308
  1.7 21.5 %copy-start = (f32[800,128]{1,0:T(8,128)}, f32[800,128]{1,0:T(8,128)S(1)}, u32[]{:S(2)}) copy-start(f32[800,128]{1,0:T(8,128)S(1)} %pack.1.refs_2_) | copy-start | bytes 1228804
  1.7 12.5 %collective-permute-start.4 = (f32[800,128]{1,0:T(8,128)S(1)}, f32[800,128]{1,0:T(8,128)S(1)}, u32[]{:S(2)}, u32[]{:S(2)}) collective-permute-start(f32[800,128]{1,0:T(8,128)S(1)} %pack.1.refs_2_), channel_id=1, source_target_pairs={{0,2},{1,3},{2,0},{3,1},{4,6},{5,7},{6,4},{7,5},{8,10},{9,11},{10,... | collective-permute-start | bytes 1228808 | tf_op jit(solution)/shard_map/ppermute | solution.py:24
  4.7 36.1 %collective-permute-start.3 = (f32[800,128]{1,0:T(8,128)S(1)}, f32[800,128]{1,0:T(8,128)S(1)}, u32[]{:S(2)}, u32[]{:S(2)}) collective-permute-start(f32[800,128]{1,0:T(8,128)S(1)} %pack.1.refs_2_), channel_id=1, source_target_pairs={{0,1},{1,0},{2,3},{3,2},{4,5},{5,4},{6,7},{7,6},{8,9},{9,8},{10,11... | collective-permute-start | bytes 1228808 | tf_op jit(solution)/shard_map/ppermute | solution.py:24
  14.2 9.0 %copy-start.4 = (f32[800,128]{1,0:T(8,128)}, f32[800,128]{1,0:T(8,128)S(1)}, u32[]{:S(2)}) copy-start(f32[800,128]{1,0:T(8,128)S(1)} %collective-permute-done.4.refs_4_) | copy-start | bytes 1228804
  14.2 26.6 %collective-permute-start.5 = (f32[800,128]{1,0:T(8,128)S(1)}, f32[800,128]{1,0:T(8,128)S(1)}, u32[]{:S(2)}, u32[]{:S(2)}) collective-permute-start(f32[800,128]{1,0:T(8,128)S(1)} %collective-permute-done.4.refs_4_), channel_id=1, source_target_pairs={{0,1},{1,0},{2,3},{3,2},{4,5},{5,4},{6,7},{7,6},{8,9},{9,8},{10,11... | collective-permute-start | bytes 1228808 | tf_op jit(solution)/shard_map/ppermute | solution.py:24
  14.2 2.3 %collective-permute-start = (f32[32,256]{1,0:T(8,128)S(1)}, f32[32,256]{1,0:T(8,128)S(1)}, u32[]{:S(2)}, u32[]{:S(2)}) collective-permute-start(f32[32,256]{1,0:T(8,128)S(1)} %copy-done.9), channel_id=1, source_target_pairs={{0,1},{1,0},{2,3},{3,2},{4,5},{5,4},{6,7},{7,6},{8,9},{9,8},{10,11... | collective-permute-start | bytes 98312 | tf_op jit(solution)/shard_map/ppermute | solution.py:24
  14.7 3.9 %collective-permute-start.1 = (f32[32,256]{1,0:T(8,128)S(1)}, f32[32,256]{1,0:T(8,128)S(1)}, u32[]{:S(2)}, u32[]{:S(2)}) collective-permute-start(f32[32,256]{1,0:T(8,128)S(1)} %copy-done.9), channel_id=1, source_target_pairs={{0,2},{1,3},{2,0},{3,1},{4,6},{5,7},{6,4},{7,5},{8,10},{9,11},{10,... | collective-permute-start | bytes 98312 | tf_op jit(solution)/shard_map/ppermute | solution.py:24
  16.4 3.7 %collective-permute-start.2 = (f32[32,256]{1,0:T(8,128)S(1)}, f32[32,256]{1,0:T(8,128)S(1)}, u32[]{:S(2)}, u32[]{:S(2)}) collective-permute-start(f32[32,256]{1,0:T(8,128)S(1)} %copy-done.9), channel_id=1, source_target_pairs={{0,3},{1,2},{2,1},{3,0},{4,7},{5,6},{6,5},{7,4},{8,11},{9,10},{10,... | collective-permute-start | bytes 98312 | tf_op jit(solution)/shard_map/ppermute | solution.py:24
  23.2 3.8 %collective-permute-start.7 = (f32[32,128]{1,0:T(8,128)S(1)}, f32[32,128]{1,0:T(8,128)S(1)}, u32[]{:S(2)}, u32[]{:S(2)}) collective-permute-start(f32[32,128]{1,0:T(8,128)S(1)} %get-tuple-element.24), channel_id=1, source_target_pairs={{0,2},{1,3},{2,0},{3,1},{4,6},{5,7},{6,4},{7,5},{8,10},{9,11},{10,... | collective-permute-start | bytes 49160 | tf_op jit(solution)/shard_map/ppermute | solution.py:24
  23.6 3.4 %collective-permute-start.8 = (f32[32,128]{1,0:T(8,128)S(1)}, f32[32,128]{1,0:T(8,128)S(1)}, u32[]{:S(2)}, u32[]{:S(2)}) collective-permute-start(f32[32,128]{1,0:T(8,128)S(1)} %get-tuple-element.24), channel_id=1, source_target_pairs={{0,3},{1,2},{2,1},{3,0},{4,7},{5,6},{6,5},{7,4},{8,11},{9,10},{10,... | collective-permute-start | bytes 49160 | tf_op jit(solution)/shard_map/ppermute | solution.py:24
  24.7 2.3 %collective-permute-start.6 = (f32[32,128]{1,0:T(8,128)S(1)}, f32[32,128]{1,0:T(8,128)S(1)}, u32[]{:S(2)}, u32[]{:S(2)}) collective-permute-start(f32[32,128]{1,0:T(8,128)S(1)} %get-tuple-element.24), channel_id=1, source_target_pairs={{0,1},{1,0},{2,3},{3,2},{4,5},{5,4},{6,7},{7,6},{8,9},{9,8},{10,11... | collective-permute-start | bytes 49160 | tf_op jit(solution)/shard_map/ppermute | solution.py:24
  27.0 20.0 %collective-permute-start.9 = (f32[32,128]{1,0:T(8,128)S(1)}, f32[32,128]{1,0:T(8,128)S(1)}, u32[]{:S(2)}, u32[]{:S(2)}) collective-permute-start(f32[32,128]{1,0:T(8,128)S(1)} %add_add_fusion.1), channel_id=1, source_target_pairs={{0,4},{4,0},{8,12},{12,8},{16,20},{20,16},{24,28},{28,24},{1,5},{5... | collective-permute-start | bytes 49160 | tf_op jit(solution)/shard_map/ppermute | solution.py:24
  29.4 11.4 %all-to-all-start = ((s32[8,2,128]{2,1,0:T(2,128)}), s32[8,2,128]{2,1,0:T(2,128)S(1)}, u32[]{:S(2)}, u32[]{:S(2)}) async-start(s32[8,2,128]{2,1,0:T(2,128)} %broadcast_in_dim.20), calls=%async_computation | async-start | bytes 16384 | tf_op jit(solution)/shard_map/all_to_all | solution.py:291
  47.2 3.8 %collective-permute-start.11 = (f32[32,128]{1,0:T(8,128)S(1)}, f32[32,128]{1,0:T(8,128)S(1)}, u32[]{:S(2)}, u32[]{:S(2)}) collective-permute-start(f32[32,128]{1,0:T(8,128)S(1)} %convolution_subtract_fusion.5), channel_id=1, source_target_pairs={{0,4},{4,0},{8,12},{12,8},{16,20},{20,16},{24,28},{28,24},{1,5},{5... | collective-permute-start | bytes 49160 | tf_op jit(solution)/shard_map/ppermute | solution.py:24
  47.8 4.6 %collective-permute-start.10 = (f32[32,128]{1,0:T(8,128)S(1)}, f32[32,128]{1,0:T(8,128)S(1)}, u32[]{:S(2)}, u32[]{:S(2)}) collective-permute-start(f32[32,128]{1,0:T(8,128)S(1)} %convolution_subtract_fusion.5), channel_id=1, source_target_pairs={{0,12},{4,8},{8,4},{12,0},{16,28},{20,24},{24,20},{28,16},{1,13},{... | collective-permute-start | bytes 49160 | tf_op jit(solution)/shard_map/ppermute | solution.py:24
  52.7 5.0 %collective-permute-start.13 = (f32[32,128]{1,0:T(8,128)S(1)}, f32[32,128]{1,0:T(8,128)S(1)}, u32[]{:S(2)}, u32[]{:S(2)}) collective-permute-start(f32[32,128]{1,0:T(8,128)S(1)} %convolution_subtract_fusion.4), channel_id=1, source_target_pairs={{0,8},{4,12},{8,0},{12,4},{16,24},{20,28},{24,16},{28,20},{1,9},{5... | collective-permute-start | bytes 49160 | tf_op jit(solution)/shard_map/ppermute | solution.py:24
  53.3 5.5 %collective-permute-start.12 = (f32[32,128]{1,0:T(8,128)S(1)}, f32[32,128]{1,0:T(8,128)S(1)}, u32[]{:S(2)}, u32[]{:S(2)}) collective-permute-start(f32[32,128]{1,0:T(8,128)S(1)} %convolution_subtract_fusion.4), channel_id=1, source_target_pairs={{0,24},{4,28},{8,16},{12,20},{16,8},{20,12},{24,0},{28,4},{1,25},{... | collective-permute-start | bytes 49160 | tf_op jit(solution)/shard_map/ppermute | solution.py:24
  54.7 16.7 %collective-permute-start.20 = (f32[256,128]{1,0:T(8,128)S(1)}, f32[256,128]{1,0:T(8,128)S(1)}, u32[]{:S(2)}, u32[]{:S(2)}) collective-permute-start(f32[256,128]{1,0:T(8,128)S(1)} %bitcast.31), channel_id=1, source_target_pairs={{0,1},{1,0},{2,3},{3,2},{4,5},{5,4},{6,7},{7,6},{8,9},{9,8},{10,11... | collective-permute-start | bytes 393224 | tf_op jit(solution)/shard_map/ppermute | solution.py:24
  54.7 11.8 %collective-permute-start.21 = (f32[256,128]{1,0:T(8,128)S(1)}, f32[256,128]{1,0:T(8,128)S(1)}, u32[]{:S(2)}, u32[]{:S(2)}) collective-permute-start(f32[256,128]{1,0:T(8,128)S(1)} %bitcast.32), channel_id=1, source_target_pairs={{0,2},{1,3},{2,0},{3,1},{4,6},{5,7},{6,4},{7,5},{8,10},{9,11},{10,... | collective-permute-start | bytes 393224 | tf_op jit(solution)/shard_map/ppermute | solution.py:24
  56.2 7.0 %collective-permute-start.14 = (f32[160,128]{1,0:T(8,128)S(1)}, f32[160,128]{1,0:T(8,128)S(1)}, u32[]{:S(2)}, u32[]{:S(2)}) collective-permute-start(f32[160,128]{1,0:T(8,128)S(1)} %get-tuple-element.27), channel_id=1, source_target_pairs={{0,16},{4,20},{8,24},{12,28},{16,0},{20,4},{24,8},{28,12},{1,17},{... | collective-permute-start | bytes 245768 | tf_op jit(solution)/shard_map/ppermute | solution.py:24
  63.6 14.7 %copy-start.1 = (f32[1,256,1024]{2,1,0:T(8,128)S(1)}, f32[1,256,1024]{2,1,0:T(8,128)}, u32[]{:S(2)}) copy-start(f32[1,256,1024]{2,1,0:T(8,128)} %param.16) | copy-start | bytes 3145732
  63.6 3.8 %collective-permute-start.15 = (f32[32,128]{1,0:T(8,128)S(1)}, f32[32,128]{1,0:T(8,128)S(1)}, u32[]{:S(2)}, u32[]{:S(2)}) collective-permute-start(f32[32,128]{1,0:T(8,128)S(1)} %get-tuple-element.41), channel_id=1, source_target_pairs={{0,8},{4,12},{8,0},{12,4},{16,24},{20,28},{24,16},{28,20},{1,9},{5... | collective-permute-start | bytes 49160 | tf_op jit(solution)/shard_map/ppermute | solution.py:24
  63.7 5.6 %collective-permute-start.16 = (f32[32,128]{1,0:T(8,128)S(1)}, f32[32,128]{1,0:T(8,128)S(1)}, u32[]{:S(2)}, u32[]{:S(2)}) collective-permute-start(f32[32,128]{1,0:T(8,128)S(1)} %get-tuple-element.40), channel_id=1, source_target_pairs={{0,24},{4,28},{8,16},{12,20},{16,8},{20,12},{24,0},{28,4},{1,25},{... | collective-permute-start | bytes 49160 | tf_op jit(solution)/shard_map/ppermute | solution.py:24
  66.6 4.8 %collective-permute-start.22 = (f32[256,128]{1,0:T(8,128)S(1)}, f32[256,128]{1,0:T(8,128)S(1)}, u32[]{:S(2)}, u32[]{:S(2)}) collective-permute-start(f32[256,128]{1,0:T(8,128)S(1)} %collective-permute-done.21.refs_2_), channel_id=1, source_target_pairs={{0,1},{1,0},{2,3},{3,2},{4,5},{5,4},{6,7},{7,6},{8,9},{9,8},{10,11... | collective-permute-start | bytes 393224 | tf_op jit(solution)/shard_map/ppermute | solution.py:24
  69.5 7.0 %collective-permute-start.17 = (f32[32,128]{1,0:T(8,128)S(1)}, f32[32,128]{1,0:T(8,128)S(1)}, u32[]{:S(2)}, u32[]{:S(2)}) collective-permute-start(f32[32,128]{1,0:T(8,128)S(1)} %get-tuple-element.39), channel_id=1, source_target_pairs={{0,4},{4,0},{8,12},{12,8},{16,20},{20,16},{24,28},{28,24},{1,5},{5... | collective-permute-start | bytes 49160 | tf_op jit(solution)/shard_map/ppermute | solution.py:24
  71.1 5.4 %collective-permute-start.18 = (f32[32,128]{1,0:T(8,128)S(1)}, f32[32,128]{1,0:T(8,128)S(1)}, u32[]{:S(2)}, u32[]{:S(2)}) collective-permute-start(f32[32,128]{1,0:T(8,128)S(1)} %get-tuple-element.38), channel_id=1, source_target_pairs={{0,12},{4,8},{8,4},{12,0},{16,28},{20,24},{24,20},{28,16},{1,13},{... | collective-permute-start | bytes 49160 | tf_op jit(solution)/shard_map/ppermute | solution.py:24
  73.4 6.1 %collective-permute-start.23 = (f32[32,128]{1,0:T(8,128)S(1)}, f32[32,128]{1,0:T(8,128)S(1)}, u32[]{:S(2)}, u32[]{:S(2)}) collective-permute-start(f32[32,128]{1,0:T(8,128)S(1)} %convolution_subtract_fusion.3), channel_id=1, source_target_pairs={{0,16},{4,20},{8,24},{12,28},{16,0},{20,4},{24,8},{28,12},{1,17},{... | collective-permute-start | bytes 49160 | tf_op jit(solution)/shard_map/ppermute | solution.py:24
  76.7 3.8 %collective-permute-start.19 = (f32[32,128]{1,0:T(8,128)S(1)}, f32[32,128]{1,0:T(8,128)S(1)}, u32[]{:S(2)}, u32[]{:S(2)}) collective-permute-start(f32[32,128]{1,0:T(8,128)S(1)} %slice.34), channel_id=1, source_target_pairs={{0,4},{4,0},{8,12},{12,8},{16,20},{20,16},{24,28},{28,24},{1,5},{5... | collective-permute-start | bytes 49160 | tf_op jit(solution)/shard_map/ppermute | solution.py:24
  81.9 4.0 %collective-permute-start.25 = (f32[32,128]{1,0:T(8,128)S(1)}, f32[32,128]{1,0:T(8,128)S(1)}, u32[]{:S(2)}, u32[]{:S(2)}) collective-permute-start(f32[32,128]{1,0:T(8,128)S(1)} %get-tuple-element.31), channel_id=1, source_target_pairs={{0,2},{1,3},{2,0},{3,1},{4,6},{5,7},{6,4},{7,5},{8,10},{9,11},{10,... | collective-permute-start | bytes 49160 | tf_op jit(solution)/shard_map/ppermute | solution.py:24
  82.6 3.3 %collective-permute-start.26 = (f32[32,128]{1,0:T(8,128)S(1)}, f32[32,128]{1,0:T(8,128)S(1)}, u32[]{:S(2)}, u32[]{:S(2)}) collective-permute-start(f32[32,128]{1,0:T(8,128)S(1)} %get-tuple-element.31), channel_id=1, source_target_pairs={{0,3},{1,2},{2,1},{3,0},{4,7},{5,6},{6,5},{7,4},{8,11},{9,10},{10,... | collective-permute-start | bytes 49160 | tf_op jit(solution)/shard_map/ppermute | solution.py:24
  82.6 3.3 %collective-permute-start.24 = (f32[32,128]{1,0:T(8,128)S(1)}, f32[32,128]{1,0:T(8,128)S(1)}, u32[]{:S(2)}, u32[]{:S(2)}) collective-permute-start(f32[32,128]{1,0:T(8,128)S(1)} %get-tuple-element.31), channel_id=1, source_target_pairs={{0,1},{1,0},{2,3},{3,2},{4,5},{5,4},{6,7},{7,6},{8,9},{9,8},{10,11... | collective-permute-start | bytes 49160 | tf_op jit(solution)/shard_map/ppermute | solution.py:24
  (8 other events, 31.4 us)

commit v4 on v3

--- a/solution.py
+++ b/solution.py
@@ -227,7 +227,7 @@
     lane = lax.broadcasted_iota(jnp.int32, (block, 2 * block), 1)
     table = jnp.concatenate([gram, (row == lane)[:, :block].astype(jnp.float32)], 1)
     pivots = jnp.ones((block, 2 * block), jnp.float32)
-    width = 8
+    width = 16
     for start in range(0, block, width):
         columns = [
             jnp.broadcast_to(table[:, k : k + 1], table.shape)
@@ -276,8 +276,6 @@
     total_rows = groups * (leaf_rows + sep_rows)
     level = level_of(group, top)
 
-    leaf_pieces = gathered_pieces(rhs_leaf, "front")
-
     bulk = pl.pallas_call(
         pack,
         out_shape=pltpu.VMEM((sep_rows + 2 * couple + rhs_sep.shape[0], sep_width), jnp.float32),
@@ -285,6 +283,8 @@
         out_specs=pl.BlockSpec(memory_space=pltpu.VMEM),
         name="pack",
     )(inv_sep[0], push_sep[0], pull_sep[0], rhs_sep)
+    first_rhs, bulk = lax.optimization_barrier((rhs_leaf, bulk))
+    leaf_pieces = gathered_pieces(first_rhs, "front")
     bulk = doubled_pieces(bulk, "front")
 
     lists = jnp.concatenate([rows_leaf, rows_sep], 0)
@@ -330,7 +330,11 @@
         in_specs=[vmem] * (2 + len(bulk)),
         out_specs=(vmem,) * len(shapes),
         name="reduce_front",
-    )(pivot_sep, lists.reshape(2 * groups, couple), *bulk)
+    )(
+        pivot_sep,
+        *held([lists.reshape(2 * groups, couple)]),
+        *[piece if k % 2 == 0 else held([piece])[0] for k, piece in enumerate(bulk)],
+    )
 
     pull_pieces = doubled_pieces(pull_leaf[0], "front")
     leaf_turned = pl.pallas_call(

time: 101 us -> 99.3 us (0.983)
  no operation moved by 1% of the time
where the time goes in v4:
time: 99.3 us; the launch traced here: 98.9 us
  waiting for transfers between devices  34.9 us (35%)
  starting transfers between devices  32.6 us (33%)
  Pallas kernels  15.9 us (16%)
  blocking collectives  10.6 us (11%)
  matrix products  3.08 us (3%)
  between operations  1.02 us (1%)
    ppermute x27, waiting for transfers between devices, swap(): lax.ppermute(value, axis, [(one, one ^ mask) for one in range(count)])  28.3 us
    ppermute x27, starting transfers between devices, swap(): lax.ppermute(value, axis, [(one, one ^ mask) for one in range(count)])  27.7 us
    all_to_all x1, blocking collectives, on_device(): lax.all_to_all(jnp.broadcast_to(inner[None], (groups,) + inner.shape), 'l...  10.6 us
    all_to_all x1, waiting for transfers between devices, on_device(): lax.all_to_all(jnp.broadcast_to(lists[None], (groups,) + lists.shape), 'l...  6.52 us
    pallas_call x1, Pallas kernels, on_device(): pl.pallas_call(lambda *refs: reduce_front(top, *refs), out_shape=tuple((p...  5.03 us
    all_to_all x1, starting transfers between devices, on_device(): lax.all_to_all(jnp.broadcast_to(lists[None], (groups,) + lists.shape), 'l...  4.88 us
    pallas_call x1, Pallas kernels, on_device(): pl.pallas_call(lambda *refs: finish(total_rows, *refs), out_shape=(jax.Sh...  3.43 us
    dot_general x11, matrix products, mm(): lax.dot_general(former, latter, (((left,), (right,)), ((), ())), precisio...  3.08 us
  transfers between devices with their start and end apart: 28, of which 13 were waited for; matrix products, arithmetic and copies ran while one was open for 3% of the time, Pallas kernels for 10%

profile of v4, /device:TPU:0, one launch (start us, length us, event | category | flops | bytes accessed | tf_op | source)
XLA Modules:
  0.0 98.9 jit_solution(686861020703538724)
XLA Ops:
  1.7 3.0 %collective-permute-start.4 = (f32[800,128]{1,0:T(8,128)S(1)}, f32[800,128]{1,0:T(8,128)S(1)}, u32[]{:S(2)}, u32[]{:S(2)}) collective-permute-start(f32[800,128]{1,0:T(8,128)S(1)} %pack.1.refs_2_), channel_id=1, source_target_pairs={{0,2},{1,3},{2,0},{3,1},{4,6},{5,7},{6,4},{7,5},{8,10},{9,11},{10,... | collective-permute-start | bytes 1228808 | tf_op jit(solution)/shard_map/ppermute | solution.py:24
  4.7 9.5 %collective-permute-done.4.refs_4_ = f32[800,128]{1,0:T(8,128)S(1)} collective-permute-done((f32[800,128]{1,0:T(8,128)S(1)}, f32[800,128]{1,0:T(8,128)S(1)}, u32[]{:S(2)}, u32[]{:S(2)}) %collective-permute-start.4) | collective-permute-done | bytes 409632 | tf_op jit(solution)/shard_map/ppermute | solution.py:24
  14.7 1.7 %collective-permute-start.1 = (f32[32,256]{1,0:T(8,128)S(1)}, f32[32,256]{1,0:T(8,128)S(1)}, u32[]{:S(2)}, u32[]{:S(2)}) collective-permute-start(f32[32,256]{1,0:T(8,128)S(1)} %copy-done.6), channel_id=1, source_target_pairs={{0,2},{1,3},{2,0},{3,1},{4,6},{5,7},{6,4},{7,5},{8,10},{9,11},{10,... | collective-permute-start | bytes 98312 | tf_op jit(solution)/shard_map/ppermute | solution.py:24
  16.4 2.2 %collective-permute-done.1.refs_2_ = f32[32,256]{1,0:T(8,128)S(1)} collective-permute-done((f32[32,256]{1,0:T(8,128)S(1)}, f32[32,256]{1,0:T(8,128)S(1)}, u32[]{:S(2)}, u32[]{:S(2)}) %collective-permute-start.1) | collective-permute-done | bytes 32800 | tf_op jit(solution)/shard_map/ppermute | solution.py:24
  18.6 1.5 %collective-permute-done.2.refs_3_ = f32[32,256]{1,0:T(8,128)S(1)} collective-permute-done((f32[32,256]{1,0:T(8,128)S(1)}, f32[32,256]{1,0:T(8,128)S(1)}, u32[]{:S(2)}, u32[]{:S(2)}) %collective-permute-start.2) | collective-permute-done | bytes 32800 | tf_op jit(solution)/shard_map/ppermute | solution.py:24
  20.1 3.0 %solve_leaf.1 = (f32[32,256]{1,0:T(8,128)S(1)}, f32[32,128]{1,0:T(8,128)S(1)}) custom-call(s32[1,1024]{1,0:T(1,128)} %pivot_ref.3, f32[256,1024]{1,0:T(8,128)} %bitcast.28, f32[128,256]{1,0:T(8,128)} %bitcast.30, f32[32,256]{1,0:T(8,128)} %refs_0_.1, f32[32,256]{1,0:T(8,128)S(1)} %collective-permute-done.refs_1_, ...), custom_call_target="tpu_custom_call" | custom-call | tf_op jit(solution)/shard_map/solve_leaf/pallas_call | solution.py:296
  23.5 1.1 %collective-permute-start.8 = (f32[32,128]{1,0:T(8,128)S(1)}, f32[32,128]{1,0:T(8,128)S(1)}, u32[]{:S(2)}, u32[]{:S(2)}) collective-permute-start(f32[32,128]{1,0:T(8,128)S(1)} %get-tuple-element.28), channel_id=1, source_target_pairs={{0,3},{1,2},{2,1},{3,0},{4,7},{5,6},{6,5},{7,4},{8,11},{9,10},{10,... | collective-permute-start | bytes 49160 | tf_op jit(solution)/shard_map/ppermute | solution.py:24
  25.4 1.6 %collective-permute-done.7 = f32[32,128]{1,0:T(8,128)S(1)} collective-permute-done((f32[32,128]{1,0:T(8,128)S(1)}, f32[32,128]{1,0:T(8,128)S(1)}, u32[]{:S(2)}, u32[]{:S(2)}) %collective-permute-start.7) | collective-permute-done | bytes 16416 | tf_op jit(solution)/shard_map/ppermute | solution.py:24
  27.0 1.8 %collective-permute-start.9 = (f32[32,128]{1,0:T(8,128)S(1)}, f32[32,128]{1,0:T(8,128)S(1)}, u32[]{:S(2)}, u32[]{:S(2)}) collective-permute-start(f32[32,128]{1,0:T(8,128)S(1)} %add_add_fusion.1), channel_id=1, source_target_pairs={{0,4},{4,0},{8,12},{12,8},{16,20},{20,16},{24,28},{28,24},{1,5},{5... | collective-permute-start | bytes 49160 | tf_op jit(solution)/shard_map/ppermute | solution.py:24
  29.4 4.9 %all-to-all-start = ((s32[8,2,128]{2,1,0:T(2,128)}), s32[8,2,128]{2,1,0:T(2,128)S(1)}, u32[]{:S(2)}, u32[]{:S(2)}) async-start(s32[8,2,128]{2,1,0:T(2,128)} %broadcast_in_dim.20), calls=%async_computation | async-start | bytes 16384 | tf_op jit(solution)/shard_map/all_to_all | solution.py:291
  34.2 6.5 %all-to-all-done = s32[8,2,128]{2,1,0:T(2,128)S(1)} async-done(((s32[8,2,128]{2,1,0:T(2,128)}), s32[8,2,128]{2,1,0:T(2,128)S(1)}, u32[]{:S(2)}, u32[]{:S(2)}) %all-to-all-start) | async-done | bytes 8224 | tf_op jit(solution)/shard_map/all_to_all | solution.py:291
  40.8 5.0 %reduce_front.1 = (f32[256,128]{1,0:T(8,128)S(1)}, f32[160,128]{1,0:T(8,128)S(1)}, f32[256,128]{1,0:T(8,128)S(1)}, f32[256,256]{1,0:T(8,128)S(1)}, f32[128,256]{...) custom-call(s32[1,512]{1,0:T(1,128)} %refs_0_.2, s32[16,128]{1,0:T(8,128)S(1)} %bitcast.27, ...), custom_call_target="tpu_custom_call" | custom-call | tf_op jit(solution)/shard_map/reduce_front/pallas_call | solution.py:327
  46.6 1.4 %collective-permute-start.10 = (f32[32,128]{1,0:T(8,128)S(1)}, f32[32,128]{1,0:T(8,128)S(1)}, u32[]{:S(2)}, u32[]{:S(2)}) collective-permute-start(f32[32,128]{1,0:T(8,128)S(1)} %convolution_subtract_fusion.5), channel_id=1, source_target_pairs={{0,12},{4,8},{8,4},{12,0},{16,28},{20,24},{24,20},{28,16},{1,13},{... | collective-permute-start | bytes 49160 | tf_op jit(solution)/shard_map/ppermute | solution.py:24
  48.1 1.8 %collective-permute-done.11 = f32[32,128]{1,0:T(8,128)S(1)} collective-permute-done((f32[32,128]{1,0:T(8,128)S(1)}, f32[32,128]{1,0:T(8,128)S(1)}, u32[]{:S(2)}, u32[]{:S(2)}) %collective-permute-start.11) | collective-permute-done | bytes 16416 | tf_op jit(solution)/shard_map/ppermute | solution.py:24
  49.8 1.4 %collective-permute-done.10 = f32[32,128]{1,0:T(8,128)S(1)} collective-permute-done((f32[32,128]{1,0:T(8,128)S(1)}, f32[32,128]{1,0:T(8,128)S(1)}, u32[]{:S(2)}, u32[]{:S(2)}) %collective-permute-start.10) | collective-permute-done | bytes 16416 | tf_op jit(solution)/shard_map/ppermute | solution.py:24
  52.1 1.4 %collective-permute-start.12 = (f32[32,128]{1,0:T(8,128)S(1)}, f32[32,128]{1,0:T(8,128)S(1)}, u32[]{:S(2)}, u32[]{:S(2)}) collective-permute-start(f32[32,128]{1,0:T(8,128)S(1)} %convolution_subtract_fusion.4), channel_id=1, source_target_pairs={{0,24},{4,28},{8,16},{12,20},{16,8},{20,12},{24,0},{28,4},{1,25},{... | collective-permute-start | bytes 49160 | tf_op jit(solution)/shard_map/ppermute | solution.py:24
  53.6 1.4 %collective-permute-start.21 = (f32[256,128]{1,0:T(8,128)S(1)}, f32[256,128]{1,0:T(8,128)S(1)}, u32[]{:S(2)}, u32[]{:S(2)}) collective-permute-start(f32[256,128]{1,0:T(8,128)S(1)} %bitcast.33), channel_id=1, source_target_pairs={{0,2},{1,3},{2,0},{3,1},{4,6},{5,7},{6,4},{7,5},{8,10},{9,11},{10,... | collective-permute-start | bytes 393224 | tf_op jit(solution)/shard_map/ppermute | solution.py:24
  55.0 1.5 %collective-permute-start.14 = (f32[160,128]{1,0:T(8,128)S(1)}, f32[160,128]{1,0:T(8,128)S(1)}, u32[]{:S(2)}, u32[]{:S(2)}) collective-permute-start(f32[160,128]{1,0:T(8,128)S(1)} %get-tuple-element.31), channel_id=1, source_target_pairs={{0,16},{4,20},{8,24},{12,28},{16,0},{20,4},{24,8},{28,12},{1,17},{... | collective-permute-start | bytes 245768 | tf_op jit(solution)/shard_map/ppermute | solution.py:24
  56.5 1.2 %collective-permute-done.12 = f32[32,128]{1,0:T(8,128)S(1)} collective-permute-done((f32[32,128]{1,0:T(8,128)S(1)}, f32[32,128]{1,0:T(8,128)S(1)}, u32[]{:S(2)}, u32[]{:S(2)}) %collective-permute-start.12) | collective-permute-done | bytes 16416 | tf_op jit(solution)/shard_map/ppermute | solution.py:24
  58.1 3.8 %collective-permute-done.14 = f32[160,128]{1,0:T(8,128)S(1)} collective-permute-done((f32[160,128]{1,0:T(8,128)S(1)}, f32[160,128]{1,0:T(8,128)S(1)}, u32[]{:S(2)}, u32[]{:S(2)}) %collective-permute-start.14) | collective-permute-done | bytes 81952 | tf_op jit(solution)/shard_map/ppermute | solution.py:24
  62.5 2.7 %collective-permute-start.16 = (f32[32,128]{1,0:T(8,128)S(1)}, f32[32,128]{1,0:T(8,128)S(1)}, u32[]{:S(2)}, u32[]{:S(2)}) collective-permute-start(f32[32,128]{1,0:T(8,128)S(1)} %get-tuple-element.44), channel_id=1, source_target_pairs={{0,24},{4,28},{8,16},{12,20},{16,8},{20,12},{24,0},{28,4},{1,25},{... | collective-permute-start | bytes 49160 | tf_op jit(solution)/shard_map/ppermute | solution.py:24
  66.2 1.9 %collective-permute-done.16 = f32[32,128]{1,0:T(8,128)S(1)} collective-permute-done((f32[32,128]{1,0:T(8,128)S(1)}, f32[32,128]{1,0:T(8,128)S(1)}, u32[]{:S(2)}, u32[]{:S(2)}) %collective-permute-start.16) | collective-permute-done | bytes 16416 | tf_op jit(solution)/shard_map/ppermute | solution.py:24
  68.3 1.6 %collective-permute-start.17 = (f32[32,128]{1,0:T(8,128)S(1)}, f32[32,128]{1,0:T(8,128)S(1)}, u32[]{:S(2)}, u32[]{:S(2)}) collective-permute-start(f32[32,128]{1,0:T(8,128)S(1)} %get-tuple-element.43), channel_id=1, source_target_pairs={{0,4},{4,0},{8,12},{12,8},{16,20},{20,16},{24,28},{28,24},{1,5},{5... | collective-permute-start | bytes 49160 | tf_op jit(solution)/shard_map/ppermute | solution.py:24
  70.2 1.9 %turn_pull.1 = f32[128,1024]{1,0:T(8,128)S(1)} custom-call(s32[1,1024]{1,0:T(1,128)} %pivot_ref.3, f32[256,128]{1,0:T(8,128)} %bitcast.31, f32[256,128]{1,0:T(8,128)S(1)} %collective-permute-done.20.refs_1_, f32[256,128]{1,0:T(8,128)S(1)} %collective-permute-done.21.refs_2_, f32[256,128]{1,0:T(8,128)S(1)} %collective-permute-done.22.refs_3_), custom_call_target="tpu_custom_call" | custom-call | tf_op jit(solution)/shard_map/turn_pull/pallas_call | solution.py:340
  72.2 3.1 %collective-permute-start.23 = (f32[32,128]{1,0:T(8,128)S(1)}, f32[32,128]{1,0:T(8,128)S(1)}, u32[]{:S(2)}, u32[]{:S(2)}) collective-permute-start(f32[32,128]{1,0:T(8,128)S(1)} %convolution_subtract_fusion.3), channel_id=1, source_target_pairs={{0,16},{4,20},{8,24},{12,28},{16,0},{20,4},{24,8},{28,12},{1,17},{... | collective-permute-start | bytes 49160 | tf_op jit(solution)/shard_map/ppermute | solution.py:24
  75.5 1.6 %collective-permute-start.19 = (f32[32,128]{1,0:T(8,128)S(1)}, f32[32,128]{1,0:T(8,128)S(1)}, u32[]{:S(2)}, u32[]{:S(2)}) collective-permute-start(f32[32,128]{1,0:T(8,128)S(1)} %slice.34), channel_id=1, source_target_pairs={{0,4},{4,0},{8,12},{12,8},{16,20},{20,16},{24,28},{28,24},{1,5},{5... | collective-permute-start | bytes 49160 | tf_op jit(solution)/shard_map/ppermute | solution.py:24
  77.1 1.2 %fusion.8.refs_3_ = f32[128,256]{1,0:T(8,128)S(1)} fusion(f32[128,1024]{1,0:T(8,128)S(1)} %turn_pull.1, f32[1,256,1024]{2,1,0:T(8,128)S(1)} %copy-done.1), kind=kOutput, calls=%fused_computation.23 | convolution fusion | flops 402653184 | bytes 1703936 | tf_op jit(solution)/shard_map/dot_general | solution.py:13
  79.3 1.5 %project.1 = (f32[32,256]{1,0:T(8,128)S(1)}, f32[32,128]{1,0:T(8,128)S(1)}, f32[32,128]{1,0:T(8,128)S(1)}) custom-call(f32[32,256]{1,0:T(8,128)S(1)} %get-tuple-element.24.refs_0_, f32[32,256]{1,0:T(8,128)S(1)} %convolution_subtract_fusion.refs_1_, f32[32,128]{1,0:T(8,128)S(1)} %collective-permute-done.19.refs_2_, f32[128,256]{1,0:T(8,128)S(1)} %fusion.8.refs_3_, ...), custom_call_target="tpu_custom_call" | custom-call | tf_op jit(solution)/shard_map/project/pallas_call | solution.py:378
  81.4 1.5 %collective-permute-start.24 = (f32[32,128]{1,0:T(8,128)S(1)}, f32[32,128]{1,0:T(8,128)S(1)}, u32[]{:S(2)}, u32[]{:S(2)}) collective-permute-start(f32[32,128]{1,0:T(8,128)S(1)} %get-tuple-element.35), channel_id=1, source_target_pairs={{0,1},{1,0},{2,3},{3,2},{4,5},{5,4},{6,7},{7,6},{8,9},{9,8},{10,11... | collective-permute-start | bytes 49160 | tf_op jit(solution)/shard_map/ppermute | solution.py:24
  83.0 1.8 %collective-permute-done.25 = f32[32,128]{1,0:T(8,128)S(1)} collective-permute-done((f32[32,128]{1,0:T(8,128)S(1)}, f32[32,128]{1,0:T(8,128)S(1)}, u32[]{:S(2)}, u32[]{:S(2)}) %collective-permute-start.25) | collective-permute-done | bytes 16416 | tf_op jit(solution)/shard_map/ppermute | solution.py:24
  84.8 10.6 %all_to_all.10.refs_0_ = f32[8,32,128]{2,1,0:T(8,128)S(1)} all-to-all(f32[8,32,128]{2,1,0:T(8,128)S(1)} %broadcast_in_dim.23), channel_id=1, replica_groups=mesh['leaf'=8,'front'=4] {'leaf'}, dimensions={0} | all-to-all | bytes 262144 | tf_op jit(solution)/shard_map/all_to_all | solution.py:394
  95.4 3.4 %finish.1 = (f32[32,256]{1,0:T(8,128)}, f32[32,128]{1,0:T(8,128)}, f32[32,50]{1,0:T(8,128)}, f32[32,32]{1,0:T(8,128)}) custom-call(f32[8,32,128]{2,1,0:T(8,128)S(1)} %all_to_all.10.refs_0_, f32[32,256]{1,0:T(8,128)S(1)} %get-tuple-element.36.refs_1_, f32[32,128]{1,0:T(8,128)S(1)} %get-tuple-element.37.refs_2_, f32[50,256]{1,0:T(8,128)} %refs_3_.1, ...), custom_call_target="tpu_custom_call" | custom-call | tf_op jit(solution)/shard_map/finish/pallas_call | solution.py:397
  (72 shorter events, 9.2 us)
Async XLA Ops:
  0.6 13.6 %copy-start.6 = (f32[32,256]{1,0:T(8,128)S(1)}, f32[32,256]{1,0:T(8,128)}, u32[]{:S(2)}) copy-start(f32[32,256]{1,0:T(8,128)} %refs_0_.1) | copy-start | bytes 98308
  1.7 21.4 %copy-start = (f32[800,128]{1,0:T(8,128)}, f32[800,128]{1,0:T(8,128)S(1)}, u32[]{:S(2)}) copy-start(f32[800,128]{1,0:T(8,128)S(1)} %pack.1.refs_2_) | copy-start | bytes 1228804
  1.7 12.5 %collective-permute-start.4 = (f32[800,128]{1,0:T(8,128)S(1)}, f32[800,128]{1,0:T(8,128)S(1)}, u32[]{:S(2)}, u32[]{:S(2)}) collective-permute-start(f32[800,128]{1,0:T(8,128)S(1)} %pack.1.refs_2_), channel_id=1, source_target_pairs={{0,2},{1,3},{2,0},{3,1},{4,6},{5,7},{6,4},{7,5},{8,10},{9,11},{10,... | collective-permute-start | bytes 1228808 | tf_op jit(solution)/shard_map/ppermute | solution.py:24
  4.7 36.0 %collective-permute-start.3 = (f32[800,128]{1,0:T(8,128)S(1)}, f32[800,128]{1,0:T(8,128)S(1)}, u32[]{:S(2)}, u32[]{:S(2)}) collective-permute-start(f32[800,128]{1,0:T(8,128)S(1)} %pack.1.refs_2_), channel_id=1, source_target_pairs={{0,1},{1,0},{2,3},{3,2},{4,5},{5,4},{6,7},{7,6},{8,9},{9,8},{10,11... | collective-permute-start | bytes 1228808 | tf_op jit(solution)/shard_map/ppermute | solution.py:24
  14.2 8.9 %copy-start.4 = (f32[800,128]{1,0:T(8,128)}, f32[800,128]{1,0:T(8,128)S(1)}, u32[]{:S(2)}) copy-start(f32[800,128]{1,0:T(8,128)S(1)} %collective-permute-done.4.refs_4_) | copy-start | bytes 1228804
  14.2 26.6 %collective-permute-start.5 = (f32[800,128]{1,0:T(8,128)S(1)}, f32[800,128]{1,0:T(8,128)S(1)}, u32[]{:S(2)}, u32[]{:S(2)}) collective-permute-start(f32[800,128]{1,0:T(8,128)S(1)} %collective-permute-done.4.refs_4_), channel_id=1, source_target_pairs={{0,1},{1,0},{2,3},{3,2},{4,5},{5,4},{6,7},{7,6},{8,9},{9,8},{10,11... | collective-permute-start | bytes 1228808 | tf_op jit(solution)/shard_map/ppermute | solution.py:24
  14.2 2.3 %collective-permute-start = (f32[32,256]{1,0:T(8,128)S(1)}, f32[32,256]{1,0:T(8,128)S(1)}, u32[]{:S(2)}, u32[]{:S(2)}) collective-permute-start(f32[32,256]{1,0:T(8,128)S(1)} %copy-done.6), channel_id=1, source_target_pairs={{0,1},{1,0},{2,3},{3,2},{4,5},{5,4},{6,7},{7,6},{8,9},{9,8},{10,11... | collective-permute-start | bytes 98312 | tf_op jit(solution)/shard_map/ppermute | solution.py:24
  14.7 3.9 %collective-permute-start.1 = (f32[32,256]{1,0:T(8,128)S(1)}, f32[32,256]{1,0:T(8,128)S(1)}, u32[]{:S(2)}, u32[]{:S(2)}) collective-permute-start(f32[32,256]{1,0:T(8,128)S(1)} %copy-done.6), channel_id=1, source_target_pairs={{0,2},{1,3},{2,0},{3,1},{4,6},{5,7},{6,4},{7,5},{8,10},{9,11},{10,... | collective-permute-start | bytes 98312 | tf_op jit(solution)/shard_map/ppermute | solution.py:24
  16.4 3.7 %collective-permute-start.2 = (f32[32,256]{1,0:T(8,128)S(1)}, f32[32,256]{1,0:T(8,128)S(1)}, u32[]{:S(2)}, u32[]{:S(2)}) collective-permute-start(f32[32,256]{1,0:T(8,128)S(1)} %copy-done.6), channel_id=1, source_target_pairs={{0,3},{1,2},{2,1},{3,0},{4,7},{5,6},{6,5},{7,4},{8,11},{9,10},{10,... | collective-permute-start | bytes 98312 | tf_op jit(solution)/shard_map/ppermute | solution.py:24
  23.2 3.8 %collective-permute-start.7 = (f32[32,128]{1,0:T(8,128)S(1)}, f32[32,128]{1,0:T(8,128)S(1)}, u32[]{:S(2)}, u32[]{:S(2)}) collective-permute-start(f32[32,128]{1,0:T(8,128)S(1)} %get-tuple-element.28), channel_id=1, source_target_pairs={{0,2},{1,3},{2,0},{3,1},{4,6},{5,7},{6,4},{7,5},{8,10},{9,11},{10,... | collective-permute-start | bytes 49160 | tf_op jit(solution)/shard_map/ppermute | solution.py:24
  23.5 3.4 %collective-permute-start.8 = (f32[32,128]{1,0:T(8,128)S(1)}, f32[32,128]{1,0:T(8,128)S(1)}, u32[]{:S(2)}, u32[]{:S(2)}) collective-permute-start(f32[32,128]{1,0:T(8,128)S(1)} %get-tuple-element.28), channel_id=1, source_target_pairs={{0,3},{1,2},{2,1},{3,0},{4,7},{5,6},{6,5},{7,4},{8,11},{9,10},{10,... | collective-permute-start | bytes 49160 | tf_op jit(solution)/shard_map/ppermute | solution.py:24
  24.7 2.3 %collective-permute-start.6 = (f32[32,128]{1,0:T(8,128)S(1)}, f32[32,128]{1,0:T(8,128)S(1)}, u32[]{:S(2)}, u32[]{:S(2)}) collective-permute-start(f32[32,128]{1,0:T(8,128)S(1)} %get-tuple-element.28), channel_id=1, source_target_pairs={{0,1},{1,0},{2,3},{3,2},{4,5},{5,4},{6,7},{7,6},{8,9},{9,8},{10,11... | collective-permute-start | bytes 49160 | tf_op jit(solution)/shard_map/ppermute | solution.py:24
  27.0 18.8 %collective-permute-start.9 = (f32[32,128]{1,0:T(8,128)S(1)}, f32[32,128]{1,0:T(8,128)S(1)}, u32[]{:S(2)}, u32[]{:S(2)}) collective-permute-start(f32[32,128]{1,0:T(8,128)S(1)} %add_add_fusion.1), channel_id=1, source_target_pairs={{0,4},{4,0},{8,12},{12,8},{16,20},{20,16},{24,28},{28,24},{1,5},{5... | collective-permute-start | bytes 49160 | tf_op jit(solution)/shard_map/ppermute | solution.py:24
  29.4 11.4 %all-to-all-start = ((s32[8,2,128]{2,1,0:T(2,128)}), s32[8,2,128]{2,1,0:T(2,128)S(1)}, u32[]{:S(2)}, u32[]{:S(2)}) async-start(s32[8,2,128]{2,1,0:T(2,128)} %broadcast_in_dim.20), calls=%async_computation | async-start | bytes 16384 | tf_op jit(solution)/shard_map/all_to_all | solution.py:291
  46.0 3.8 %collective-permute-start.11 = (f32[32,128]{1,0:T(8,128)S(1)}, f32[32,128]{1,0:T(8,128)S(1)}, u32[]{:S(2)}, u32[]{:S(2)}) collective-permute-start(f32[32,128]{1,0:T(8,128)S(1)} %convolution_subtract_fusion.5), channel_id=1, source_target_pairs={{0,4},{4,0},{8,12},{12,8},{16,20},{20,16},{24,28},{28,24},{1,5},{5... | collective-permute-start | bytes 49160 | tf_op jit(solution)/shard_map/ppermute | solution.py:24
  46.6 4.6 %collective-permute-start.10 = (f32[32,128]{1,0:T(8,128)S(1)}, f32[32,128]{1,0:T(8,128)S(1)}, u32[]{:S(2)}, u32[]{:S(2)}) collective-permute-start(f32[32,128]{1,0:T(8,128)S(1)} %convolution_subtract_fusion.5), channel_id=1, source_target_pairs={{0,12},{4,8},{8,4},{12,0},{16,28},{20,24},{24,20},{28,16},{1,13},{... | collective-permute-start | bytes 49160 | tf_op jit(solution)/shard_map/ppermute | solution.py:24
  51.5 5.0 %collective-permute-start.13 = (f32[32,128]{1,0:T(8,128)S(1)}, f32[32,128]{1,0:T(8,128)S(1)}, u32[]{:S(2)}, u32[]{:S(2)}) collective-permute-start(f32[32,128]{1,0:T(8,128)S(1)} %convolution_subtract_fusion.4), channel_id=1, source_target_pairs={{0,8},{4,12},{8,0},{12,4},{16,24},{20,28},{24,16},{28,20},{1,9},{5... | collective-permute-start | bytes 49160 | tf_op jit(solution)/shard_map/ppermute | solution.py:24
  52.1 5.5 %collective-permute-start.12 = (f32[32,128]{1,0:T(8,128)S(1)}, f32[32,128]{1,0:T(8,128)S(1)}, u32[]{:S(2)}, u32[]{:S(2)}) collective-permute-start(f32[32,128]{1,0:T(8,128)S(1)} %convolution_subtract_fusion.4), channel_id=1, source_target_pairs={{0,24},{4,28},{8,16},{12,20},{16,8},{20,12},{24,0},{28,4},{1,25},{... | collective-permute-start | bytes 49160 | tf_op jit(solution)/shard_map/ppermute | solution.py:24
  53.6 16.6 %collective-permute-start.20 = (f32[256,128]{1,0:T(8,128)S(1)}, f32[256,128]{1,0:T(8,128)S(1)}, u32[]{:S(2)}, u32[]{:S(2)}) collective-permute-start(f32[256,128]{1,0:T(8,128)S(1)} %bitcast.32), channel_id=1, source_target_pairs={{0,1},{1,0},{2,3},{3,2},{4,5},{5,4},{6,7},{7,6},{8,9},{9,8},{10,11... | collective-permute-start | bytes 393224 | tf_op jit(solution)/shard_map/ppermute | solution.py:24
  53.6 11.8 %collective-permute-start.21 = (f32[256,128]{1,0:T(8,128)S(1)}, f32[256,128]{1,0:T(8,128)S(1)}, u32[]{:S(2)}, u32[]{:S(2)}) collective-permute-start(f32[256,128]{1,0:T(8,128)S(1)} %bitcast.33), channel_id=1, source_target_pairs={{0,2},{1,3},{2,0},{3,1},{4,6},{5,7},{6,4},{7,5},{8,10},{9,11},{10,... | collective-permute-start | bytes 393224 | tf_op jit(solution)/shard_map/ppermute | solution.py:24
  55.0 7.0 %collective-permute-start.14 = (f32[160,128]{1,0:T(8,128)S(1)}, f32[160,128]{1,0:T(8,128)S(1)}, u32[]{:S(2)}, u32[]{:S(2)}) collective-permute-start(f32[160,128]{1,0:T(8,128)S(1)} %get-tuple-element.31), channel_id=1, source_target_pairs={{0,16},{4,20},{8,24},{12,28},{16,0},{20,4},{24,8},{28,12},{1,17},{... | collective-permute-start | bytes 245768 | tf_op jit(solution)/shard_map/ppermute | solution.py:24
  62.4 14.7 %copy-start.1 = (f32[1,256,1024]{2,1,0:T(8,128)S(1)}, f32[1,256,1024]{2,1,0:T(8,128)}, u32[]{:S(2)}) copy-start(f32[1,256,1024]{2,1,0:T(8,128)} %param.16) | copy-start | bytes 3145732
  62.4 3.8 %collective-permute-start.15 = (f32[32,128]{1,0:T(8,128)S(1)}, f32[32,128]{1,0:T(8,128)S(1)}, u32[]{:S(2)}, u32[]{:S(2)}) collective-permute-start(f32[32,128]{1,0:T(8,128)S(1)} %get-tuple-element.45), channel_id=1, source_target_pairs={{0,8},{4,12},{8,0},{12,4},{16,24},{20,28},{24,16},{28,20},{1,9},{5... | collective-permute-start | bytes 49160 | tf_op jit(solution)/shard_map/ppermute | solution.py:24
  62.5 5.6 %collective-permute-start.16 = (f32[32,128]{1,0:T(8,128)S(1)}, f32[32,128]{1,0:T(8,128)S(1)}, u32[]{:S(2)}, u32[]{:S(2)}) collective-permute-start(f32[32,128]{1,0:T(8,128)S(1)} %get-tuple-element.44), channel_id=1, source_target_pairs={{0,24},{4,28},{8,16},{12,20},{16,8},{20,12},{24,0},{28,4},{1,25},{... | collective-permute-start | bytes 49160 | tf_op jit(solution)/shard_map/ppermute | solution.py:24
  65.4 4.8 %collective-permute-start.22 = (f32[256,128]{1,0:T(8,128)S(1)}, f32[256,128]{1,0:T(8,128)S(1)}, u32[]{:S(2)}, u32[]{:S(2)}) collective-permute-start(f32[256,128]{1,0:T(8,128)S(1)} %collective-permute-done.21.refs_2_), channel_id=1, source_target_pairs={{0,1},{1,0},{2,3},{3,2},{4,5},{5,4},{6,7},{7,6},{8,9},{9,8},{10,11... | collective-permute-start | bytes 393224 | tf_op jit(solution)/shard_map/ppermute | solution.py:24
  68.3 7.0 %collective-permute-start.17 = (f32[32,128]{1,0:T(8,128)S(1)}, f32[32,128]{1,0:T(8,128)S(1)}, u32[]{:S(2)}, u32[]{:S(2)}) collective-permute-start(f32[32,128]{1,0:T(8,128)S(1)} %get-tuple-element.43), channel_id=1, source_target_pairs={{0,4},{4,0},{8,12},{12,8},{16,20},{20,16},{24,28},{28,24},{1,5},{5... | collective-permute-start | bytes 49160 | tf_op jit(solution)/shard_map/ppermute | solution.py:24
  69.9 5.4 %collective-permute-start.18 = (f32[32,128]{1,0:T(8,128)S(1)}, f32[32,128]{1,0:T(8,128)S(1)}, u32[]{:S(2)}, u32[]{:S(2)}) collective-permute-start(f32[32,128]{1,0:T(8,128)S(1)} %get-tuple-element.42), channel_id=1, source_target_pairs={{0,12},{4,8},{8,4},{12,0},{16,28},{20,24},{24,20},{28,16},{1,13},{... | collective-permute-start | bytes 49160 | tf_op jit(solution)/shard_map/ppermute | solution.py:24
  72.2 6.1 %collective-permute-start.23 = (f32[32,128]{1,0:T(8,128)S(1)}, f32[32,128]{1,0:T(8,128)S(1)}, u32[]{:S(2)}, u32[]{:S(2)}) collective-permute-start(f32[32,128]{1,0:T(8,128)S(1)} %convolution_subtract_fusion.3), channel_id=1, source_target_pairs={{0,16},{4,20},{8,24},{12,28},{16,0},{20,4},{24,8},{28,12},{1,17},{... | collective-permute-start | bytes 49160 | tf_op jit(solution)/shard_map/ppermute | solution.py:24
  75.5 3.8 %collective-permute-start.19 = (f32[32,128]{1,0:T(8,128)S(1)}, f32[32,128]{1,0:T(8,128)S(1)}, u32[]{:S(2)}, u32[]{:S(2)}) collective-permute-start(f32[32,128]{1,0:T(8,128)S(1)} %slice.34), channel_id=1, source_target_pairs={{0,4},{4,0},{8,12},{12,8},{16,20},{20,16},{24,28},{28,24},{1,5},{5... | collective-permute-start | bytes 49160 | tf_op jit(solution)/shard_map/ppermute | solution.py:24
  80.8 4.0 %collective-permute-start.25 = (f32[32,128]{1,0:T(8,128)S(1)}, f32[32,128]{1,0:T(8,128)S(1)}, u32[]{:S(2)}, u32[]{:S(2)}) collective-permute-start(f32[32,128]{1,0:T(8,128)S(1)} %get-tuple-element.35), channel_id=1, source_target_pairs={{0,2},{1,3},{2,0},{3,1},{4,6},{5,7},{6,4},{7,5},{8,10},{9,11},{10,... | collective-permute-start | bytes 49160 | tf_op jit(solution)/shard_map/ppermute | solution.py:24
  81.4 3.3 %collective-permute-start.26 = (f32[32,128]{1,0:T(8,128)S(1)}, f32[32,128]{1,0:T(8,128)S(1)}, u32[]{:S(2)}, u32[]{:S(2)}) collective-permute-start(f32[32,128]{1,0:T(8,128)S(1)} %get-tuple-element.35), channel_id=1, source_target_pairs={{0,3},{1,2},{2,1},{3,0},{4,7},{5,6},{6,5},{7,4},{8,11},{9,10},{10,... | collective-permute-start | bytes 49160 | tf_op jit(solution)/shard_map/ppermute | solution.py:24
  81.4 3.3 %collective-permute-start.24 = (f32[32,128]{1,0:T(8,128)S(1)}, f32[32,128]{1,0:T(8,128)S(1)}, u32[]{:S(2)}, u32[]{:S(2)}) collective-permute-start(f32[32,128]{1,0:T(8,128)S(1)} %get-tuple-element.35), channel_id=1, source_target_pairs={{0,1},{1,0},{2,3},{3,2},{4,5},{5,4},{6,7},{7,6},{8,9},{9,8},{10,11... | collective-permute-start | bytes 49160 | tf_op jit(solution)/shard_map/ppermute | solution.py:24
  (5 other events, 29.2 us)

commit v5 on v4

--- a/solution.py
+++ b/solution.py
@@ -161,15 +161,14 @@
 
 
 def project(top, *refs):
-    state_ref, below_ref, moved_in_ref, lift_ref, pair_ref, above_ref, back_ref = refs[:7]
-    below_map_ref, rest_ref, metric_ref, basis_leaf_ref, basis_sep_ref = refs[7:12]
-    leaf_ref, sep_ref, inner_ref = refs[12:]
-    couple = moved_in_ref.shape[1]
+    state_ref, leaf_above_ref, lift_ref, pair_ref, above_ref, back_ref = refs[:6]
+    below_map_ref, rest_ref, metric_ref, basis_leaf_ref, basis_sep_ref = refs[6:11]
+    leaf_ref, sep_ref, inner_ref = refs[11:]
+    couple = leaf_above_ref.shape[1]
     block = state_ref.shape[0]
     rank = basis_leaf_ref.shape[0]
     level = level_of(lax.axis_index("leaf"), top)
-    above = jnp.where(level == 1, below_ref[:, couple:], moved_in_ref[...])
-    leaf = state_ref[...] - mm(above, lift_ref[...])
+    leaf = state_ref[...] - mm(leaf_above_ref[...], lift_ref[...])
     width = sep_ref.shape[1]
     is_root = level > top
     upper = jnp.where(is_root, back_ref[...], pair_ref[:, couple:])
@@ -351,6 +350,9 @@
 
     pair = jnp.concatenate([swap(leaf_push, "leaf", 1), leaf_push], 1)
     pair = jnp.where(level == 1, pair, 0.0)
+    gift = row_base[:, :couple] - mm(pair, turn_weights[:, :couple])
+    gift = jnp.concatenate([down_weights[:, :couple], gift], 0)
+    gift = swap(gift, "leaf", 1)
     for height in range(2, top + 1):
         step = 2 ** (height - 2)
         term = push_base - mm(pair, up_weights)
@@ -366,12 +368,18 @@
     for height in range(top, 1, -1):
         step = 2 ** (height - 2)
         below = row_base - mm(above, down_weights)
+        lower = swap(below[:, :couple], "leaf", 3 * step)
         upper = swap(below[:, couple:], "leaf", step)
-        lower = swap(below[:, :couple], "leaf", 3 * step)
+        if height == 2:
+            across = swap(below[:, :couple], "leaf", 2)
         is_upper = (group // (2 * step)) % 2 == 1
         above = jnp.where(level == height - 1, jnp.where(is_upper, upper, lower), above)
-    below = row_base - mm(above, down_weights)
-    moved_in = swap(below[:, :couple], "leaf", 1)
+    odd = level == 1
+    own_way = jnp.concatenate([down_weights[:, couple:], row_base[:, couple:]], 0)
+    way = jnp.where(odd, own_way, gift)
+    source = jnp.where(odd, above, jnp.where(level == 2, below[:, couple:], across))
+    leaf_above = way[couple:] - mm(source, way[:couple])
+
     rank = basis_leaf.shape[0]
     metric = mm(basis_leaf, basis_leaf, 1, 1) + mm(basis_sep, basis_sep, 1, 1)
     lanes = -(-(3 * rank - block + 1) // 128) * 128
@@ -382,11 +390,11 @@
             pltpu.VMEM((block, sep_width), jnp.float32),
             pltpu.VMEM((block, lanes), jnp.float32),
         ),
-        in_specs=[vmem] * 12,
+        in_specs=[vmem] * 11,
         out_specs=(vmem,) * 3,
         name="project",
     )(
-        *held([leaf_state, below, moved_in, leaf_lift, pair, above, back, below_map, rest, metric]),
+        *held([leaf_state, leaf_above, leaf_lift, pair, above, back, below_map, rest, metric]),
         basis_leaf,
         basis_sep,
     )

time: 99.3 us -> 85.1 us (0.86)
  waiting for transfers between devices: 34.9 us -> 15.8 us
  starting transfers between devices: 32.6 us -> 36.1 us
  blocking collectives: 10.6 us -> 11.7 us
    ppermute x27 -> x28, waiting for transfers between devices: 28.3 us -> 15.8 us  [swap(): lax.ppermute(value, axis, [(one, one ^ mask) for one in range(count)])]
    all_to_all x1, waiting for transfers between devices: 6.52 us -> 0.01 us  [on_device(): lax.all_to_all(jnp.broadcast_to(lists[None], (groups,) + lists.shape), 'l...]
    ppermute x27 -> x28, starting transfers between devices: 27.7 us -> 30 us  [swap(): lax.ppermute(value, axis, [(one, one ^ mask) for one in range(count)])]
    all_to_all x1, starting transfers between devices: 4.88 us -> 6.09 us  [on_device(): lax.all_to_all(jnp.broadcast_to(lists[None], (groups,) + lists.shape), 'l...]
    all_to_all x1, blocking collectives: 10.6 us -> 11.7 us  [on_device(): lax.all_to_all(jnp.broadcast_to(inner[None], (groups,) + inner.shape), 'l...]
    dot_general x11 -> x12, matrix products: 3.08 us -> 3.24 us  [mm(): lax.dot_general(former, latter, (((left,), (right,)), ((), ())), precisio...]
  transfers between devices with their start and end apart: 28 -> 29, of which waited for: 13 -> 8; matrix products, arithmetic and copies ran while one was open for 3% -> 4% of each run, Pallas kernels for 10% -> 12%
where the time goes in v5:
time: 85.1 us; the launch traced here: 84.7 us
  starting transfers between devices  36.1 us (42%)
  Pallas kernels  16 us (19%)
  waiting for transfers between devices  15.8 us (19%)
  blocking collectives  11.7 us (14%)
  matrix products  3.24 us (4%)
  between operations  1.11 us (1%)
    ppermute x28, starting transfers between devices, swap(): lax.ppermute(value, axis, [(one, one ^ mask) for one in range(count)])  30 us
    ppermute x28, waiting for transfers between devices, swap(): lax.ppermute(value, axis, [(one, one ^ mask) for one in range(count)])  15.8 us
    all_to_all x1, blocking collectives, on_device(): lax.all_to_all(jnp.broadcast_to(inner[None], (groups,) + inner.shape), 'l...  11.7 us
    all_to_all x1, starting transfers between devices, on_device(): lax.all_to_all(jnp.broadcast_to(lists[None], (groups,) + lists.shape), 'l...  6.09 us
    pallas_call x1, Pallas kernels, on_device(): pl.pallas_call(lambda *refs: reduce_front(top, *refs), out_shape=tuple((p...  5.01 us
    pallas_call x1, Pallas kernels, on_device(): pl.pallas_call(lambda *refs: finish(total_rows, *refs), out_shape=(jax.Sh...  3.44 us
    dot_general x12, matrix products, mm(): lax.dot_general(former, latter, (((left,), (right,)), ((), ())), precisio...  3.24 us
    pallas_call x1, Pallas kernels, on_device(): pl.pallas_call(solve_leaf, out_shape=(pltpu.VMEM((block, leaf_width), jnp...  3.09 us
  transfers between devices with their start and end apart: 29, of which 8 were waited for; matrix products, arithmetic and copies ran while one was open for 4% of the time, Pallas kernels for 12%

profile of v5, /device:TPU:0, one launch (start us, length us, event | category | flops | bytes accessed | tf_op | source)
XLA Modules:
  0.0 84.7 jit_solution(525524127143010353)
XLA Ops:
  0.7 1.1 %pack.1.refs_2_ = f32[800,128]{1,0:T(8,128)S(1)} custom-call(f32[128,512]{1,0:T(8,128)} %bitcast.27, f32[128,128]{1,0:T(8,128)} %bitcast.32, f32[128,128]{1,0:T(8,128)} %bitcast.33, f32[32,128]{1,0:T(8,128)} %rhs_ref.1), custom_call_target="tpu_custom_call" | custom-call | tf_op jit(solution)/shard_map/pack/pallas_call | solution.py:278
  2.3 2.6 %collective-permute-start.1 = (f32[32,256]{1,0:T(8,128)S(1)}, f32[32,256]{1,0:T(8,128)S(1)}, u32[]{:S(2)}, u32[]{:S(2)}) collective-permute-start(f32[32,256]{1,0:T(8,128)S(1)} %copy-done.6), channel_id=1, source_target_pairs={{0,2},{1,3},{2,0},{3,1},{4,6},{5,7},{6,4},{7,5},{8,10},{9,11},{10,... | collective-permute-start | bytes 98312 | tf_op jit(solution)/shard_map/ppermute | solution.py:24
  5.5 6.1 %all-to-all-start = ((s32[8,2,128]{2,1,0:T(2,128)}), s32[8,2,128]{2,1,0:T(2,128)S(1)}, u32[]{:S(2)}, u32[]{:S(2)}) async-start(s32[8,2,128]{2,1,0:T(2,128)} %broadcast_in_dim.20), calls=%async_computation | async-start | bytes 16384 | tf_op jit(solution)/shard_map/all_to_all | solution.py:290
  11.6 1.5 %collective-permute-start.4 = (f32[800,128]{1,0:T(8,128)S(1)}, f32[800,128]{1,0:T(8,128)}, u32[]{:S(2)}, u32[]{:S(2)}) collective-permute-start(f32[800,128]{1,0:T(8,128)S(1)} %pack.1.refs_2_), channel_id=1, source_target_pairs={{0,2},{1,3},{2,0},{3,1},{4,6},{5,7},{6,4},{7,5},{8,10},{9,11},{10,... | collective-permute-start | bytes 1228808 | tf_op jit(solution)/shard_map/ppermute | solution.py:24
  13.9 3.1 %solve_leaf.1 = (f32[32,256]{1,0:T(8,128)S(1)}, f32[32,128]{1,0:T(8,128)S(1)}) custom-call(s32[1,1024]{1,0:T(1,128)} %pivot_ref.3, f32[256,1024]{1,0:T(8,128)} %bitcast.26, f32[128,256]{1,0:T(8,128)} %bitcast.28, f32[32,256]{1,0:T(8,128)} %refs_0_.1, f32[32,256]{1,0:T(8,128)S(1)} %collective-permute-done.refs_1_, ...), custom_call_target="tpu_custom_call" | custom-call | tf_op jit(solution)/shard_map/solve_leaf/pallas_call | solution.py:295
  17.0 1.5 %collective-permute-start.7 = (f32[32,128]{1,0:T(8,128)S(1)}, f32[32,128]{1,0:T(8,128)S(1)}, u32[]{:S(2)}, u32[]{:S(2)}) collective-permute-start(f32[32,128]{1,0:T(8,128)S(1)} %get-tuple-element.29), channel_id=1, source_target_pairs={{0,2},{1,3},{2,0},{3,1},{4,6},{5,7},{6,4},{7,5},{8,10},{9,11},{10,... | collective-permute-start | bytes 49160 | tf_op jit(solution)/shard_map/ppermute | solution.py:24
  18.5 0.6 collective-permute-start.6
  19.5 6.9 %collective-permute-done.7 = f32[32,128]{1,0:T(8,128)S(1)} collective-permute-done((f32[32,128]{1,0:T(8,128)S(1)}, f32[32,128]{1,0:T(8,128)S(1)}, u32[]{:S(2)}, u32[]{:S(2)}) %collective-permute-start.7) | collective-permute-done | bytes 16416 | tf_op jit(solution)/shard_map/ppermute | solution.py:24
  27.5 1.8 %collective-permute-start.9 = (f32[32,128]{1,0:T(8,128)S(1)}, f32[32,128]{1,0:T(8,128)S(1)}, u32[]{:S(2)}, u32[]{:S(2)}) collective-permute-start(f32[32,128]{1,0:T(8,128)S(1)} %add_add_fusion.1), channel_id=1, source_target_pairs={{0,4},{4,0},{8,12},{12,8},{16,20},{20,16},{24,28},{28,24},{1,5},{5... | collective-permute-start | bytes 49160 | tf_op jit(solution)/shard_map/ppermute | solution.py:24
  29.3 1.9 %turn_pull.1 = f32[128,1024]{1,0:T(8,128)S(1)} custom-call(s32[1,1024]{1,0:T(1,128)} %pivot_ref.3, f32[256,128]{1,0:T(8,128)} %bitcast.29, f32[256,128]{1,0:T(8,128)S(1)} %collective-permute-done.21.refs_1_, f32[256,128]{1,0:T(8,128)S(1)} %collective-permute-done.22.refs_2_, f32[256,128]{1,0:T(8,128)S(1)} %collective-permute-done.23.refs_3_), custom_call_target="tpu_custom_call" | custom-call | tf_op jit(solution)/shard_map/turn_pull/pallas_call | solution.py:339
  31.2 1.2 %fusion.25.refs_2_ = f32[128,256]{1,0:T(8,128)S(1)} fusion(f32[128,1024]{1,0:T(8,128)S(1)} %turn_pull.1, f32[1,256,1024]{2,1,0:T(8,128)S(1)} %copy-done.1), kind=kOutput, calls=%fused_computation.38 | convolution fusion | flops 402653184 | bytes 1703936 | tf_op jit(solution)/shard_map/dot_general | solution.py:13
  32.5 5.0 %reduce_front.1 = (f32[256,128]{1,0:T(8,128)S(1)}, f32[160,128]{1,0:T(8,128)S(1)}, f32[256,128]{1,0:T(8,128)S(1)}, f32[256,256]{1,0:T(8,128)S(1)}, f32[128,256]{...) custom-call(s32[1,512]{1,0:T(1,128)} %refs_0_.2, s32[16,128]{1,0:T(8,128)S(1)} %bitcast.25, ...), custom_call_target="tpu_custom_call" | custom-call | tf_op jit(solution)/shard_map/reduce_front/pallas_call | solution.py:326
  37.7 1.1 %collective-permute-start.11 = (f32[32,128]{1,0:T(8,128)S(1)}, f32[32,128]{1,0:T(8,128)S(1)}, u32[]{:S(2)}, u32[]{:S(2)}) collective-permute-start(f32[32,128]{1,0:T(8,128)S(1)} %convolution_subtract_fusion.5), channel_id=1, source_target_pairs={{0,4},{4,0},{8,12},{12,8},{16,20},{20,16},{24,28},{28,24},{1,5},{5... | collective-permute-start | bytes 49160 | tf_op jit(solution)/shard_map/ppermute | solution.py:24
  38.8 1.9 %collective-permute-start.10 = (f32[32,128]{1,0:T(8,128)S(1)}, f32[32,128]{1,0:T(8,128)S(1)}, u32[]{:S(2)}, u32[]{:S(2)}) collective-permute-start(f32[32,128]{1,0:T(8,128)S(1)} %convolution_subtract_fusion.5), channel_id=1, source_target_pairs={{0,12},{4,8},{8,4},{12,0},{16,28},{20,24},{24,20},{28,16},{1,13},{... | collective-permute-start | bytes 49160 | tf_op jit(solution)/shard_map/ppermute | solution.py:24
  40.7 2.4 %collective-permute-start.15 = (f32[160,128]{1,0:T(8,128)S(1)}, f32[160,128]{1,0:T(8,128)S(1)}, u32[]{:S(2)}, u32[]{:S(2)}) collective-permute-start(f32[160,128]{1,0:T(8,128)S(1)} %get-tuple-element.32), channel_id=1, source_target_pairs={{0,16},{4,20},{8,24},{12,28},{16,0},{20,4},{24,8},{28,12},{1,17},{... | collective-permute-start | bytes 245768 | tf_op jit(solution)/shard_map/ppermute | solution.py:24
  43.6 1.5 %collective-permute-start.13 = (f32[32,128]{1,0:T(8,128)S(1)}, f32[32,128]{1,0:T(8,128)S(1)}, u32[]{:S(2)}, u32[]{:S(2)}) collective-permute-start(f32[32,128]{1,0:T(8,128)S(1)} %convolution_subtract_fusion.4), channel_id=1, source_target_pairs={{0,8},{4,12},{8,0},{12,4},{16,24},{20,28},{24,16},{28,20},{1,9},{5... | collective-permute-start | bytes 49160 | tf_op jit(solution)/shard_map/ppermute | solution.py:24
  45.1 2.5 %collective-permute-start.12 = (f32[32,128]{1,0:T(8,128)S(1)}, f32[32,128]{1,0:T(8,128)S(1)}, u32[]{:S(2)}, u32[]{:S(2)}) collective-permute-start(f32[32,128]{1,0:T(8,128)S(1)} %convolution_subtract_fusion.4), channel_id=1, source_target_pairs={{0,24},{4,28},{8,16},{12,20},{16,8},{20,12},{24,0},{28,4},{1,25},{... | collective-permute-start | bytes 49160 | tf_op jit(solution)/shard_map/ppermute | solution.py:24
  47.8 2.8 %collective-permute-done.12 = f32[32,128]{1,0:T(8,128)S(1)} collective-permute-done((f32[32,128]{1,0:T(8,128)S(1)}, f32[32,128]{1,0:T(8,128)S(1)}, u32[]{:S(2)}, u32[]{:S(2)}) %collective-permute-start.12) | collective-permute-done | bytes 16416 | tf_op jit(solution)/shard_map/ppermute | solution.py:24
  51.6 2.5 %collective-permute-start.17 = (f32[32,128]{1,0:T(8,128)S(1)}, f32[32,128]{1,0:T(8,128)S(1)}, u32[]{:S(2)}, u32[]{:S(2)}) collective-permute-start(f32[32,128]{1,0:T(8,128)S(1)} %get-tuple-element.46), channel_id=1, source_target_pairs={{0,24},{4,28},{8,16},{12,20},{16,8},{20,12},{24,0},{28,4},{1,25},{... | collective-permute-start | bytes 49160 | tf_op jit(solution)/shard_map/ppermute | solution.py:24
  54.2 1.2 %collective-permute-start.14 = (f32[160,128]{1,0:T(8,128)S(1)}, f32[160,128]{1,0:T(8,128)S(1)}, u32[]{:S(2)}, u32[]{:S(2)}) collective-permute-start(f32[160,128]{1,0:T(8,128)S(1)} %pad_maximum_fusion), channel_id=1, source_target_pairs={{0,4},{4,0},{8,12},{12,8},{16,20},{20,16},{24,28},{28,24},{1,5},{5... | collective-permute-start | bytes 245768 | tf_op jit(solution)/shard_map/ppermute | solution.py:24
  55.3 0.8 collective-permute-start.24
  56.1 1.1 %collective-permute-done.17 = f32[32,128]{1,0:T(8,128)S(1)} collective-permute-done((f32[32,128]{1,0:T(8,128)S(1)}, f32[32,128]{1,0:T(8,128)S(1)}, u32[]{:S(2)}, u32[]{:S(2)}) %collective-permute-start.17) | collective-permute-done | bytes 16416 | tf_op jit(solution)/shard_map/ppermute | solution.py:24
  57.4 1.1 %collective-permute-start.18 = (f32[32,128]{1,0:T(8,128)S(1)}, f32[32,128]{1,0:T(8,128)S(1)}, u32[]{:S(2)}, u32[]{:S(2)}) collective-permute-start(f32[32,128]{1,0:T(8,128)S(1)} %get-tuple-element.45), channel_id=1, source_target_pairs={{0,4},{4,0},{8,12},{12,8},{16,20},{20,16},{24,28},{28,24},{1,5},{5... | collective-permute-start | bytes 49160 | tf_op jit(solution)/shard_map/ppermute | solution.py:24
  59.1 1.9 %collective-permute-start.20 = (f32[32,128]{1,0:T(8,128)S(1)}, f32[32,128]{1,0:T(8,128)S(1)}, u32[]{:S(2)}, u32[]{:S(2)}) collective-permute-start(f32[32,128]{1,0:T(8,128)S(1)} %get-tuple-element.44), channel_id=1, source_target_pairs={{0,8},{4,12},{8,0},{12,4},{16,24},{20,28},{24,16},{28,20},{1,9},{5... | collective-permute-start | bytes 49160 | tf_op jit(solution)/shard_map/ppermute | solution.py:24
  61.2 1.9 %collective-permute-done.19 = f32[32,128]{1,0:T(8,128)S(1)} collective-permute-done((f32[32,128]{1,0:T(8,128)S(1)}, f32[32,128]{1,0:T(8,128)S(1)}, u32[]{:S(2)}, u32[]{:S(2)}) %collective-permute-start.19) | collective-permute-done | bytes 16416 | tf_op jit(solution)/shard_map/ppermute | solution.py:24
  63.4 1.5 %project.1 = (f32[32,256]{1,0:T(8,128)S(1)}, f32[32,128]{1,0:T(8,128)S(1)}, f32[32,128]{1,0:T(8,128)S(1)}) custom-call(f32[32,256]{1,0:T(8,128)S(1)} %get-tuple-element.24.refs_0_, f32[32,128]{1,0:T(8,128)S(1)} %slice_subtract_fusion.1.refs_1_, f32[128,256]{1,0:T(8,128)S(1)} %fusion.25.refs_2_, f32[32,256]{1,0:T(8,128)S(1)} %maximum_select_fusion.3.refs_3_, ...), custom_call_target="tpu_custom_call" | custom-call | tf_op jit(solution)/shard_map/project/pallas_call | solution.py:386
  64.8 1.6 %collective-permute-start.26 = (f32[32,128]{1,0:T(8,128)S(1)}, f32[32,128]{1,0:T(8,128)S(1)}, u32[]{:S(2)}, u32[]{:S(2)}) collective-permute-start(f32[32,128]{1,0:T(8,128)S(1)} %get-tuple-element.35), channel_id=1, source_target_pairs={{0,2},{1,3},{2,0},{3,1},{4,6},{5,7},{6,4},{7,5},{8,10},{9,11},{10,... | collective-permute-start | bytes 49160 | tf_op jit(solution)/shard_map/ppermute | solution.py:24
  66.4 0.6 collective-permute-start.25
  67.0 1.6 %collective-permute-done.26 = f32[32,128]{1,0:T(8,128)S(1)} collective-permute-done((f32[32,128]{1,0:T(8,128)S(1)}, f32[32,128]{1,0:T(8,128)S(1)}, u32[]{:S(2)}, u32[]{:S(2)}) %collective-permute-start.26) | collective-permute-done | bytes 16416 | tf_op jit(solution)/shard_map/ppermute | solution.py:24
  68.6 0.9 %collective-permute-done.27 = f32[32,128]{1,0:T(8,128)S(1)} collective-permute-done((f32[32,128]{1,0:T(8,128)S(1)}, f32[32,128]{1,0:T(8,128)S(1)}, u32[]{:S(2)}, u32[]{:S(2)}) %collective-permute-start.27) | collective-permute-done | bytes 16416 | tf_op jit(solution)/shard_map/ppermute | solution.py:24
  69.6 11.7 %all_to_all.10.refs_0_ = f32[8,32,128]{2,1,0:T(8,128)S(1)} all-to-all(f32[8,32,128]{2,1,0:T(8,128)S(1)} %broadcast_in_dim.23), channel_id=1, replica_groups=mesh['leaf'=8,'front'=4] {'leaf'}, dimensions={0} | all-to-all | bytes 262144 | tf_op jit(solution)/shard_map/all_to_all | solution.py:402
  81.3 3.4 %finish.1 = (f32[32,256]{1,0:T(8,128)}, f32[32,128]{1,0:T(8,128)}, f32[32,50]{1,0:T(8,128)}, f32[32,32]{1,0:T(8,128)}) custom-call(f32[8,32,128]{2,1,0:T(8,128)S(1)} %all_to_all.10.refs_0_, f32[32,256]{1,0:T(8,128)S(1)} %get-tuple-element.36.refs_1_, f32[32,128]{1,0:T(8,128)S(1)} %get-tuple-element.37.refs_2_, f32[50,256]{1,0:T(8,128)} %refs_3_.1, ...), custom_call_target="tpu_custom_call" | custom-call | tf_op jit(solution)/shard_map/finish/pallas_call | solution.py:405
  (78 shorter events, 6.1 us)
Async XLA Ops:
  0.7 13.0 %copy-start.2 = (f32[50,256]{1,0:T(8,128)S(1)}, f32[50,256]{1,0:T(8,128)}, u32[]{:S(2)}) copy-start(f32[50,256]{1,0:T(8,128)} %refs_3_.1) | copy-start | bytes 153604
  1.8 24.7 %copy-start = (f32[800,128]{1,0:T(8,128)}, f32[800,128]{1,0:T(8,128)S(1)}, u32[]{:S(2)}) copy-start(f32[800,128]{1,0:T(8,128)S(1)} %pack.1.refs_2_) | copy-start | bytes 1228804
  1.8 12.1 %collective-permute-start = (f32[32,256]{1,0:T(8,128)S(1)}, f32[32,256]{1,0:T(8,128)S(1)}, u32[]{:S(2)}, u32[]{:S(2)}) collective-permute-start(f32[32,256]{1,0:T(8,128)S(1)} %copy-done.6), channel_id=1, source_target_pairs={{0,1},{1,0},{2,3},{3,2},{4,5},{5,4},{6,7},{7,6},{8,9},{9,8},{10,11... | collective-permute-start | bytes 98312 | tf_op jit(solution)/shard_map/ppermute | solution.py:24
  2.3 11.5 %collective-permute-start.1 = (f32[32,256]{1,0:T(8,128)S(1)}, f32[32,256]{1,0:T(8,128)S(1)}, u32[]{:S(2)}, u32[]{:S(2)}) collective-permute-start(f32[32,256]{1,0:T(8,128)S(1)} %copy-done.6), channel_id=1, source_target_pairs={{0,2},{1,3},{2,0},{3,1},{4,6},{5,7},{6,4},{7,5},{8,10},{9,11},{10,... | collective-permute-start | bytes 98312 | tf_op jit(solution)/shard_map/ppermute | solution.py:24
  4.9 9.0 %collective-permute-start.2 = (f32[32,256]{1,0:T(8,128)S(1)}, f32[32,256]{1,0:T(8,128)S(1)}, u32[]{:S(2)}, u32[]{:S(2)}) collective-permute-start(f32[32,256]{1,0:T(8,128)S(1)} %copy-done.6), channel_id=1, source_target_pairs={{0,3},{1,2},{2,1},{3,0},{4,7},{5,6},{6,5},{7,4},{8,11},{9,10},{10,... | collective-permute-start | bytes 98312 | tf_op jit(solution)/shard_map/ppermute | solution.py:24
  5.5 26.9 %all-to-all-start = ((s32[8,2,128]{2,1,0:T(2,128)}), s32[8,2,128]{2,1,0:T(2,128)S(1)}, u32[]{:S(2)}, u32[]{:S(2)}) async-start(s32[8,2,128]{2,1,0:T(2,128)} %broadcast_in_dim.20), calls=%async_computation | async-start | bytes 16384 | tf_op jit(solution)/shard_map/all_to_all | solution.py:290
  11.6 15.4 %collective-permute-start.4 = (f32[800,128]{1,0:T(8,128)S(1)}, f32[800,128]{1,0:T(8,128)}, u32[]{:S(2)}, u32[]{:S(2)}) collective-permute-start(f32[800,128]{1,0:T(8,128)S(1)} %pack.1.refs_2_), channel_id=1, source_target_pairs={{0,2},{1,3},{2,0},{3,1},{4,6},{5,7},{6,4},{7,5},{8,10},{9,11},{10,... | collective-permute-start | bytes 1228808 | tf_op jit(solution)/shard_map/ppermute | solution.py:24
  13.1 13.8 %collective-permute-start.22 = (f32[256,128]{1,0:T(8,128)S(1)}, f32[256,128]{1,0:T(8,128)S(1)}, u32[]{:S(2)}, u32[]{:S(2)}) collective-permute-start(f32[256,128]{1,0:T(8,128)S(1)} %bitcast.30), channel_id=1, source_target_pairs={{0,2},{1,3},{2,0},{3,1},{4,6},{5,7},{6,4},{7,5},{8,10},{9,11},{10,... | collective-permute-start | bytes 393224 | tf_op jit(solution)/shard_map/ppermute | solution.py:24
  13.9 17.3 %copy-start.1 = (f32[1,256,1024]{2,1,0:T(8,128)S(1)}, f32[1,256,1024]{2,1,0:T(8,128)}, u32[]{:S(2)}) copy-start(f32[1,256,1024]{2,1,0:T(8,128)} %param.16) | copy-start | bytes 3145732
  17.0 9.4 %collective-permute-start.7 = (f32[32,128]{1,0:T(8,128)S(1)}, f32[32,128]{1,0:T(8,128)S(1)}, u32[]{:S(2)}, u32[]{:S(2)}) collective-permute-start(f32[32,128]{1,0:T(8,128)S(1)} %get-tuple-element.29), channel_id=1, source_target_pairs={{0,2},{1,3},{2,0},{3,1},{4,6},{5,7},{6,4},{7,5},{8,10},{9,11},{10,... | collective-permute-start | bytes 49160 | tf_op jit(solution)/shard_map/ppermute | solution.py:24
  18.5 7.9 %collective-permute-start.8 = (f32[32,128]{1,0:T(8,128)S(1)}, f32[32,128]{1,0:T(8,128)S(1)}, u32[]{:S(2)}, u32[]{:S(2)}) collective-permute-start(f32[32,128]{1,0:T(8,128)S(1)} %get-tuple-element.29), channel_id=1, source_target_pairs={{0,3},{1,2},{2,1},{3,0},{4,7},{5,6},{6,5},{7,4},{8,11},{9,10},{10,... | collective-permute-start | bytes 49160 | tf_op jit(solution)/shard_map/ppermute | solution.py:24
  18.5 8.9 %collective-permute-start.6 = (f32[32,128]{1,0:T(8,128)S(1)}, f32[32,128]{1,0:T(8,128)S(1)}, u32[]{:S(2)}, u32[]{:S(2)}) collective-permute-start(f32[32,128]{1,0:T(8,128)S(1)} %get-tuple-element.29), channel_id=1, source_target_pairs={{0,1},{1,0},{2,3},{3,2},{4,5},{5,4},{6,7},{7,6},{8,9},{9,8},{10,11... | collective-permute-start | bytes 49160 | tf_op jit(solution)/shard_map/ppermute | solution.py:24
  26.4 6.0 %collective-permute-start.3 = (f32[800,128]{1,0:T(8,128)S(1)}, f32[800,128]{1,0:T(8,128)S(1)}, u32[]{:S(2)}, u32[]{:S(2)}) collective-permute-start(f32[800,128]{1,0:T(8,128)S(1)} %pack.1.refs_2_), channel_id=1, source_target_pairs={{0,1},{1,0},{2,3},{3,2},{4,5},{5,4},{6,7},{7,6},{8,9},{9,8},{10,11... | collective-permute-start | bytes 1228808 | tf_op jit(solution)/shard_map/ppermute | solution.py:24
  26.4 2.8 %collective-permute-start.21 = (f32[256,128]{1,0:T(8,128)S(1)}, f32[256,128]{1,0:T(8,128)S(1)}, u32[]{:S(2)}, u32[]{:S(2)}) collective-permute-start(f32[256,128]{1,0:T(8,128)S(1)} %bitcast.31), channel_id=1, source_target_pairs={{0,1},{1,0},{2,3},{3,2},{4,5},{5,4},{6,7},{7,6},{8,9},{9,8},{10,11... | collective-permute-start | bytes 393224 | tf_op jit(solution)/shard_map/ppermute | solution.py:24
  26.9 2.3 %collective-permute-start.23 = (f32[256,128]{1,0:T(8,128)S(1)}, f32[256,128]{1,0:T(8,128)S(1)}, u32[]{:S(2)}, u32[]{:S(2)}) collective-permute-start(f32[256,128]{1,0:T(8,128)S(1)} %collective-permute-done.22.refs_2_), channel_id=1, source_target_pairs={{0,1},{1,0},{2,3},{3,2},{4,5},{5,4},{6,7},{7,6},{8,9},{9,8},{10,11... | collective-permute-start | bytes 393224 | tf_op jit(solution)/shard_map/ppermute | solution.py:24
  27.0 5.4 %collective-permute-start.5 = (f32[800,128]{1,0:T(8,128)}, f32[800,128]{1,0:T(8,128)S(1)}, u32[]{:S(2)}, u32[]{:S(2)}) collective-permute-start(f32[800,128]{1,0:T(8,128)} %collective-permute-done.4.refs_4_), channel_id=1, source_target_pairs={{0,1},{1,0},{2,3},{3,2},{4,5},{5,4},{6,7},{7,6},{8,9},{9,8},{10,11... | collective-permute-start | bytes 1228808 | tf_op jit(solution)/shard_map/ppermute | solution.py:24
  27.5 10.0 %collective-permute-start.9 = (f32[32,128]{1,0:T(8,128)S(1)}, f32[32,128]{1,0:T(8,128)S(1)}, u32[]{:S(2)}, u32[]{:S(2)}) collective-permute-start(f32[32,128]{1,0:T(8,128)S(1)} %add_add_fusion.1), channel_id=1, source_target_pairs={{0,4},{4,0},{8,12},{12,8},{16,20},{20,16},{24,28},{28,24},{1,5},{5... | collective-permute-start | bytes 49160 | tf_op jit(solution)/shard_map/ppermute | solution.py:24
  37.7 5.4 %collective-permute-start.11 = (f32[32,128]{1,0:T(8,128)S(1)}, f32[32,128]{1,0:T(8,128)S(1)}, u32[]{:S(2)}, u32[]{:S(2)}) collective-permute-start(f32[32,128]{1,0:T(8,128)S(1)} %convolution_subtract_fusion.5), channel_id=1, source_target_pairs={{0,4},{4,0},{8,12},{12,8},{16,20},{20,16},{24,28},{28,24},{1,5},{5... | collective-permute-start | bytes 49160 | tf_op jit(solution)/shard_map/ppermute | solution.py:24
  38.8 4.6 %collective-permute-start.10 = (f32[32,128]{1,0:T(8,128)S(1)}, f32[32,128]{1,0:T(8,128)S(1)}, u32[]{:S(2)}, u32[]{:S(2)}) collective-permute-start(f32[32,128]{1,0:T(8,128)S(1)} %convolution_subtract_fusion.5), channel_id=1, source_target_pairs={{0,12},{4,8},{8,4},{12,0},{16,28},{20,24},{24,20},{28,16},{1,13},{... | collective-permute-start | bytes 49160 | tf_op jit(solution)/shard_map/ppermute | solution.py:24
  40.7 10.4 %collective-permute-start.15 = (f32[160,128]{1,0:T(8,128)S(1)}, f32[160,128]{1,0:T(8,128)S(1)}, u32[]{:S(2)}, u32[]{:S(2)}) collective-permute-start(f32[160,128]{1,0:T(8,128)S(1)} %get-tuple-element.32), channel_id=1, source_target_pairs={{0,16},{4,20},{8,24},{12,28},{16,0},{20,4},{24,8},{28,12},{1,17},{... | collective-permute-start | bytes 245768 | tf_op jit(solution)/shard_map/ppermute | solution.py:24
  43.6 4.2 %collective-permute-start.13 = (f32[32,128]{1,0:T(8,128)S(1)}, f32[32,128]{1,0:T(8,128)S(1)}, u32[]{:S(2)}, u32[]{:S(2)}) collective-permute-start(f32[32,128]{1,0:T(8,128)S(1)} %convolution_subtract_fusion.4), channel_id=1, source_target_pairs={{0,8},{4,12},{8,0},{12,4},{16,24},{20,28},{24,16},{28,20},{1,9},{5... | collective-permute-start | bytes 49160 | tf_op jit(solution)/shard_map/ppermute | solution.py:24
  45.1 5.5 %collective-permute-start.12 = (f32[32,128]{1,0:T(8,128)S(1)}, f32[32,128]{1,0:T(8,128)S(1)}, u32[]{:S(2)}, u32[]{:S(2)}) collective-permute-start(f32[32,128]{1,0:T(8,128)S(1)} %convolution_subtract_fusion.4), channel_id=1, source_target_pairs={{0,24},{4,28},{8,16},{12,20},{16,8},{20,12},{24,0},{28,4},{1,25},{... | collective-permute-start | bytes 49160 | tf_op jit(solution)/shard_map/ppermute | solution.py:24
  51.5 4.6 %collective-permute-start.16 = (f32[32,128]{1,0:T(8,128)S(1)}, f32[32,128]{1,0:T(8,128)S(1)}, u32[]{:S(2)}, u32[]{:S(2)}) collective-permute-start(f32[32,128]{1,0:T(8,128)S(1)} %get-tuple-element.47), channel_id=1, source_target_pairs={{0,8},{4,12},{8,0},{12,4},{16,24},{20,28},{24,16},{28,20},{1,9},{5... | collective-permute-start | bytes 49160 | tf_op jit(solution)/shard_map/ppermute | solution.py:24
  51.6 5.6 %collective-permute-start.17 = (f32[32,128]{1,0:T(8,128)S(1)}, f32[32,128]{1,0:T(8,128)S(1)}, u32[]{:S(2)}, u32[]{:S(2)}) collective-permute-start(f32[32,128]{1,0:T(8,128)S(1)} %get-tuple-element.46), channel_id=1, source_target_pairs={{0,24},{4,28},{8,16},{12,20},{16,8},{20,12},{24,0},{28,4},{1,25},{... | collective-permute-start | bytes 49160 | tf_op jit(solution)/shard_map/ppermute | solution.py:24
  54.2 5.0 %collective-permute-start.14 = (f32[160,128]{1,0:T(8,128)S(1)}, f32[160,128]{1,0:T(8,128)S(1)}, u32[]{:S(2)}, u32[]{:S(2)}) collective-permute-start(f32[160,128]{1,0:T(8,128)S(1)} %pad_maximum_fusion), channel_id=1, source_target_pairs={{0,4},{4,0},{8,12},{12,8},{16,20},{20,16},{24,28},{28,24},{1,5},{5... | collective-permute-start | bytes 245768 | tf_op jit(solution)/shard_map/ppermute | solution.py:24
  55.3 8.0 %collective-permute-start.24 = (f32[32,128]{1,0:T(8,128)S(1)}, f32[32,128]{1,0:T(8,128)S(1)}, u32[]{:S(2)}, u32[]{:S(2)}) collective-permute-start(f32[32,128]{1,0:T(8,128)S(1)} %convolution_subtract_fusion.3), channel_id=1, source_target_pairs={{0,16},{4,20},{8,24},{12,28},{16,0},{20,4},{24,8},{28,12},{1,17},{... | collective-permute-start | bytes 49160 | tf_op jit(solution)/shard_map/ppermute | solution.py:24
  57.4 3.8 %collective-permute-start.18 = (f32[32,128]{1,0:T(8,128)S(1)}, f32[32,128]{1,0:T(8,128)S(1)}, u32[]{:S(2)}, u32[]{:S(2)}) collective-permute-start(f32[32,128]{1,0:T(8,128)S(1)} %get-tuple-element.45), channel_id=1, source_target_pairs={{0,4},{4,0},{8,12},{12,8},{16,20},{20,16},{24,28},{28,24},{1,5},{5... | collective-permute-start | bytes 49160 | tf_op jit(solution)/shard_map/ppermute | solution.py:24
  58.5 4.6 %collective-permute-start.19 = (f32[32,128]{1,0:T(8,128)S(1)}, f32[32,128]{1,0:T(8,128)S(1)}, u32[]{:S(2)}, u32[]{:S(2)}) collective-permute-start(f32[32,128]{1,0:T(8,128)S(1)} %get-tuple-element.44), channel_id=1, source_target_pairs={{0,12},{4,8},{8,4},{12,0},{16,28},{20,24},{24,20},{28,16},{1,13},{... | collective-permute-start | bytes 49160 | tf_op jit(solution)/shard_map/ppermute | solution.py:24
  59.1 4.0 %collective-permute-start.20 = (f32[32,128]{1,0:T(8,128)S(1)}, f32[32,128]{1,0:T(8,128)S(1)}, u32[]{:S(2)}, u32[]{:S(2)}) collective-permute-start(f32[32,128]{1,0:T(8,128)S(1)} %get-tuple-element.44), channel_id=1, source_target_pairs={{0,8},{4,12},{8,0},{12,4},{16,24},{20,28},{24,16},{28,20},{1,9},{5... | collective-permute-start | bytes 49160 | tf_op jit(solution)/shard_map/ppermute | solution.py:24
  64.8 3.8 %collective-permute-start.26 = (f32[32,128]{1,0:T(8,128)S(1)}, f32[32,128]{1,0:T(8,128)S(1)}, u32[]{:S(2)}, u32[]{:S(2)}) collective-permute-start(f32[32,128]{1,0:T(8,128)S(1)} %get-tuple-element.35), channel_id=1, source_target_pairs={{0,2},{1,3},{2,0},{3,1},{4,6},{5,7},{6,4},{7,5},{8,10},{9,11},{10,... | collective-permute-start | bytes 49160 | tf_op jit(solution)/shard_map/ppermute | solution.py:24
  66.4 3.2 %collective-permute-start.27 = (f32[32,128]{1,0:T(8,128)S(1)}, f32[32,128]{1,0:T(8,128)S(1)}, u32[]{:S(2)}, u32[]{:S(2)}) collective-permute-start(f32[32,128]{1,0:T(8,128)S(1)} %get-tuple-element.35), channel_id=1, source_target_pairs={{0,3},{1,2},{2,1},{3,0},{4,7},{5,6},{6,5},{7,4},{8,11},{9,10},{10,... | collective-permute-start | bytes 49160 | tf_op jit(solution)/shard_map/ppermute | solution.py:24
  66.4 3.2 %collective-permute-start.25 = (f32[32,128]{1,0:T(8,128)S(1)}, f32[32,128]{1,0:T(8,128)S(1)}, u32[]{:S(2)}, u32[]{:S(2)}) collective-permute-start(f32[32,128]{1,0:T(8,128)S(1)} %get-tuple-element.35), channel_id=1, source_target_pairs={{0,1},{1,0},{2,3},{3,2},{4,5},{5,4},{6,7},{7,6},{8,9},{9,8},{10,11... | collective-permute-start | bytes 49160 | tf_op jit(solution)/shard_map/ppermute | solution.py:24
  (7 other events, 35.5 us)
